TPU v7x, 256 devices: a whole 4x4x8 slice. The times are simulated.
256 devices in a mesh: gx: 8 (over z), gy: 4 (over y), gz: 8 (over x, core).
Axes of the slice: x: 4, y: 4, z: 8, core: 2. Of those that a mesh axis runs over, the one named last changes fastest.
Arguments:
- field: bfloat16 [32, 64, 32, 1024], P(None, 'gx', 'gy', 'gz'), may hold values from -6 to 6
- mixing: bfloat16 [32, 32], replicated, may hold values from -1 to 1
- kernel_fine: bfloat16 [3, 3, 3, 32, 32], replicated, may hold values from -0.21875 to 0.21875
- kernel_half: bfloat16 [3, 3, 3, 32, 32], replicated, may hold values from -1.5 to 1.5
- kernel_quarter: bfloat16 [3, 3, 3, 32, 32], replicated, may hold values from -4 to 4
- kernel_eighth: bfloat16 [3, 3, 3, 32, 32], replicated, may hold values from -6 to 6
Outputs:
- layer_out: bfloat16 [32, 64, 32, 1024], P(None, 'gx', 'gy', 'gz')
All inputs are finite; a program needn't handle non-finite values.
Results may differ from a plain program's by a relative error of at most 0.008.
Values may be sent and summed in bfloat16 or wider, within the bound.
No kernel may reach another device: no remote copies, remote signals or barrier semaphores. Data moves between devices by JAX's collectives and lax.ppermute only.
A program may use at most 128 MiB of HBM per device.

v0:
```python
import jax
import jax.numpy as jnp
from jax import lax
from jax.sharding import PartitionSpec as P


def padded_2(block, sides, width):
    for axis, dim in sides:
        count = lax.axis_size(axis)
        forward = [(i, i + 1) for i in range(count - 1)]
        backward = [(target, source) for source, target in forward]
        low = lax.ppermute(
            lax.slice_in_dim(block, block.shape[dim] - width, None, axis=dim), axis, forward
        )
        high = lax.ppermute(lax.slice_in_dim(block, 0, width, axis=dim), axis, backward)
        block = jnp.concatenate([low, block, high], axis=dim)
    return block


def restrict(values):
    chans, sizex, sizey, sizez = values.shape
    blocks = values.astype(jnp.float32).reshape(chans, sizex // 2, 2, sizey // 2, 2, sizez // 2, 2)
    return jnp.mean(blocks, axis=(2, 4, 6)).astype(jnp.bfloat16)


def conv_valid(padded, kernel):
    result = lax.conv_general_dilated(
        padded[None],
        kernel,
        (1, 1, 1),
        "VALID",
        dimension_numbers=("NCDHW", "DHWIO", "NCDHW"),
        preferred_element_type=jnp.float32,
    )
    return result[0]


def refine_padded(padded, dimension):
    length = padded.shape[dimension]
    inner = lax.slice_in_dim(padded, 1, length - 1, axis=dimension)
    lower = lax.slice_in_dim(padded, 0, length - 2, axis=dimension)
    upper = lax.slice_in_dim(padded, 2, length, axis=dimension)
    even_cells = 0.75 * inner + 0.25 * lower
    odd_cells = 0.75 * inner + 0.25 * upper
    joined = jnp.stack([even_cells, odd_cells], axis=dimension + 1)
    shape_out = list(inner.shape)
    shape_out[dimension] = shape_out[dimension] * 2
    return joined.reshape(shape_out)


def prolong_local(values):
    padded = padded_2(values, (("gx", 1), ("gy", 2), ("gz", 3)), 1)
    current = padded.astype(jnp.float32)
    for dimension in (1, 2, 3):
        current = refine_padded(current, dimension)
    return current


def level_rims(values):
    return padded_2(values, (("gx", 1), ("gy", 2), ("gz", 3)), 1)


def on_device(field, mixing, kernel_fine, kernel_half, kernel_quarter, kernel_eighth):
    kernels = (kernel_fine, kernel_half, kernel_quarter, kernel_eighth)
    outputs = []
    fine_padded = padded_2(field, (("gx", 1), ("gy", 2), ("gz", 3)), 1)
    outputs.append(conv_valid(fine_padded, kernel_fine))
    current = field
    for depth in (1, 2):
        current = restrict(current)
        outputs.append(conv_valid(level_rims(current), kernels[depth]))
    current = restrict(current)
    padded = padded_2(current, (("gx", 1), ("gy", 2), ("gz", 3)), 1)
    outputs.append(conv_valid(padded, kernel_eighth))
    carried = outputs[3].astype(jnp.bfloat16)
    for depth in (2, 1):
        carried = (outputs[depth] + prolong_local(carried)).astype(jnp.bfloat16)
    chans = field.shape[0]
    mixed = jnp.dot(mixing, field.reshape(chans, -1), preferred_element_type=jnp.float32).reshape(
        field.shape
    )
    total = mixed + outputs[0] + prolong_local(carried)
    return jax.nn.gelu(total, approximate=True).astype(jnp.bfloat16)


def solution(mesh):
    placed = (P(None, "gx", "gy", "gz"), P(), P(), P(), P(), P())
    return jax.shard_map(
        on_device, mesh=mesh, in_specs=placed, out_specs=P(None, "gx", "gy", "gz"), check_vma=False
    )
```

profile of v0, /device:TPU:64, one launch (start us, length us, event | category | flops | bytes accessed | tf_op | source)
XLA Modules:
  0.0 224.8 jit_solution(1576073533978478552)
XLA Ops:
  0.0 3.7 %copy.131 = f32[32,8,8,128]{0,3,2,1:T(8,128)} copy(bf16[32,8,8,128]{3,2,1,0:T(8,128)(2,1)} %param.6) | data formatting | bytes 1572864 | tf_op jit(solution)/shard_map/reshape | solution.py:22
  3.7 4.9 %reduce_sum.34 = f32[32,4,4,64]{0,3,2,1:T(8,128)S(1)} reduce(f32[32,4,2,4,2,64,2]{0,6,5,4,3,2,1:T(2,128)} %bitcast.162, f32[]{:T(128)} %constant.8.clone.1), dimensions={2,4,6}, to_apply=%region_0.0 | reduce | flops 229376 | bytes 1179652 | tf_op jit(solution)/shard_map/reduce_sum | solution.py:23
  9.1 3.8 %collective-permute-start.18 = (bf16[32,1,1,16]{0,3,2,1:T(8,128)(2,1)S(1)}, bf16[32,1,1,16]{0,3,2,1:T(8,128)(2,1)S(1)}, u32[]{:S(2)}, u32[]{:S(2)}) collective-permute-start(bf16[32,1,1,16]{0,3,2,1:T(8,128)(2,1)S(1)} %fusion.89), channel_id=1, source_target_pairs={{0,32},{32,64},{64,96},{96,128},{128,160},{160,192},{192,224},{1,3... | collective-permute-start | bytes 3080 | tf_op jit(solution)/shard_map/ppermute | solution.py:12
  15.0 4.6 %collective-permute-done.19 = bf16[32,1,1,16]{0,3,2,1:T(8,128)(2,1)S(1)} collective-permute-done((bf16[32,1,1,16]{0,3,2,1:T(8,128)(2,1)S(1)}, bf16[32,1,1,16]{0,3,2,1:T(8,128)(2,1)S(1)}, u32[]{:S(2)}, u32[]{:S(2)}) %collective-permute-start.19) | collective-permute-done | bytes 1056 | tf_op jit(solution)/shard_map/ppermute | solution.py:15
  19.6 3.5 %collective-permute-start.20 = (bf16[32,3,1,16]{0,3,2,1:T(8,128)(2,1)S(1)}, bf16[32,3,1,16]{0,3,2,1:T(8,128)(2,1)S(1)}, u32[]{:S(2)}, u32[]{:S(2)}) collective-permute-start(bf16[32,3,1,16]{0,3,2,1:T(8,128)(2,1)S(1)} %pad_maximum_fusion.16), channel_id=1, source_target_pairs={{0,8},{8,16},{16,24},{1,9},{9,17},{17,25},{2,10},{10,18},{18,26},{... | collective-permute-start | bytes 9224 | tf_op jit(solution)/shard_map/ppermute | solution.py:12
  24.4 4.2 %collective-permute-done.21 = bf16[32,3,1,16]{0,3,2,1:T(8,128)(2,1)S(1)} collective-permute-done((bf16[32,3,1,16]{0,3,2,1:T(8,128)(2,1)S(1)}, bf16[32,3,1,16]{0,3,2,1:T(8,128)(2,1)S(1)}, u32[]{:S(2)}, u32[]{:S(2)}) %collective-permute-start.21) | collective-permute-done | bytes 3104 | tf_op jit(solution)/shard_map/ppermute | solution.py:15
  31.3 3.5 %collective-permute-done.23 = bf16[32,3,3,1]{0,3,2,1:T(2,128)(2,1)S(1)} collective-permute-done((bf16[32,3,3,1]{0,3,2,1:T(2,128)(2,1)S(1)}, bf16[32,3,3,1]{0,3,2,1:T(2,128)(2,1)S(1)}, u32[]{:S(2)}, u32[]{:S(2)}) %collective-permute-start.23) | collective-permute-done | bytes 608 | tf_op jit(solution)/shard_map/ppermute | solution.py:15
  35.4 5.1 %collective-permute-start.24 = (bf16[32,1,1,16]{0,3,2,1:T(8,128)(2,1)S(1)}, bf16[32,1,1,16]{0,3,2,1:T(8,128)(2,1)S(1)}, u32[]{:S(2)}, u32[]{:S(2)}) collective-permute-start(bf16[32,1,1,16]{0,3,2,1:T(8,128)(2,1)S(1)} %slice_bitcast_fusion.4), channel_id=1, source_target_pairs={{0,32},{32,64},{64,96},{96,128},{128,160},{160,192},{192,224},{1,3... | collective-permute-start | bytes 3080 | tf_op jit(solution)/shard_map/ppermute | solution.py:12
  42.5 3.9 %collective-permute-start.12 = (bf16[32,1,2,32]{0,3,2,1:T(8,128)(2,1)S(1)}, bf16[32,1,2,32]{0,3,2,1:T(8,128)(2,1)S(1)}, u32[]{:S(2)}, u32[]{:S(2)}) collective-permute-start(bf16[32,1,2,32]{0,3,2,1:T(8,128)(2,1)S(1)} %get-tuple-element.55), channel_id=1, source_target_pairs={{0,32},{32,64},{64,96},{96,128},{128,160},{160,192},{192,224},{1,3... | collective-permute-start | bytes 12296 | tf_op jit(solution)/shard_map/ppermute | solution.py:12
  48.4 3.5 %collective-permute-start.26 = (bf16[32,3,1,16]{0,3,2,1:T(8,128)(2,1)S(1)}, bf16[32,3,1,16]{0,3,2,1:T(8,128)(2,1)S(1)}, u32[]{:S(2)}, u32[]{:S(2)}) collective-permute-start(bf16[32,3,1,16]{0,3,2,1:T(8,128)(2,1)S(1)} %pad_maximum_fusion.17), channel_id=1, source_target_pairs={{0,8},{8,16},{16,24},{1,9},{9,17},{17,25},{2,10},{10,18},{18,26},{... | collective-permute-start | bytes 9224 | tf_op jit(solution)/shard_map/ppermute | solution.py:12
  53.3 4.2 %collective-permute-done.27 = bf16[32,3,1,16]{0,3,2,1:T(8,128)(2,1)S(1)} collective-permute-done((bf16[32,3,1,16]{0,3,2,1:T(8,128)(2,1)S(1)}, bf16[32,3,1,16]{0,3,2,1:T(8,128)(2,1)S(1)}, u32[]{:S(2)}, u32[]{:S(2)}) %collective-permute-start.27) | collective-permute-done | bytes 3104 | tf_op jit(solution)/shard_map/ppermute | solution.py:15
  60.8 3.2 %collective-permute-start.14 = (bf16[32,4,1,32]{0,3,2,1:T(8,128)(2,1)S(1)}, bf16[32,4,1,32]{0,3,2,1:T(8,128)(2,1)S(1)}, u32[]{:S(2)}, u32[]{:S(2)}) collective-permute-start(bf16[32,4,1,32]{0,3,2,1:T(8,128)(2,1)S(1)} %get-tuple-element.45), channel_id=1, source_target_pairs={{0,8},{8,16},{16,24},{1,9},{9,17},{17,25},{2,10},{10,18},{18,26},{... | collective-permute-start | bytes 24584 | tf_op jit(solution)/shard_map/ppermute | solution.py:12
  65.6 4.2 %collective-permute-done.15 = bf16[32,4,1,32]{0,3,2,1:T(8,128)(2,1)S(1)} collective-permute-done((bf16[32,4,1,32]{0,3,2,1:T(8,128)(2,1)S(1)}, bf16[32,4,1,32]{0,3,2,1:T(8,128)(2,1)S(1)}, u32[]{:S(2)}, u32[]{:S(2)}) %collective-permute-start.15) | collective-permute-done | bytes 8224 | tf_op jit(solution)/shard_map/ppermute | solution.py:15
  69.9 3.4 %collective-permute-start.16 = (bf16[32,4,4,1]{0,3,2,1:T(2,128)(2,1)S(1)}, bf16[32,4,4,1]{0,3,2,1:T(2,128)(2,1)S(1)}, u32[]{:S(2)}, u32[]{:S(2)}) collective-permute-start(bf16[32,4,4,1]{0,3,2,1:T(2,128)(2,1)S(1)} %get-tuple-element.39), channel_id=1, source_target_pairs={{0,1},{1,2},{2,3},{3,4},{4,5},{5,6},{6,7},{8,9},{9,10},{10,11},{11... | collective-permute-start | bytes 3080 | tf_op jit(solution)/shard_map/ppermute | solution.py:12
  74.7 4.3 %collective-permute-done.17 = bf16[32,4,4,1]{0,3,2,1:T(2,128)(2,1)S(1)} collective-permute-done((bf16[32,4,4,1]{0,3,2,1:T(2,128)(2,1)S(1)}, bf16[32,4,4,1]{0,3,2,1:T(2,128)(2,1)S(1)}, u32[]{:S(2)}, u32[]{:S(2)}) %collective-permute-start.17) | collective-permute-done | bytes 1056 | tf_op jit(solution)/shard_map/ppermute | solution.py:15
  80.1 3.9 %collective-permute-start.30 = (bf16[32,1,2,32]{0,2,3,1:T(2,128)(2,1)S(1)}, bf16[32,1,2,32]{0,2,3,1:T(2,128)(2,1)S(1)}, u32[]{:S(2)}, u32[]{:S(2)}) collective-permute-start(bf16[32,1,2,32]{0,2,3,1:T(2,128)(2,1)S(1)} %get-tuple-element.53), channel_id=1, source_target_pairs={{0,32},{32,64},{64,96},{96,128},{128,160},{160,192},{192,224},{1,3... | collective-permute-start | bytes 12296 | tf_op jit(solution)/shard_map/ppermute | solution.py:12
  86.0 4.1 %collective-permute-done.31 = bf16[32,1,2,32]{0,2,3,1:T(2,128)(2,1)S(1)} collective-permute-done((bf16[32,1,2,32]{0,2,3,1:T(2,128)(2,1)S(1)}, bf16[32,1,2,32]{0,2,3,1:T(2,128)(2,1)S(1)}, u32[]{:S(2)}, u32[]{:S(2)}) %collective-permute-start.31) | collective-permute-done | bytes 4128 | tf_op jit(solution)/shard_map/ppermute | solution.py:15
  93.6 5.1 %collective-permute-start.6 = (bf16[32,1,4,64]{0,3,2,1:T(8,128)(2,1)S(1)}, bf16[32,1,4,64]{0,3,2,1:T(8,128)(2,1)S(1)}, u32[]{:S(2)}, u32[]{:S(2)}) collective-permute-start(bf16[32,1,4,64]{0,3,2,1:T(8,128)(2,1)S(1)} %get-tuple-element.35), channel_id=1, source_target_pairs={{0,32},{32,64},{64,96},{96,128},{128,160},{160,192},{192,224},{1,3... | collective-permute-start | bytes 49160 | tf_op jit(solution)/shard_map/ppermute | solution.py:12
  105.1 4.4 %collective-permute-start.8 = (bf16[32,6,1,64]{0,3,2,1:T(8,128)(2,1)S(1)}, bf16[32,6,1,64]{0,3,2,1:T(8,128)(2,1)S(1)}, u32[]{:S(2)}, u32[]{:S(2)}) collective-permute-start(bf16[32,6,1,64]{0,3,2,1:T(8,128)(2,1)S(1)} %get-tuple-element.23), channel_id=1, source_target_pairs={{0,8},{8,16},{16,24},{1,9},{9,17},{17,25},{2,10},{10,18},{18,26},{... | collective-permute-start | bytes 73736 | tf_op jit(solution)/shard_map/ppermute | solution.py:12
  111.7 4.4 %collective-permute-done.9 = bf16[32,6,1,64]{0,3,2,1:T(8,128)(2,1)S(1)} collective-permute-done((bf16[32,6,1,64]{0,3,2,1:T(8,128)(2,1)S(1)}, bf16[32,6,1,64]{0,3,2,1:T(8,128)(2,1)S(1)}, u32[]{:S(2)}, u32[]{:S(2)}) %collective-permute-start.9) | collective-permute-done | bytes 24608 | tf_op jit(solution)/shard_map/ppermute | solution.py:15
  121.4 3.2 %collective-permute-done.11 = bf16[32,6,6,1]{0,3,2,1:T(2,128)(2,1)S(1)} collective-permute-done((bf16[32,6,6,1]{0,3,2,1:T(2,128)(2,1)S(1)}, bf16[32,6,6,1]{0,3,2,1:T(2,128)(2,1)S(1)}, u32[]{:S(2)}, u32[]{:S(2)}) %collective-permute-start.11) | collective-permute-done | bytes 2336 | tf_op jit(solution)/shard_map/ppermute | solution.py:15
  128.1 3.9 %collective-permute-start.36 = (bf16[32,1,4,64]{0,2,3,1:T(4,128)(2,1)S(1)}, bf16[32,1,4,64]{0,2,3,1:T(4,128)(2,1)S(1)}, u32[]{:S(2)}, u32[]{:S(2)}) collective-permute-start(bf16[32,1,4,64]{0,2,3,1:T(4,128)(2,1)S(1)} %get-tuple-element.29), channel_id=1, source_target_pairs={{0,32},{32,64},{64,96},{96,128},{128,160},{160,192},{192,224},{1,3... | collective-permute-start | bytes 49160 | tf_op jit(solution)/shard_map/ppermute | solution.py:12
  134.0 3.9 %collective-permute-start = (bf16[32,1,8,128]{3,0,2,1:T(8,128)(2,1)S(1)}, bf16[32,1,8,128]{3,0,2,1:T(8,128)(2,1)S(1)}, u32[]{:S(2)}, u32[]{:S(2)}) collective-permute-start(bf16[32,1,8,128]{3,0,2,1:T(8,128)(2,1)S(1)} %copy.186), channel_id=1, source_target_pairs={{0,32},{32,64},{64,96},{96,128},{128,160},{160,192},{192,224},{1,3... | collective-permute-start | bytes 196616 | tf_op jit(solution)/shard_map/ppermute | solution.py:12
  145.9 2.8 %collective-permute-done.38 = bf16[32,6,1,64]{0,2,3,1:T(2,128)(2,1)S(1)} collective-permute-done((bf16[32,6,1,64]{0,2,3,1:T(2,128)(2,1)S(1)}, bf16[32,6,1,64]{0,2,3,1:T(2,128)(2,1)S(1)}, u32[]{:S(2)}, u32[]{:S(2)}) %collective-permute-start.38) | collective-permute-done | bytes 24608 | tf_op jit(solution)/shard_map/ppermute | solution.py:12
  148.8 4.6 %collective-permute-done.39 = bf16[32,6,1,64]{0,2,3,1:T(2,128)(2,1)S(1)} collective-permute-done((bf16[32,6,1,64]{0,2,3,1:T(2,128)(2,1)S(1)}, bf16[32,6,1,64]{0,2,3,1:T(2,128)(2,1)S(1)}, u32[]{:S(2)}, u32[]{:S(2)}) %collective-permute-start.39) | collective-permute-done | bytes 24608 | tf_op jit(solution)/shard_map/ppermute | solution.py:15
  167.6 6.3 %collective-permute-start.4 = (bf16[32,10,10,1]{0,2,3,1:T(8,128)(2,1)}, bf16[32,10,10,1]{0,2,3,1:T(8,128)(2,1)}, u32[]{:S(2)}, u32[]{:S(2)}) collective-permute-start(bf16[32,10,10,1]{0,2,3,1:T(8,128)(2,1)} %copy.123), channel_id=1, source_target_pairs={{0,1},{1,2},{2,3},{3,4},{4,5},{5,6},{6,7},{8,9},{9,10},{10,11},{11... | collective-permute-start | bytes 19208 | tf_op jit(solution)/shard_map/ppermute | solution.py:12
  178.6 3.1 %copy.167 = f32[32,8,8,64,2]{0,2,4,3,1:T(8,128)} copy(f32[32,8,8,64,2]{3,1,2,0,4:T(8,128)S(1)} %pad_maximum_fusion) | data formatting | bytes 2097152 | tf_op jit(solution)/shard_map/stack | solution.py:45
  181.7 3.7 %copy.168 = f32[32,8,8,128]{3,0,2,1:T(8,128)} copy(f32[32,8,8,128]{0,2,3,1:T(8,128)} %bitcast.161) | data formatting | bytes 2097152 | tf_op jit(solution)/shard_map/reshape | solution.py:48
  189.7 6.0 %reshape.91 = bf16[32,10,10,1,8,17]{5,4,0,2,1,3:T(8,128)(2,1)} reshape(bf16[32,10,10,1,136]{4,0,2,1,3:T(8,128)(2,1)S(1)} %pad) | data formatting | bytes 1740800 | tf_op jit(solution)/shard_map/conv_general_dilated | solution.py:27
  195.8 10.2 %copy.128 = bf16[32,10,10,1,8,17]{0,4,5,2,1,3:T(8,128)(2,1)} copy(bf16[32,10,10,1,8,17]{5,4,0,2,1,3:T(8,128)(2,1)} %reshape.91) | data formatting | bytes 1740800 | tf_op jit(solution)/shard_map/conv_general_dilated | solution.py:27
  207.1 9.9 %broadcast_select_fusion = f32[8,8,8,17,32]{4,2,3,1,0:T(8,128)S(1)} fusion(pred[8,17]{0,1:T(8,128)(4,1)S(1)} %copy-done.10, bf16[3,3,3,32,32]{4,3,2,1,0:T(8,128)(2,1)S(1)} %copy-done, bf16[32,10,10,1,7,2]{0,4,5,2,1,3:T(8,128)(2,1)S(1)} %slice.258, bf16[32,10,10,1,8,17]{0,4,5,2,1,3:T(8,128)(2,1)} %copy.128), kind=kOutput, calls=%fused_computation.8 | convolution fusion | flops 484493312 | bytes 2129544 | tf_op jit(solution)/shard_map/conv_general_dilated | solution.py:27
  220.1 2.9 %copy.173 = f32[8,8,1,128,32]{3,4,1,0,2:T(8,128)S(1)} copy(f32[8,8,1,128,32]{4,1,3,0,2:T(8,128)} %slice.259) | data formatting | bytes 2097152
  (194 shorter events, 81.0 us)
Async XLA Ops:
  9.1 5.9 %collective-permute-start.18 = (bf16[32,1,1,16]{0,3,2,1:T(8,128)(2,1)S(1)}, bf16[32,1,1,16]{0,3,2,1:T(8,128)(2,1)S(1)}, u32[]{:S(2)}, u32[]{:S(2)}) collective-permute-start(bf16[32,1,1,16]{0,3,2,1:T(8,128)(2,1)S(1)} %fusion.89), channel_id=1, source_target_pairs={{0,32},{32,64},{64,96},{96,128},{128,160},{160,192},{192,224},{1,3... | collective-permute-start | bytes 3080 | tf_op jit(solution)/shard_map/ppermute | solution.py:12
  12.9 6.6 %collective-permute-start.19 = (bf16[32,1,1,16]{0,3,2,1:T(8,128)(2,1)S(1)}, bf16[32,1,1,16]{0,3,2,1:T(8,128)(2,1)S(1)}, u32[]{:S(2)}, u32[]{:S(2)}) collective-permute-start(bf16[32,1,1,16]{0,3,2,1:T(8,128)(2,1)S(1)} %fusion.89), channel_id=1, source_target_pairs={{32,0},{64,32},{96,64},{128,96},{160,128},{192,160},{224,192},{33,... | collective-permute-start | bytes 3080 | tf_op jit(solution)/shard_map/ppermute | solution.py:15
  35.4 12.9 %collective-permute-start.24 = (bf16[32,1,1,16]{0,3,2,1:T(8,128)(2,1)S(1)}, bf16[32,1,1,16]{0,3,2,1:T(8,128)(2,1)S(1)}, u32[]{:S(2)}, u32[]{:S(2)}) collective-permute-start(bf16[32,1,1,16]{0,3,2,1:T(8,128)(2,1)S(1)} %slice_bitcast_fusion.4), channel_id=1, source_target_pairs={{0,32},{32,64},{64,96},{96,128},{128,160},{160,192},{192,224},{1,3... | collective-permute-start | bytes 3080 | tf_op jit(solution)/shard_map/ppermute | solution.py:12
  40.6 7.8 %collective-permute-start.25 = (bf16[32,1,1,16]{0,3,2,1:T(8,128)(2,1)S(1)}, bf16[32,1,1,16]{0,3,2,1:T(8,128)(2,1)S(1)}, u32[]{:S(2)}, u32[]{:S(2)}) collective-permute-start(bf16[32,1,1,16]{0,3,2,1:T(8,128)(2,1)S(1)} %slice_bitcast_fusion.4), channel_id=1, source_target_pairs={{32,0},{64,32},{96,64},{128,96},{160,128},{192,160},{224,192},{33,... | collective-permute-start | bytes 3080 | tf_op jit(solution)/shard_map/ppermute | solution.py:15
  42.5 10.7 %collective-permute-start.12 = (bf16[32,1,2,32]{0,3,2,1:T(8,128)(2,1)S(1)}, bf16[32,1,2,32]{0,3,2,1:T(8,128)(2,1)S(1)}, u32[]{:S(2)}, u32[]{:S(2)}) collective-permute-start(bf16[32,1,2,32]{0,3,2,1:T(8,128)(2,1)S(1)} %get-tuple-element.55), channel_id=1, source_target_pairs={{0,32},{32,64},{64,96},{96,128},{128,160},{160,192},{192,224},{1,3... | collective-permute-start | bytes 12296 | tf_op jit(solution)/shard_map/ppermute | solution.py:12
  46.4 6.8 %collective-permute-start.13 = (bf16[32,1,2,32]{0,3,2,1:T(8,128)(2,1)S(1)}, bf16[32,1,2,32]{0,3,2,1:T(8,128)(2,1)S(1)}, u32[]{:S(2)}, u32[]{:S(2)}) collective-permute-start(bf16[32,1,2,32]{0,3,2,1:T(8,128)(2,1)S(1)} %get-tuple-element.56), channel_id=1, source_target_pairs={{32,0},{64,32},{96,64},{128,96},{160,128},{192,160},{224,192},{33,... | collective-permute-start | bytes 12296 | tf_op jit(solution)/shard_map/ppermute | solution.py:15
  51.9 5.6 %collective-permute-start.27 = (bf16[32,3,1,16]{0,3,2,1:T(8,128)(2,1)S(1)}, bf16[32,3,1,16]{0,3,2,1:T(8,128)(2,1)S(1)}, u32[]{:S(2)}, u32[]{:S(2)}) collective-permute-start(bf16[32,3,1,16]{0,3,2,1:T(8,128)(2,1)S(1)} %pad_maximum_fusion.17), channel_id=1, source_target_pairs={{8,0},{16,8},{24,16},{9,1},{17,9},{25,17},{10,2},{18,10},{26,18},{... | collective-permute-start | bytes 9224 | tf_op jit(solution)/shard_map/ppermute | solution.py:15
  57.5 7.8 %collective-permute-start.28 = (bf16[32,3,3,1]{0,3,2,1:T(2,128)(2,1)S(1)}, bf16[32,3,3,1]{0,3,2,1:T(2,128)(2,1)S(1)}, u32[]{:S(2)}, u32[]{:S(2)}) collective-permute-start(bf16[32,3,3,1]{0,3,2,1:T(2,128)(2,1)S(1)} %get-tuple-element.49), channel_id=1, source_target_pairs={{0,1},{1,2},{2,3},{3,4},{4,5},{5,6},{6,7},{8,9},{9,10},{10,11},{11... | collective-permute-start | bytes 1736 | tf_op jit(solution)/shard_map/ppermute | solution.py:12
  59.5 5.8 %collective-permute-start.29 = (bf16[32,3,3,1]{0,3,2,1:T(2,128)(2,1)S(1)}, bf16[32,3,3,1]{0,3,2,1:T(2,128)(2,1)S(1)}, u32[]{:S(2)}, u32[]{:S(2)}) collective-permute-start(bf16[32,3,3,1]{0,3,2,1:T(2,128)(2,1)S(1)} %get-tuple-element.50), channel_id=1, source_target_pairs={{1,0},{2,1},{3,2},{4,3},{5,4},{6,5},{7,6},{9,8},{10,9},{11,10},{12... | collective-permute-start | bytes 1736 | tf_op jit(solution)/shard_map/ppermute | solution.py:15
  64.0 5.8 %collective-permute-start.15 = (bf16[32,4,1,32]{0,3,2,1:T(8,128)(2,1)S(1)}, bf16[32,4,1,32]{0,3,2,1:T(8,128)(2,1)S(1)}, u32[]{:S(2)}, u32[]{:S(2)}) collective-permute-start(bf16[32,4,1,32]{0,3,2,1:T(8,128)(2,1)S(1)} %get-tuple-element.46), channel_id=1, source_target_pairs={{8,0},{16,8},{24,16},{9,1},{17,9},{25,17},{10,2},{18,10},{26,18},{... | collective-permute-start | bytes 24584 | tf_op jit(solution)/shard_map/ppermute | solution.py:15
  73.3 5.7 %collective-permute-start.17 = (bf16[32,4,4,1]{0,3,2,1:T(2,128)(2,1)S(1)}, bf16[32,4,4,1]{0,3,2,1:T(2,128)(2,1)S(1)}, u32[]{:S(2)}, u32[]{:S(2)}) collective-permute-start(bf16[32,4,4,1]{0,3,2,1:T(2,128)(2,1)S(1)} %get-tuple-element.40), channel_id=1, source_target_pairs={{1,0},{2,1},{3,2},{4,3},{5,4},{6,5},{7,6},{9,8},{10,9},{11,10},{12... | collective-permute-start | bytes 3080 | tf_op jit(solution)/shard_map/ppermute | solution.py:15
  80.1 5.9 %collective-permute-start.30 = (bf16[32,1,2,32]{0,2,3,1:T(2,128)(2,1)S(1)}, bf16[32,1,2,32]{0,2,3,1:T(2,128)(2,1)S(1)}, u32[]{:S(2)}, u32[]{:S(2)}) collective-permute-start(bf16[32,1,2,32]{0,2,3,1:T(2,128)(2,1)S(1)} %get-tuple-element.53), channel_id=1, source_target_pairs={{0,32},{32,64},{64,96},{96,128},{128,160},{160,192},{192,224},{1,3... | collective-permute-start | bytes 12296 | tf_op jit(solution)/shard_map/ppermute | solution.py:12
  84.0 6.1 %collective-permute-start.31 = (bf16[32,1,2,32]{0,2,3,1:T(2,128)(2,1)S(1)}, bf16[32,1,2,32]{0,2,3,1:T(2,128)(2,1)S(1)}, u32[]{:S(2)}, u32[]{:S(2)}) collective-permute-start(bf16[32,1,2,32]{0,2,3,1:T(2,128)(2,1)S(1)} %get-tuple-element.54), channel_id=1, source_target_pairs={{32,0},{64,32},{96,64},{128,96},{160,128},{192,160},{224,192},{33,... | collective-permute-start | bytes 12296 | tf_op jit(solution)/shard_map/ppermute | solution.py:15
  90.3 10.3 %collective-permute-start.32 = (bf16[32,4,1,32]{0,2,3,1:T(2,128)(2,1)S(1)}, bf16[32,4,1,32]{0,2,3,1:T(2,128)(2,1)S(1)}, u32[]{:S(2)}, u32[]{:S(2)}) collective-permute-start(bf16[32,4,1,32]{0,2,3,1:T(2,128)(2,1)S(1)} %get-tuple-element.43), channel_id=1, source_target_pairs={{0,8},{8,16},{16,24},{1,9},{9,17},{17,25},{2,10},{10,18},{18,26},{... | collective-permute-start | bytes 24584 | tf_op jit(solution)/shard_map/ppermute | solution.py:12
  92.2 8.4 %collective-permute-start.33 = (bf16[32,4,1,32]{0,2,3,1:T(2,128)(2,1)S(1)}, bf16[32,4,1,32]{0,2,3,1:T(2,128)(2,1)S(1)}, u32[]{:S(2)}, u32[]{:S(2)}) collective-permute-start(bf16[32,4,1,32]{0,2,3,1:T(2,128)(2,1)S(1)} %get-tuple-element.44), channel_id=1, source_target_pairs={{8,0},{16,8},{24,16},{9,1},{17,9},{25,17},{10,2},{18,10},{26,18},{... | collective-permute-start | bytes 24584 | tf_op jit(solution)/shard_map/ppermute | solution.py:15
  93.6 10.7 %collective-permute-start.6 = (bf16[32,1,4,64]{0,3,2,1:T(8,128)(2,1)S(1)}, bf16[32,1,4,64]{0,3,2,1:T(8,128)(2,1)S(1)}, u32[]{:S(2)}, u32[]{:S(2)}) collective-permute-start(bf16[32,1,4,64]{0,3,2,1:T(8,128)(2,1)S(1)} %get-tuple-element.35), channel_id=1, source_target_pairs={{0,32},{32,64},{64,96},{96,128},{128,160},{160,192},{192,224},{1,3... | collective-permute-start | bytes 49160 | tf_op jit(solution)/shard_map/ppermute | solution.py:12
  98.7 6.3 %collective-permute-start.7 = (bf16[32,1,4,64]{0,3,2,1:T(8,128)(2,1)S(1)}, bf16[32,1,4,64]{0,3,2,1:T(8,128)(2,1)S(1)}, u32[]{:S(2)}, u32[]{:S(2)}) collective-permute-start(bf16[32,1,4,64]{0,3,2,1:T(8,128)(2,1)S(1)} %get-tuple-element.36), channel_id=1, source_target_pairs={{32,0},{64,32},{96,64},{128,96},{160,128},{192,160},{224,192},{33,... | collective-permute-start | bytes 49160 | tf_op jit(solution)/shard_map/ppermute | solution.py:15
  100.7 10.1 %collective-permute-start.34 = (bf16[32,4,4,1]{0,2,3,1:T(4,128)(2,1)S(1)}, bf16[32,4,4,1]{0,2,3,1:T(4,128)(2,1)S(1)}, u32[]{:S(2)}, u32[]{:S(2)}) collective-permute-start(bf16[32,4,4,1]{0,2,3,1:T(4,128)(2,1)S(1)} %get-tuple-element.37), channel_id=1, source_target_pairs={{0,1},{1,2},{2,3},{3,4},{4,5},{5,6},{6,7},{8,9},{9,10},{10,11},{11... | collective-permute-start | bytes 3080 | tf_op jit(solution)/shard_map/ppermute | solution.py:12
  103.0 7.8 %collective-permute-start.35 = (bf16[32,4,4,1]{0,2,3,1:T(4,128)(2,1)S(1)}, bf16[32,4,4,1]{0,2,3,1:T(4,128)(2,1)S(1)}, u32[]{:S(2)}, u32[]{:S(2)}) collective-permute-start(bf16[32,4,4,1]{0,2,3,1:T(4,128)(2,1)S(1)} %get-tuple-element.38), channel_id=1, source_target_pairs={{1,0},{2,1},{3,2},{4,3},{5,4},{6,5},{7,6},{9,8},{10,9},{11,10},{12... | collective-permute-start | bytes 3080 | tf_op jit(solution)/shard_map/ppermute | solution.py:15
  105.1 6.7 %collective-permute-start.8 = (bf16[32,6,1,64]{0,3,2,1:T(8,128)(2,1)S(1)}, bf16[32,6,1,64]{0,3,2,1:T(8,128)(2,1)S(1)}, u32[]{:S(2)}, u32[]{:S(2)}) collective-permute-start(bf16[32,6,1,64]{0,3,2,1:T(8,128)(2,1)S(1)} %get-tuple-element.23), channel_id=1, source_target_pairs={{0,8},{8,16},{16,24},{1,9},{9,17},{17,25},{2,10},{10,18},{18,26},{... | collective-permute-start | bytes 73736 | tf_op jit(solution)/shard_map/ppermute | solution.py:12
  109.5 6.7 %collective-permute-start.9 = (bf16[32,6,1,64]{0,3,2,1:T(8,128)(2,1)S(1)}, bf16[32,6,1,64]{0,3,2,1:T(8,128)(2,1)S(1)}, u32[]{:S(2)}, u32[]{:S(2)}) collective-permute-start(bf16[32,6,1,64]{0,3,2,1:T(8,128)(2,1)S(1)} %get-tuple-element.24), channel_id=1, source_target_pairs={{8,0},{16,8},{24,16},{9,1},{17,9},{25,17},{10,2},{18,10},{26,18},{... | collective-permute-start | bytes 73736 | tf_op jit(solution)/shard_map/ppermute | solution.py:15
  128.1 13.1 %collective-permute-start.36 = (bf16[32,1,4,64]{0,2,3,1:T(4,128)(2,1)S(1)}, bf16[32,1,4,64]{0,2,3,1:T(4,128)(2,1)S(1)}, u32[]{:S(2)}, u32[]{:S(2)}) collective-permute-start(bf16[32,1,4,64]{0,2,3,1:T(4,128)(2,1)S(1)} %get-tuple-element.29), channel_id=1, source_target_pairs={{0,32},{32,64},{64,96},{96,128},{128,160},{160,192},{192,224},{1,3... | collective-permute-start | bytes 49160 | tf_op jit(solution)/shard_map/ppermute | solution.py:12
  132.1 9.1 %collective-permute-start.37 = (bf16[32,1,4,64]{0,2,3,1:T(4,128)(2,1)S(1)}, bf16[32,1,4,64]{0,2,3,1:T(4,128)(2,1)S(1)}, u32[]{:S(2)}, u32[]{:S(2)}) collective-permute-start(bf16[32,1,4,64]{0,2,3,1:T(4,128)(2,1)S(1)} %get-tuple-element.30), channel_id=1, source_target_pairs={{32,0},{64,32},{96,64},{128,96},{160,128},{192,160},{224,192},{33,... | collective-permute-start | bytes 49160 | tf_op jit(solution)/shard_map/ppermute | solution.py:15
  134.0 11.4 %collective-permute-start = (bf16[32,1,8,128]{3,0,2,1:T(8,128)(2,1)S(1)}, bf16[32,1,8,128]{3,0,2,1:T(8,128)(2,1)S(1)}, u32[]{:S(2)}, u32[]{:S(2)}) collective-permute-start(bf16[32,1,8,128]{3,0,2,1:T(8,128)(2,1)S(1)} %copy.186), channel_id=1, source_target_pairs={{0,32},{32,64},{64,96},{96,128},{128,160},{160,192},{192,224},{1,3... | collective-permute-start | bytes 196616 | tf_op jit(solution)/shard_map/ppermute | solution.py:12
  138.0 7.8 %collective-permute-start.1 = (bf16[32,1,8,128]{3,0,2,1:T(8,128)(2,1)S(1)}, bf16[32,1,8,128]{3,0,2,1:T(8,128)(2,1)S(1)}, u32[]{:S(2)}, u32[]{:S(2)}) collective-permute-start(bf16[32,1,8,128]{3,0,2,1:T(8,128)(2,1)S(1)} %copy.187), channel_id=1, source_target_pairs={{32,0},{64,32},{96,64},{128,96},{160,128},{192,160},{224,192},{33,... | collective-permute-start | bytes 196616 | tf_op jit(solution)/shard_map/ppermute | solution.py:15
  142.1 6.6 %collective-permute-start.38 = (bf16[32,6,1,64]{0,2,3,1:T(2,128)(2,1)S(1)}, bf16[32,6,1,64]{0,2,3,1:T(2,128)(2,1)S(1)}, u32[]{:S(2)}, u32[]{:S(2)}) collective-permute-start(bf16[32,6,1,64]{0,2,3,1:T(2,128)(2,1)S(1)} %get-tuple-element.21), channel_id=1, source_target_pairs={{0,8},{8,16},{16,24},{1,9},{9,17},{17,25},{2,10},{10,18},{18,26},{... | collective-permute-start | bytes 73736 | tf_op jit(solution)/shard_map/ppermute | solution.py:12
  144.1 9.3 %collective-permute-start.39 = (bf16[32,6,1,64]{0,2,3,1:T(2,128)(2,1)S(1)}, bf16[32,6,1,64]{0,2,3,1:T(2,128)(2,1)S(1)}, u32[]{:S(2)}, u32[]{:S(2)}) collective-permute-start(bf16[32,6,1,64]{0,2,3,1:T(2,128)(2,1)S(1)} %get-tuple-element.22), channel_id=1, source_target_pairs={{8,0},{16,8},{24,16},{9,1},{17,9},{25,17},{10,2},{18,10},{26,18},{... | collective-permute-start | bytes 73736 | tf_op jit(solution)/shard_map/ppermute | solution.py:15
  153.7 6.7 %collective-permute-start.40 = (bf16[32,6,6,1]{3,0,2,1:T(8,128)(2,1)S(1)}, bf16[32,6,6,1]{3,0,2,1:T(8,128)(2,1)S(1)}, u32[]{:S(2)}, u32[]{:S(2)}) collective-permute-start(bf16[32,6,6,1]{3,0,2,1:T(8,128)(2,1)S(1)} %get-tuple-element.25), channel_id=1, source_target_pairs={{0,1},{1,2},{2,3},{3,4},{4,5},{5,6},{6,7},{8,9},{9,10},{10,11},{11... | collective-permute-start | bytes 6920 | tf_op jit(solution)/shard_map/ppermute | solution.py:12
  157.2 6.9 %collective-permute-start.2 = (bf16[32,10,1,128]{3,0,2,1:T(8,128)(2,1)S(1)}, bf16[32,10,1,128]{3,0,2,1:T(8,128)(2,1)S(1)}, u32[]{:S(2)}, u32[]{:S(2)}) collective-permute-start(bf16[32,10,1,128]{3,0,2,1:T(8,128)(2,1)S(1)} %get-tuple-element.13), channel_id=1, source_target_pairs={{0,8},{8,16},{16,24},{1,9},{9,17},{17,25},{2,10},{10,18},{18,26},{... | collective-permute-start | bytes 245768 | tf_op jit(solution)/shard_map/ppermute | solution.py:12
  159.1 6.3 %collective-permute-start.3 = (bf16[32,10,1,128]{3,0,2,1:T(8,128)(2,1)S(1)}, bf16[32,10,1,128]{3,0,2,1:T(8,128)(2,1)S(1)}, u32[]{:S(2)}, u32[]{:S(2)}) collective-permute-start(bf16[32,10,1,128]{3,0,2,1:T(8,128)(2,1)S(1)} %get-tuple-element.14), channel_id=1, source_target_pairs={{8,0},{16,8},{24,16},{9,1},{17,9},{25,17},{10,2},{18,10},{26,18},{... | collective-permute-start | bytes 245768 | tf_op jit(solution)/shard_map/ppermute | solution.py:15
  167.6 17.8 %collective-permute-start.4 = (bf16[32,10,10,1]{0,2,3,1:T(8,128)(2,1)}, bf16[32,10,10,1]{0,2,3,1:T(8,128)(2,1)}, u32[]{:S(2)}, u32[]{:S(2)}) collective-permute-start(bf16[32,10,10,1]{0,2,3,1:T(8,128)(2,1)} %copy.123), channel_id=1, source_target_pairs={{0,1},{1,2},{2,3},{3,4},{4,5},{5,6},{6,7},{8,9},{9,10},{10,11},{11... | collective-permute-start | bytes 19208 | tf_op jit(solution)/shard_map/ppermute | solution.py:12
  175.5 11.4 %collective-permute-start.5 = (bf16[32,10,10,1]{0,2,3,1:T(8,128)(2,1)}, bf16[32,10,10,1]{0,2,3,1:T(8,128)(2,1)}, u32[]{:S(2)}, u32[]{:S(2)}) collective-permute-start(bf16[32,10,10,1]{0,2,3,1:T(8,128)(2,1)} %copy.124), channel_id=1, source_target_pairs={{1,0},{2,1},{3,2},{4,3},{5,4},{6,5},{7,6},{9,8},{10,9},{11,10},{12... | collective-permute-start | bytes 19208 | tf_op jit(solution)/shard_map/ppermute | solution.py:15
  (24 other events, 523.1 us)
where the time goes:
time: 228 us; the launch traced here: 225 us
  starting transfers between devices  102 us (45%)
  local copies, waits for them, and re-layouts  48.1 us (21%)
  waiting for transfers between devices  47.1 us (21%)
  matrix products  13.1 us (6%)
  other arithmetic  13 us (6%)
    ppermute x21, starting transfers between devices, padded_2(): lax.ppermute(lax.slice_in_dim(block, block.shape[dim] - width, None, axis...  70.2 us
    ppermute x21, waiting for transfers between devices, padded_2(): lax.ppermute(lax.slice_in_dim(block, 0, width, axis=dim), axis, backward)  44 us
    ppermute x21, starting transfers between devices, padded_2(): lax.ppermute(lax.slice_in_dim(block, 0, width, axis=dim), axis, backward)  32 us
    conv_general_dilated x14, local copies, waits for them, and re-layouts, conv_valid(): lax.conv_general_dilated(padded[None], kernel, (1, 1, 1), 'VALID', dimens...  20.8 us
    conv_general_dilated x4, matrix products, conv_valid(): lax.conv_general_dilated(padded[None], kernel, (1, 1, 1), 'VALID', dimens...  12.4 us
    reduce_sum x4, other arithmetic, restrict(): return jnp.mean(blocks, axis=(2, 4, 6)).astype(jnp.bfloat16)  5.33 us
    unnamed x37, local copies, waits for them, and re-layouts  5.2 us
  transfers between devices with their start and end apart: 42, of which 16 were waited for; matrix products, arithmetic and copies ran while one was open for 9% of the time, Pallas kernels for 0%

commit v1 on v0

v1 whole, which is shorter than its diff:
```python
import jax
import jax.numpy as jnp
import numpy as np
from jax import lax
from jax.experimental import pallas as pl
from jax.experimental.pallas import tpu as pltpu
from jax.sharding import PartitionSpec as P

INTERPRET = False
F32, BF16 = jnp.float32, jnp.bfloat16
LANES = 128


def tables():
    r1 = np.zeros((512, 128), np.float32)
    r2 = np.zeros((512, 128), np.float32)
    r3 = np.zeros((512, 384), np.float32)
    for s in range(4):
        base = s * 128
        for z in range(128):
            r1[base + z, 2 + z // 2] = 0.125
        r1[base, 72 + s] = 1.0
        r1[base + 127, 76 + s] = 1.0
        for z in range(64):
            r2[base + 2 + z, 2 + z // 2] = 0.125
        for k, lane in enumerate((2, 3, 72, 73, 74, 75)):
            r2[base + lane, 40 + 6 * s + k] = 1.0
        for k, lane in enumerate((76, 77, 78, 79, 64, 65)):
            r2[base + lane, 64 + 6 * s + k] = 1.0
        for z in range(32):
            r3[base + 2 + z, 2 + z // 2] = 0.125
        for sub in range(4):
            tile = (2 * (s // 2) + sub // 2) * 4 + 2 * (s % 2) + sub % 2
            for k in range(6):
                r3[base + 40 + 6 * sub + k, 128 + 6 * tile + k] = 1.0
                r3[base + 64 + 6 * sub + k, 256 + 6 * tile + k] = 1.0
        for k in range(2):
            r3[base + 2 + k, 128 + 96 + 2 * s + k] = 1.0
            r3[base + 32 + k, 256 + 96 + 2 * s + k] = 1.0
            for half in range(2):
                r3[base + 2 + 2 * k + half, 128 + 104 + k] = 0.125
                r3[base + 30 + 2 * k + half, 256 + 104 + k] = 0.125
    up = np.zeros((128, 128), np.float32)
    up0 = np.zeros((128, 128), np.float32)
    for out in range(128):
        step = -1 if out % 2 == 0 else 1
        centre = out // 2 + 1
        if 0 <= centre + step:
            up[centre, out] += 0.75
            up[centre + step, out] += 0.25
        centre = out // 2 + 2
        up0[centre, out] += 0.75
        up0[centre + step, out] += 0.25
    return tuple(m.astype(BF16) for m in (r1, r2, r3, up, up0))


def dot(a, b):
    return jnp.dot(a, b, preferred_element_type=F32)


def call(kernel, outs, args, scratch=(), scalars=1):
    specs = [pl.BlockSpec(memory_space=pltpu.SMEM)] * scalars
    specs += [pl.BlockSpec(memory_space=pltpu.VMEM)] * (len(args) - scalars)
    return pl.pallas_call(
        kernel,
        out_shape=[jax.ShapeDtypeStruct(shape, BF16) for shape in outs],
        in_specs=specs,
        out_specs=[pl.BlockSpec(memory_space=pltpu.VMEM)] * len(outs),
        scratch_shapes=list(scratch),
        compiler_params=pltpu.CompilerParams(vmem_limit_bytes=48 * 1024 * 1024),
        interpret=INTERPRET,
    )(*args)


def restrict_kernel(field, r1, r2, r3, x_out, t1_out, t2_out, t3_out, msg_out, rows):
    rows[...] = field[...].astype(F32).reshape(2048, LANES)
    for x in range(8):
        for y in range(8):
            x_out[x, y] = rows[pl.ds(x * 8 + y, 32, stride=64), :].astype(BF16)

    def four(ref, x, y):
        return jnp.concatenate(
            [ref[2 * x, 2 * y], ref[2 * x, 2 * y + 1], ref[2 * x + 1, 2 * y], ref[2 * x + 1, 2 * y + 1]],
            axis=1,
        )

    for x in range(4):
        left = jnp.concatenate([four(x_out, x, y) for y in range(4)], axis=0)
        t1_out[x] = dot(left, r1[...]).astype(BF16).reshape(4, 32, LANES)
    left = jnp.concatenate([four(t1_out, x, y) for x in range(2) for y in range(2)], axis=0)
    t2_out[...] = dot(left, r2[...]).astype(BF16).reshape(2, 2, 32, LANES)
    t3 = dot(four(t2_out, 0, 0), r3[...]).astype(BF16)
    t3_out[...] = t3[:, :128]
    msg_out[0] = t3[:, 128:256]
    msg_out[1] = t3[:, 256:]


def lanes():
    return lax.broadcasted_iota(jnp.int32, (32, LANES), 1)


def rolled(value, shift):
    shift %= LANES
    return pltpu.roll(value, shift, 1) if shift else value


def depth_kernel(flags, x_ref, t1, t2, t3, from_lo, from_hi, t1_out, t2_out, t3_out, lo_out, hi_out):
    lane = lanes()
    low = jnp.where(flags[4] > 0, from_lo[...].astype(F32), 0.0)
    high = jnp.where(flags[5] > 0, from_hi[...].astype(F32), 0.0)

    def joined(own, mask_lo, shift_lo, mask_hi, shift_hi):
        value = own.astype(F32)
        value = jnp.where(mask_lo, rolled(low, shift_lo), value)
        return jnp.where(mask_hi, rolled(high, shift_hi), value).astype(BF16)

    mask_lo = (lane >= 124) | (lane < 2)
    mask_hi = (lane >= 66) & (lane < 72)
    for x in range(4):
        for y in range(4):
            tile = 4 * x + y
            value = joined(t1[x, y], mask_lo, 124 - 6 * tile, mask_hi, 66 - 6 * tile)
            t1_out[x, y] = value
            (lo_out if x < 2 else hi_out)[8 + 4 * (x % 2) + y] = value
    for x in range(2):
        for y in range(2):
            tile = 2 * x + y
            value = joined(
                t2[x, y], lane < 2, 32 - 2 * tile, (lane >= 34) & (lane < 36), 34 - 96 - 2 * tile
            )
            t2_out[x, y] = value
            lo_out[16 + tile] = value
            hi_out[16 + tile] = value
    value = joined(t3[...], lane < 2, 24, (lane >= 18) & (lane < 20), 18 - 104)
    t3_out[...] = value
    lo_out[20] = value
    hi_out[20] = value
    lo_out[0:8] = x_ref[0]
    hi_out[0:8] = x_ref[7]


def kept(flag, value):
    return jnp.where(flag > 0, value, jnp.zeros_like(value))


def width_kernel(flags, x_ref, t1, t2, t3, xr_lo, xr_hi, xr_lo2, xr_hi2, lo_out, hi_out, two_out):
    has_lo, has_hi, has_lo2, has_hi2 = flags[0], flags[1], flags[6], flags[7]
    for out, fine_y, half_y in ((lo_out, 0, 0), (hi_out, 7, 2)):
        out[0] = kept(has_lo, xr_lo[fine_y])
        out[9] = kept(has_hi, xr_hi[fine_y])
        for x in range(8):
            out[1 + x] = x_ref[x, fine_y]
        for x in range(2):
            for y in range(2):
                out[10 + 2 * x + y] = kept(has_lo, xr_lo[8 + 4 * x + half_y + y])
                out[10 + 2 * (x + 6) + y] = kept(has_hi, xr_hi[8 + 4 * x + half_y + y])
                out[26 + 2 * x + y] = kept(has_lo, xr_lo[16 + 2 * x + y])
                out[26 + 2 * (x + 4) + y] = kept(has_hi, xr_hi[16 + 2 * x + y])
                out[26 + 2 * (x + 2) + y] = t2[x, y]
        for x in range(4):
            for y in range(2):
                out[10 + 2 * (x + 2) + y] = t1[x, half_y + y]
        row = (
            kept(has_lo2, xr_lo2[...]),
            kept(has_lo, xr_lo[20]),
            t3[...],
            kept(has_hi, xr_hi[20]),
            kept(has_hi2, xr_hi2[...]),
        )
        for x in range(5):
            out[38 + x] = row[x]
            two_out[x] = row[x]


def final_kernel(
    flags, x_ref, t1, t2, t3, xr_lo, xr_hi, xr_lo2, xr_hi2, yr_lo, yr_hi, yr_two,
    w0, mix, w1, w2, w3, up, up0, out_ref, f0, e0, f1, e1, e2, e3, v3, v2, v1, q1, rows,
):
    x_lo, x_hi, y_lo, y_hi, z_lo, z_hi, x_lo2, x_hi2, y_lo2, y_hi2 = (flags[i] for i in range(10))
    lane = lanes()

    def spread(ref, i, j, value):
        wide = value.astype(F32)
        ref[i, j, 0:32] = rolled(wide, 1).astype(BF16)
        ref[i, j, 32:64] = value
        ref[i, j, 64:96] = rolled(wide, -1).astype(BF16)

    for i in range(5):
        spread(e3, i, 0, kept(y_lo2, yr_two[i]))
        spread(e3, i, 1, kept(y_lo, yr_lo[38 + i]))
        spread(e3, i, 3, kept(y_hi, yr_hi[38 + i]))
        spread(e3, i, 4, kept(y_hi2, yr_two[i]))
    spread(e3, 0, 2, kept(x_lo2, xr_lo2[...]))
    spread(e3, 1, 2, kept(x_lo, xr_lo[20]))
    spread(e3, 2, 2, t3[...])
    spread(e3, 3, 2, kept(x_hi, xr_hi[20]))
    spread(e3, 4, 2, kept(x_hi2, xr_hi2[...]))
    for i in range(6):
        for k in range(2):
            spread(e2, i, k, kept(y_lo, yr_lo[26 + 2 * i + k]))
            spread(e2, i, 4 + k, kept(y_hi, yr_hi[26 + 2 * i + k]))
    for i in range(2):
        for k in range(2):
            spread(e2, i, 2 + k, kept(x_lo, xr_lo[16 + 2 * i + k]))
            spread(e2, 2 + i, 2 + k, t2[i, k])
            spread(e2, 4 + i, 2 + k, kept(x_hi, xr_hi[16 + 2 * i + k]))
    for i in range(8):
        for k in range(2):
            f1[i, k] = kept(y_lo, yr_lo[10 + 2 * i + k])
            f1[i, 6 + k] = kept(y_hi, yr_hi[10 + 2 * i + k])
    for i in range(2):
        for k in range(4):
            f1[i, 2 + k] = kept(x_lo, xr_lo[8 + 4 * i + k])
            f1[6 + i, 2 + k] = kept(x_hi, xr_hi[8 + 4 * i + k])
    f1[2:6, 2:6] = t1[...]

    def fill1(i, carry):
        for j in range(8):
            spread(e1, i, j, f1[i, j])
        return carry

    lax.fori_loop(0, 8, fill1, 0)

    for i in range(10):
        f0[i, 0] = kept(y_lo, yr_lo[i])
        f0[i, 9] = kept(y_hi, yr_hi[i])
    for k in range(8):
        f0[0, 1 + k] = kept(x_lo, xr_lo[k])
        f0[9, 1 + k] = kept(x_hi, xr_hi[k])
    f0[1:9, 1:9] = x_ref[...]

    def fill0(half, carry):
        for part in range(2):
            i = 2 * half + part
            coarse = half + 1 + part
            sx = 1 - part
            for j in range(10):
                s = 2 * sx + (j + 1) % 2
                value = f0[i, j]
                wide = value.astype(F32)
                column = f1[coarse, (j + 1) // 2 + 1].astype(F32)
                e0[i, j, 0:32] = jnp.where(lane == 0, rolled(column, 4 - s), rolled(wide, 1)).astype(BF16)
                e0[i, j, 32:64] = value
                e0[i, j, 64:96] = jnp.where(lane == 127, rolled(column, 59 - s), rolled(wide, -1)).astype(BF16)
        return carry

    lax.fori_loop(0, 5, fill0, 0)

    def gathered(ref, x, ys):
        return jnp.concatenate(
            [
                jnp.concatenate([ref[x + d, y : y + 3].reshape(288, LANES) for y in ys], axis=1)
                for d in range(3)
            ],
            axis=0,
        )

    def weighted(weight, value):
        return lax.dot_general(weight, value, (((0,), (0,)), ((), ())), preferred_element_type=F32)

    def along(before, centre, after):
        return [0.75 * centre + 0.25 * before, 0.75 * centre + 0.25 * after]

    def limits(count):
        inside = (lane >= 1) & (lane <= count + 2)
        inside &= (lane != 1) | (z_lo > 0)
        return inside & ((lane != count + 2) | (z_hi > 0))

    def cell_flag(position, last, lo, hi):
        return lo if position == 0 else hi if position == last else None

    def prolonged(ref, count):
        wide = dot(ref[...].reshape(count * count * 32, LANES), up[...]).reshape(count, count, 32, LANES)
        made = 2 * count - 2

        def refined(cells):
            out = []
            for k in range(made):
                cell = k - 1
                centre = cell // 2 + 1
                other = centre - 1 if cell % 2 == 0 else centre + 1
                out.append(0.75 * cells[centre] + 0.25 * cells[other])
            return out

        by_x = refined([wide[i] for i in range(count)])
        return [refined([row[j] for j in range(count)]) for row in by_x]

    def level(e_ref, w_ref, v_ref, size, cells, above):
        keep = limits(cells)
        for i in range(size):
            for j in range(0, size, 2):
                ys = [j, j + 1] if j + 1 < size else [j]
                value = weighted(w_ref[...], gathered(e_ref, i, ys))
                for n, y in enumerate(ys):
                    part = value[:, LANES * n : LANES * (n + 1)]
                    if above is not None:
                        part = part + above[i][y]
                    good = keep
                    for flag in (cell_flag(i, size - 1, x_lo, x_hi), cell_flag(y, size - 1, y_lo, y_hi)):
                        if flag is not None:
                            good = good & (flag > 0)
                    v_ref[i, y] = jnp.where(good, part, 0.0).astype(BF16)

    level(e3, w3, v3, 3, 16, None)
    level(e2, w2, v2, 4, 32, prolonged(v3, 3))
    level(e1, w1, v1, 6, 64, prolonged(v2, 4))
    for i in range(6):
        q1[i] = dot(v1[i].reshape(6 * 32, LANES), up0[...]).reshape(6, 32, LANES)

    weight = jnp.concatenate([w0[...], mix[...]], axis=0)

    def fine(c, carry):
        for part in range(2):
            x = 2 * c + part
            row = 0.75 * q1[c + 1] + 0.25 * q1[c + 2 * part]
            for y in range(0, 8, 2):
                middle = jnp.concatenate([f0[x + 1, y + 1], f0[x + 1, y + 2]], axis=1)
                value = weighted(weight, jnp.concatenate([gathered(e0, x, [y, y + 1]), middle], axis=0))
                centre = y // 2 + 1
                for n, extra in enumerate(along(row[centre - 1], row[centre], row[centre + 1])):
                    total = value[:, LANES * n : LANES * (n + 1)] + extra
                    rows[pl.ds(x * 8 + y + n, 32, stride=64), :] = jax.nn.gelu(total, approximate=True)
        return carry

    lax.fori_loop(0, 4, fine, 0)
    out_ref[...] = rows[...].reshape(32, 8, 8, LANES).astype(BF16)


def turned(value, axis, step):
    count = lax.axis_size(axis)
    return lax.ppermute(value, axis, [(i, (i + step) % count) for i in range(count)])


def on_device(field, mixing, kernel_fine, kernel_half, kernel_quarter, kernel_eighth):
    gx, gy, gz = (lax.axis_index(a) for a in ("gx", "gy", "gz"))
    nx, ny, nz = (lax.axis_size(a) for a in ("gx", "gy", "gz"))
    slot = lax.iota(jnp.int32, 16)
    place = jnp.where((slot < 2) | (slot == 6) | (slot == 7), gx, jnp.where((slot == 4) | (slot == 5), gz, gy))
    first = np.array([1, 0, 1, 0, 1, 0, 2, 0, 2, 0] + [0] * 6, np.int32)
    last = np.array([nx, nx - 1, ny, ny - 1, nz, nz - 1, nx, nx - 2, ny, ny - 2] + [99] * 6, np.int32)
    flags = ((place >= first) & (place < last)).astype(jnp.int32)
    r1, r2, r3, up, up0 = (jnp.asarray(m) for m in tables())
    tile = (32, LANES)

    x_own, t1, t2, t3, msg = call(
        restrict_kernel,
        [(8, 8) + tile, (4, 4) + tile, (2, 2) + tile, tile, (2,) + tile],
        [field, r1, r2, r3],
        [pltpu.VMEM((2048, LANES), F32)],
        0,
    )
    from_hi = turned(msg[0], "gz", -1)
    from_lo = turned(msg[1], "gz", 1)
    t1, t2, t3, x_msg_lo, x_msg_hi = call(
        depth_kernel,
        [(4, 4) + tile, (2, 2) + tile, tile, (21,) + tile, (21,) + tile],
        [flags, x_own, t1, t2, t3, from_lo, from_hi],
    )
    xr_hi = turned(x_msg_lo, "gx", -1)
    xr_lo = turned(x_msg_hi, "gx", 1)
    xr_hi2 = turned(t3, "gx", -2)
    xr_lo2 = turned(t3, "gx", 2)
    y_msg_lo, y_msg_hi, two = call(
        width_kernel,
        [(43,) + tile, (43,) + tile, (5,) + tile],
        [flags, x_own, t1, t2, t3, xr_lo, xr_hi, xr_lo2, xr_hi2],
    )
    yr_hi = turned(y_msg_lo, "gy", -1)
    yr_lo = turned(y_msg_hi, "gy", 1)
    assert ny == 4
    yr_two = turned(two, "gy", 2)
    flat = [k.reshape(864, 32) for k in (kernel_fine, kernel_half, kernel_quarter, kernel_eighth)]
    (out,) = call(
        final_kernel,
        [(32, 8, 8, LANES)],
        [flags, x_own, t1, t2, t3, xr_lo, xr_hi, xr_lo2, xr_hi2, yr_lo, yr_hi, yr_two,
         flat[0], mixing.T, flat[1], flat[2], flat[3], up, up0],
        [
            pltpu.VMEM((10, 10) + tile, BF16),
            pltpu.VMEM((10, 10, 96, LANES), BF16),
            pltpu.VMEM((8, 8) + tile, BF16),
            pltpu.VMEM((8, 8, 96, LANES), BF16),
            pltpu.VMEM((6, 6, 96, LANES), BF16),
            pltpu.VMEM((5, 5, 96, LANES), BF16),
            pltpu.VMEM((3, 3) + tile, BF16),
            pltpu.VMEM((4, 4) + tile, BF16),
            pltpu.VMEM((6, 6) + tile, BF16),
            pltpu.VMEM((6, 6) + tile, F32),
            pltpu.VMEM((2048, LANES), F32),
        ],
    )
    return out


def solution(mesh):
    placed = (P(None, "gx", "gy", "gz"), P(), P(), P(), P(), P())
    return jax.shard_map(
        on_device, mesh=mesh, in_specs=placed, out_specs=P(None, "gx", "gy", "gz"), check_vma=False
    )
```

time: 228 us -> 47.3 us (0.21)
  the two profiles are of different devices: /device:TPU:64 before, /device:TPU:8 now
where the time goes in v1:
time: 47.3 us; the launch traced here: 47.1 us
  starting transfers between devices  15.6 us (33%)
  waiting for transfers between devices  14.5 us (31%)
  Pallas kernels  12.2 us (26%)
  local copies, waits for them, and re-layouts  4.65 us (10%)
    ppermute x9, starting transfers between devices, turned(): lax.ppermute(value, axis, [(i, (i + step) % count) for i in range(count)])  15.6 us
    ppermute x9, waiting for transfers between devices, turned(): lax.ppermute(value, axis, [(i, (i + step) % count) for i in range(count)])  14.5 us
    pallas_call x4, Pallas kernels, call(): pl.pallas_call(kernel, out_shape=[jax.ShapeDtypeStruct(shape, BF16) for s...  12.2 us
    unnamed x27, local copies, waits for them, and re-layouts  4.64 us
  transfers between devices with their start and end apart: 9, of which 5 were waited for; matrix products, arithmetic and copies ran while one was open for 0% of the time, Pallas kernels for 0%

profile of v1, /device:TPU:8, one launch (start us, length us, event | category | flops | bytes accessed | tf_op | source)
XLA Modules:
  0.0 47.1 jit_solution(3517334543101109491)
XLA Ops:
  0.0 1.0 %copy-done = bf16[32,8,8,128]{3,2,1,0:T(8,128)(2,1)S(1)} copy-done((bf16[32,8,8,128]{3,2,1,0:T(8,128)(2,1)S(1)}, bf16[32,8,8,128]{3,2,1,0:T(8,128)(2,1)}, u32[]{:S(2)}) %copy-start) | copy-done | bytes 524312
  1.0 1.0 %copy-done.1 = bf16[512,384]{1,0:T(8,128)(2,1)S(1)} copy-done((bf16[512,384]{1,0:T(8,128)(2,1)S(1)}, bf16[512,384]{1,0:T(8,128)(2,1)}, u32[]{:S(2)}) %copy-start.1) | copy-done | bytes 393240
  2.0 0.9 %copy-done.6 = bf16[512,128]{1,0:T(8,128)(2,1)S(1)} copy-done((bf16[512,128]{1,0:T(8,128)(2,1)S(1)}, bf16[512,128]{1,0:T(8,128)(2,1)}, u32[]{:S(2)}) %copy-start.6) | copy-done | bytes 131096
  2.9 0.9 %copy-done.7 = bf16[512,128]{1,0:T(8,128)(2,1)S(1)} copy-done((bf16[512,128]{1,0:T(8,128)(2,1)S(1)}, bf16[512,128]{1,0:T(8,128)(2,1)}, u32[]{:S(2)}) %copy-start.7) | copy-done | bytes 131096
  3.8 1.2 %shard_map.127 = (bf16[8,8,32,128]{3,2,1,0:T(8,128)(2,1)S(1)}, bf16[4,4,32,128]{3,2,1,0:T(8,128)(2,1)S(1)}, bf16[2,2,32,128]{3,2,1,0:T(8,128)(2,1)S(1)}, bf16[32...) custom-call(bf16[32,8,8,128]{3,2,1,0:T(8,128)(2,1)S(1)} %copy-done, bf16[512,128]{1,0:T(8,128)(2,1)S(1)} %copy-done.7, ...), custom_call_target="tpu_custom_call" | custom-call | tf_op jit(solution)/shard_map/pallas_call | solution.py:64
  5.1 2.2 %collective-permute-start.1 = (bf16[32,128]{1,0:T(8,128)(2,1)S(1)}, bf16[32,128]{1,0:T(8,128)(2,1)S(1)}, u32[]{:S(2)}, u32[]{:S(2)}) collective-permute-start(bf16[32,128]{1,0:T(8,128)(2,1)S(1)} %get-tuple-element.31), channel_id=1, source_target_pairs={{0,7},{1,0},{2,1},{3,2},{4,3},{5,4},{6,5},{7,6},{8,15},{9,8},{10,9... | collective-permute-start | bytes 24584 | tf_op jit(solution)/shard_map/ppermute | solution.py:331
  7.3 0.0 collective-permute-start
  7.3 0.7 %copy-done.11 = s32[16]{0:T(128)S(1)} copy-done((s32[16]{0:T(128)S(1)}, s32[16]{0:T(128)}, u32[]{:S(2)}) %copy-start.11) | copy-done | bytes 88
  8.0 0.0 copy-done.12
  8.0 0.7 %collective-permute-done.1.from_hi = bf16[32,128]{1,0:T(8,128)(2,1)S(1)} collective-permute-done((bf16[32,128]{1,0:T(8,128)(2,1)S(1)}, bf16[32,128]{1,0:T(8,128)(2,1)S(1)}, u32[]{:S(2)}, u32[]{:S(2)}) %collective-permute-start.1) | collective-permute-done | bytes 8224 | tf_op jit(solution)/shard_map/ppermute | solution.py:331
  8.7 2.9 %collective-permute-done.from_lo = bf16[32,128]{1,0:T(8,128)(2,1)S(1)} collective-permute-done((bf16[32,128]{1,0:T(8,128)(2,1)S(1)}, bf16[32,128]{1,0:T(8,128)(2,1)S(1)}, u32[]{:S(2)}, u32[]{:S(2)}) %collective-permute-start) | collective-permute-done | bytes 8224 | tf_op jit(solution)/shard_map/ppermute | solution.py:331
  11.6 0.7 %shard_map.128 = (bf16[4,4,32,128]{3,2,1,0:T(8,128)(2,1)S(1)}, bf16[2,2,32,128]{3,2,1,0:T(8,128)(2,1)S(1)}, bf16[32,128]{1,0:T(8,128)(2,1)S(1)}, bf16[21,32,128]...) custom-call(s32[16]{0:T(128)S(1)} %and_convert_fusion.flags, bf16[8,8,32,128]{3,2,1,0:T(8,128)(2,1)S(1)} %get-tuple-element.18.x_ref, ...), custom_call_target="tpu_custom_call" | custom-call | tf_op jit(solution)/shard_map/pallas_call | solution.py:64
  12.3 2.0 %collective-permute-start.2 = (bf16[21,32,128]{2,1,0:T(8,128)(2,1)S(1)}, bf16[21,32,128]{2,1,0:T(8,128)(2,1)S(1)}, u32[]{:S(2)}, u32[]{:S(2)}) collective-permute-start(bf16[21,32,128]{2,1,0:T(8,128)(2,1)S(1)} %get-tuple-element.26), channel_id=1, source_target_pairs={{0,32},{32,64},{64,96},{96,128},{128,160},{160,192},{192,224},{224... | collective-permute-start | bytes 516104 | tf_op jit(solution)/shard_map/ppermute | solution.py:331
  14.3 4.0 %collective-permute-start.3 = (bf16[21,32,128]{2,1,0:T(8,128)(2,1)S(1)}, bf16[21,32,128]{2,1,0:T(8,128)(2,1)S(1)}, u32[]{:S(2)}, u32[]{:S(2)}) collective-permute-start(bf16[21,32,128]{2,1,0:T(8,128)(2,1)S(1)} %get-tuple-element.27), channel_id=1, source_target_pairs={{0,224},{32,0},{64,32},{96,64},{128,96},{160,128},{192,160},{224,1... | collective-permute-start | bytes 516104 | tf_op jit(solution)/shard_map/ppermute | solution.py:331
  18.3 2.4 %collective-permute-start.5 = (bf16[32,128]{1,0:T(8,128)(2,1)S(1)}, bf16[32,128]{1,0:T(8,128)(2,1)S(1)}, u32[]{:S(2)}, u32[]{:S(2)}) collective-permute-start(bf16[32,128]{1,0:T(8,128)(2,1)S(1)} %get-tuple-element.25.t3), channel_id=1, source_target_pairs={{0,192},{32,224},{64,0},{96,32},{128,64},{160,96},{192,128},{224,1... | collective-permute-start | bytes 24584 | tf_op jit(solution)/shard_map/ppermute | solution.py:331
  20.7 0.5 %collective-permute-start.4 = (bf16[32,128]{1,0:T(8,128)(2,1)S(1)}, bf16[32,128]{1,0:T(8,128)(2,1)S(1)}, u32[]{:S(2)}, u32[]{:S(2)}) collective-permute-start(bf16[32,128]{1,0:T(8,128)(2,1)S(1)} %get-tuple-element.25.t3), channel_id=1, source_target_pairs={{0,64},{32,96},{64,128},{96,160},{128,192},{160,224},{192,0},{224,... | collective-permute-start | bytes 24584 | tf_op jit(solution)/shard_map/ppermute | solution.py:331
  21.2 1.6 %collective-permute-done.5.xr_hi2 = bf16[32,128]{1,0:T(8,128)(2,1)S(1)} collective-permute-done((bf16[32,128]{1,0:T(8,128)(2,1)S(1)}, bf16[32,128]{1,0:T(8,128)(2,1)S(1)}, u32[]{:S(2)}, u32[]{:S(2)}) %collective-permute-start.5) | collective-permute-done | bytes 8224 | tf_op jit(solution)/shard_map/ppermute | solution.py:331
  22.9 3.6 %collective-permute-done.4.xr_lo2 = bf16[32,128]{1,0:T(8,128)(2,1)S(1)} collective-permute-done((bf16[32,128]{1,0:T(8,128)(2,1)S(1)}, bf16[32,128]{1,0:T(8,128)(2,1)S(1)}, u32[]{:S(2)}, u32[]{:S(2)}) %collective-permute-start.4) | collective-permute-done | bytes 8224 | tf_op jit(solution)/shard_map/ppermute | solution.py:331
  26.5 0.0 collective-permute-done.2.xr_lo
  26.5 0.0 copy-start.2
  26.5 0.0 copy-start.3
  26.5 0.0 copy-start.4
  26.5 0.0 copy-start.5
  26.5 0.0 copy-start.8
  26.5 0.0 copy-start.9
  26.5 0.6 %shard_map.129 = (bf16[43,32,128]{2,1,0:T(8,128)(2,1)S(1)}, bf16[43,32,128]{2,1,0:T(8,128)(2,1)S(1)}, bf16[5,32,128]{2,1,0:T(8,128)(2,1)S(1)}) custom-call(s32[16]{0:T(128)S(1)} %and_convert_fusion.flags, bf16[8,8,32,128]{3,2,1,0:T(8,128)(2,1)S(1)} %get-tuple-element.18.x_ref, bf16[4,4,32,128]{3,2,1,0:T(8,128)(2,1)S(1)} %get-tuple-element.23.t1, ...), custom_call_target="tpu_custom_call" | custom-call | tf_op jit(solution)/shard_map/pallas_call | solution.py:64
  27.2 1.7 %collective-permute-start.6 = (bf16[43,32,128]{2,1,0:T(8,128)(2,1)S(1)}, bf16[43,32,128]{2,1,0:T(8,128)(2,1)S(1)}, u32[]{:S(2)}, u32[]{:S(2)}) collective-permute-start(bf16[43,32,128]{2,1,0:T(8,128)(2,1)S(1)} %get-tuple-element.28), channel_id=1, source_target_pairs={{0,8},{8,16},{16,24},{24,0},{1,9},{9,17},{17,25},{25,1},{2,10},{10... | collective-permute-start | bytes 1056776 | tf_op jit(solution)/shard_map/ppermute | solution.py:331
  28.9 0.5 collective-permute-start.7
  29.3 2.3 %collective-permute-start.8 = (bf16[5,32,128]{2,1,0:T(8,128)(2,1)S(1)}, bf16[5,32,128]{2,1,0:T(8,128)(2,1)S(1)}, u32[]{:S(2)}, u32[]{:S(2)}) collective-permute-start(bf16[5,32,128]{2,1,0:T(8,128)(2,1)S(1)} %get-tuple-element.30), channel_id=1, source_target_pairs={{0,16},{8,24},{16,0},{24,8},{1,17},{9,25},{17,1},{25,9},{2,18},{10... | collective-permute-start | bytes 122888 | tf_op jit(solution)/shard_map/ppermute | solution.py:331
  31.6 0.1 copy.14
  31.7 5.7 %collective-permute-done.8.yr_two = bf16[5,32,128]{2,1,0:T(8,128)(2,1)S(1)} collective-permute-done((bf16[5,32,128]{2,1,0:T(8,128)(2,1)S(1)}, bf16[5,32,128]{2,1,0:T(8,128)(2,1)S(1)}, u32[]{:S(2)}, u32[]{:S(2)}) %collective-permute-start.8) | collective-permute-done | bytes 40992 | tf_op jit(solution)/shard_map/ppermute | solution.py:331
  37.4 9.7 %shard_map.130 = bf16[32,8,8,128]{3,2,1,0:T(8,128)(2,1)} custom-call(s32[16]{0:T(128)S(1)} %and_convert_fusion.flags, bf16[8,8,32,128]{3,2,1,0:T(8,128)(2,1)S(1)} %get-tuple-element.18.x_ref, bf16[4,4,32,128]{3,2,1,0:T(8,128)(2,1)S(1)} %get-tuple-element.23.t1, bf16[2,2,32,128]{3,2,1,0:T(8,128)(2,1)S(1)} %get-tuple-element.24.t2, ...), custom_call_target="tpu_custom_call" | custom-call | tf_op jit(solution)/shard_map/pallas_call | solution.py:64
  (19 shorter events, 0.0 us)
Async XLA Ops:
  0.0 1.0 %copy-start = (bf16[32,8,8,128]{3,2,1,0:T(8,128)(2,1)S(1)}, bf16[32,8,8,128]{3,2,1,0:T(8,128)(2,1)}, u32[]{:S(2)}) copy-start(bf16[32,8,8,128]{3,2,1,0:T(8,128)(2,1)} %field.1) | copy-start | bytes 1572868
  1.0 1.0 %copy-start.1 = (bf16[512,384]{1,0:T(8,128)(2,1)S(1)}, bf16[512,384]{1,0:T(8,128)(2,1)}, u32[]{:S(2)}) copy-start(bf16[512,384]{1,0:T(8,128)(2,1)} %constant.40.clone.r3) | copy-start | bytes 1179652
  2.0 0.9 %copy-start.6 = (bf16[512,128]{1,0:T(8,128)(2,1)S(1)}, bf16[512,128]{1,0:T(8,128)(2,1)}, u32[]{:S(2)}) copy-start(bf16[512,128]{1,0:T(8,128)(2,1)} %constant.39.clone.r2) | copy-start | bytes 393220
  2.9 0.9 %copy-start.7 = (bf16[512,128]{1,0:T(8,128)(2,1)S(1)}, bf16[512,128]{1,0:T(8,128)(2,1)}, u32[]{:S(2)}) copy-start(bf16[512,128]{1,0:T(8,128)(2,1)} %constant.38.clone.r1) | copy-start | bytes 393220
  5.1 3.6 %collective-permute-start.1 = (bf16[32,128]{1,0:T(8,128)(2,1)S(1)}, bf16[32,128]{1,0:T(8,128)(2,1)S(1)}, u32[]{:S(2)}, u32[]{:S(2)}) collective-permute-start(bf16[32,128]{1,0:T(8,128)(2,1)S(1)} %get-tuple-element.31), channel_id=1, source_target_pairs={{0,7},{1,0},{2,1},{3,2},{4,3},{5,4},{6,5},{7,6},{8,15},{9,8},{10,9... | collective-permute-start | bytes 24584 | tf_op jit(solution)/shard_map/ppermute | solution.py:331
  7.3 4.3 %collective-permute-start = (bf16[32,128]{1,0:T(8,128)(2,1)S(1)}, bf16[32,128]{1,0:T(8,128)(2,1)S(1)}, u32[]{:S(2)}, u32[]{:S(2)}) collective-permute-start(bf16[32,128]{1,0:T(8,128)(2,1)S(1)} %get-tuple-element.32), channel_id=1, source_target_pairs={{0,1},{1,2},{2,3},{3,4},{4,5},{5,6},{6,7},{7,0},{8,9},{9,10},{10,1... | collective-permute-start | bytes 24584 | tf_op jit(solution)/shard_map/ppermute | solution.py:331
  7.3 0.7 %copy-start.11 = (s32[16]{0:T(128)S(1)}, s32[16]{0:T(128)}, u32[]{:S(2)}) copy-start(s32[16]{0:T(128)} %constant.37.clone) | copy-start | bytes 196
  7.3 0.7 %copy-start.12 = (s32[16]{0:T(128)S(1)}, s32[16]{0:T(128)}, u32[]{:S(2)}) copy-start(s32[16]{0:T(128)} %constant.36.clone) | copy-start | bytes 196
  12.3 14.2 %collective-permute-start.2 = (bf16[21,32,128]{2,1,0:T(8,128)(2,1)S(1)}, bf16[21,32,128]{2,1,0:T(8,128)(2,1)S(1)}, u32[]{:S(2)}, u32[]{:S(2)}) collective-permute-start(bf16[21,32,128]{2,1,0:T(8,128)(2,1)S(1)} %get-tuple-element.26), channel_id=1, source_target_pairs={{0,32},{32,64},{64,96},{96,128},{128,160},{160,192},{192,224},{224... | collective-permute-start | bytes 516104 | tf_op jit(solution)/shard_map/ppermute | solution.py:331
  14.3 12.2 %collective-permute-start.3 = (bf16[21,32,128]{2,1,0:T(8,128)(2,1)S(1)}, bf16[21,32,128]{2,1,0:T(8,128)(2,1)S(1)}, u32[]{:S(2)}, u32[]{:S(2)}) collective-permute-start(bf16[21,32,128]{2,1,0:T(8,128)(2,1)S(1)} %get-tuple-element.27), channel_id=1, source_target_pairs={{0,224},{32,0},{64,32},{96,64},{128,96},{160,128},{192,160},{224,1... | collective-permute-start | bytes 516104 | tf_op jit(solution)/shard_map/ppermute | solution.py:331
  18.3 4.5 %collective-permute-start.5 = (bf16[32,128]{1,0:T(8,128)(2,1)S(1)}, bf16[32,128]{1,0:T(8,128)(2,1)S(1)}, u32[]{:S(2)}, u32[]{:S(2)}) collective-permute-start(bf16[32,128]{1,0:T(8,128)(2,1)S(1)} %get-tuple-element.25.t3), channel_id=1, source_target_pairs={{0,192},{32,224},{64,0},{96,32},{128,64},{160,96},{192,128},{224,1... | collective-permute-start | bytes 24584 | tf_op jit(solution)/shard_map/ppermute | solution.py:331
  20.7 5.8 %collective-permute-start.4 = (bf16[32,128]{1,0:T(8,128)(2,1)S(1)}, bf16[32,128]{1,0:T(8,128)(2,1)S(1)}, u32[]{:S(2)}, u32[]{:S(2)}) collective-permute-start(bf16[32,128]{1,0:T(8,128)(2,1)S(1)} %get-tuple-element.25.t3), channel_id=1, source_target_pairs={{0,64},{32,96},{64,128},{96,160},{128,192},{160,224},{192,0},{224,... | collective-permute-start | bytes 24584 | tf_op jit(solution)/shard_map/ppermute | solution.py:331
  26.5 5.1 %copy-start.10 = (bf16[32,32]{1,0:T(8,128)(2,1)S(1)}, bf16[32,32]{1,0:T(8,128)(2,1)}, u32[]{:S(2)}) copy-start(bf16[32,32]{1,0:T(8,128)(2,1)} %param.14) | copy-start | bytes 6148
  26.5 10.9 %copy-start.2 = (bf16[3,3,3,32,32]{4,3,2,1,0:T(8,128)(2,1)S(1)}, bf16[3,3,3,32,32]{4,3,2,1,0:T(8,128)(2,1)}, u32[]{:S(2)}) copy-start(bf16[3,3,3,32,32]{4,3,2,1,0:T(8,128)(2,1)} %param.15) | copy-start | bytes 165892
  26.5 10.9 %copy-start.3 = (bf16[3,3,3,32,32]{4,3,2,1,0:T(8,128)(2,1)S(1)}, bf16[3,3,3,32,32]{4,3,2,1,0:T(8,128)(2,1)}, u32[]{:S(2)}) copy-start(bf16[3,3,3,32,32]{4,3,2,1,0:T(8,128)(2,1)} %param.16) | copy-start | bytes 165892
  26.5 10.9 %copy-start.4 = (bf16[3,3,3,32,32]{4,3,2,1,0:T(8,128)(2,1)S(1)}, bf16[3,3,3,32,32]{4,3,2,1,0:T(8,128)(2,1)}, u32[]{:S(2)}) copy-start(bf16[3,3,3,32,32]{4,3,2,1,0:T(8,128)(2,1)} %param.17) | copy-start | bytes 165892
  26.5 10.9 %copy-start.5 = (bf16[3,3,3,32,32]{4,3,2,1,0:T(8,128)(2,1)S(1)}, bf16[3,3,3,32,32]{4,3,2,1,0:T(8,128)(2,1)}, u32[]{:S(2)}) copy-start(bf16[3,3,3,32,32]{4,3,2,1,0:T(8,128)(2,1)} %param.18) | copy-start | bytes 165892
  26.5 10.9 %copy-start.8 = (bf16[128,128]{1,0:T(8,128)(2,1)S(1)}, bf16[128,128]{1,0:T(8,128)(2,1)}, u32[]{:S(2)}) copy-start(bf16[128,128]{1,0:T(8,128)(2,1)} %constant.42.clone.up0) | copy-start | bytes 98308
  26.5 10.9 %copy-start.9 = (bf16[128,128]{1,0:T(8,128)(2,1)S(1)}, bf16[128,128]{1,0:T(8,128)(2,1)}, u32[]{:S(2)}) copy-start(bf16[128,128]{1,0:T(8,128)(2,1)} %constant.41.clone.up) | copy-start | bytes 98308
  27.2 10.2 %collective-permute-start.6 = (bf16[43,32,128]{2,1,0:T(8,128)(2,1)S(1)}, bf16[43,32,128]{2,1,0:T(8,128)(2,1)S(1)}, u32[]{:S(2)}, u32[]{:S(2)}) collective-permute-start(bf16[43,32,128]{2,1,0:T(8,128)(2,1)S(1)} %get-tuple-element.28), channel_id=1, source_target_pairs={{0,8},{8,16},{16,24},{24,0},{1,9},{9,17},{17,25},{25,1},{2,10},{10... | collective-permute-start | bytes 1056776 | tf_op jit(solution)/shard_map/ppermute | solution.py:331
  28.9 8.5 %collective-permute-start.7 = (bf16[43,32,128]{2,1,0:T(8,128)(2,1)S(1)}, bf16[43,32,128]{2,1,0:T(8,128)(2,1)S(1)}, u32[]{:S(2)}, u32[]{:S(2)}) collective-permute-start(bf16[43,32,128]{2,1,0:T(8,128)(2,1)S(1)} %get-tuple-element.29), channel_id=1, source_target_pairs={{0,24},{8,0},{16,8},{24,16},{1,25},{9,1},{17,9},{25,17},{2,26},{10... | collective-permute-start | bytes 1056776 | tf_op jit(solution)/shard_map/ppermute | solution.py:331
  29.3 8.0 %collective-permute-start.8 = (bf16[5,32,128]{2,1,0:T(8,128)(2,1)S(1)}, bf16[5,32,128]{2,1,0:T(8,128)(2,1)S(1)}, u32[]{:S(2)}, u32[]{:S(2)}) collective-permute-start(bf16[5,32,128]{2,1,0:T(8,128)(2,1)S(1)} %get-tuple-element.30), channel_id=1, source_target_pairs={{0,16},{8,24},{16,0},{24,8},{1,17},{9,25},{17,1},{25,9},{2,18},{10... | collective-permute-start | bytes 122888 | tf_op jit(solution)/shard_map/ppermute | solution.py:331

commit v2 on v1

v2 whole, which is shorter than its diff:
```python
import jax
import jax.numpy as jnp
import numpy as np
from jax import lax
from jax.experimental import pallas as pl
from jax.experimental.pallas import tpu as pltpu
from jax.sharding import PartitionSpec as P

INTERPRET = False
F32, BF16 = jnp.float32, jnp.bfloat16
LANES = 128


def tables():
    r1 = np.zeros((512, 128), np.float32)
    r2 = np.zeros((512, 128), np.float32)
    r3 = np.zeros((512, 384), np.float32)
    for s in range(4):
        base = s * 128
        for z in range(128):
            r1[base + z, 2 + z // 2] = 0.125
        r1[base, 72 + s] = 1.0
        r1[base + 127, 76 + s] = 1.0
        for z in range(64):
            r2[base + 2 + z, 2 + z // 2] = 0.125
        for k, lane in enumerate((2, 3, 72, 73, 74, 75)):
            r2[base + lane, 40 + 6 * s + k] = 1.0
        for k, lane in enumerate((76, 77, 78, 79, 64, 65)):
            r2[base + lane, 64 + 6 * s + k] = 1.0
        for z in range(32):
            r3[base + 2 + z, 2 + z // 2] = 0.125
        for sub in range(4):
            tile = (2 * (s // 2) + sub // 2) * 4 + 2 * (s % 2) + sub % 2
            for k in range(6):
                r3[base + 40 + 6 * sub + k, 128 + 6 * tile + k] = 1.0
                r3[base + 64 + 6 * sub + k, 256 + 6 * tile + k] = 1.0
        for k in range(2):
            r3[base + 2 + k, 128 + 96 + 2 * s + k] = 1.0
            r3[base + 32 + k, 256 + 96 + 2 * s + k] = 1.0
            for half in range(2):
                r3[base + 2 + 2 * k + half, 128 + 104 + k] = 0.125
                r3[base + 30 + 2 * k + half, 256 + 104 + k] = 0.125
    up = np.zeros((128, 128), np.float32)
    up0 = np.zeros((128, 128), np.float32)
    for out in range(128):
        step = -1 if out % 2 == 0 else 1
        centre = out // 2 + 1
        if 0 <= centre + step:
            up[centre, out] += 0.75
            up[centre + step, out] += 0.25
        centre = out // 2 + 2
        up0[centre, out] += 0.75
        up0[centre + step, out] += 0.25
    return tuple(m.astype(BF16) for m in (np.concatenate([r1, r2, r3], axis=1), up, up0))


def dot(a, b):
    return jnp.dot(a, b, preferred_element_type=F32)


def call(kernel, outs, args, scratch=(), scalars=1, space=pltpu.VMEM, kind=BF16, flops=1 << 20):
    specs = [pl.BlockSpec(memory_space=pltpu.SMEM)] * scalars
    specs += [pl.BlockSpec(memory_space=space)] * (len(args) - scalars)
    return pl.pallas_call(
        kernel,
        out_shape=[jax.ShapeDtypeStruct(shape, kind) for shape in outs],
        in_specs=specs,
        out_specs=[pl.BlockSpec(memory_space=pltpu.VMEM)] * len(outs),
        scratch_shapes=list(scratch),
        compiler_params=pltpu.CompilerParams(vmem_limit_bytes=48 * 1024 * 1024),
        cost_estimate=pl.CostEstimate(flops=flops, transcendentals=0, bytes_accessed=1 << 20),
        interpret=INTERPRET,
    )(*args)


def restrict_kernel(field_hbm, table_hbm, x_out, t1_out, t2_out, t3_out, msg_out, field, table, rows, sems):
    copies = [
        pltpu.make_async_copy(field_hbm, field, sems.at[0]),
        pltpu.make_async_copy(table_hbm, table, sems.at[1]),
    ]
    for copy in copies:
        copy.start()
    copies[0].wait()
    rows[...] = field[...].astype(F32).reshape(2048, LANES)
    for x in range(8):
        for y in range(8):
            x_out[x, y] = rows[pl.ds(x * 8 + y, 32, stride=64), :].astype(BF16)
    copies[1].wait()

    def four(ref, x, y):
        return jnp.concatenate(
            [ref[2 * x, 2 * y], ref[2 * x, 2 * y + 1], ref[2 * x + 1, 2 * y], ref[2 * x + 1, 2 * y + 1]],
            axis=1,
        )

    for x in range(4):
        left = jnp.concatenate([four(x_out, x, y) for y in range(4)], axis=0)
        t1_out[x] = dot(left, table[:, 0:128]).astype(BF16).reshape(4, 32, LANES)
    left = jnp.concatenate([four(t1_out, x, y) for x in range(2) for y in range(2)], axis=0)
    t2_out[...] = dot(left, table[:, 128:256]).astype(BF16).reshape(2, 2, 32, LANES)
    t3 = dot(four(t2_out, 0, 0), table[:, 256:640]).astype(BF16)
    t3_out[...] = t3[:, :128]
    msg_out[0] = t3[:, 128:256]
    msg_out[1] = t3[:, 256:]


def lanes():
    return lax.broadcasted_iota(jnp.int32, (32, LANES), 1)


def rolled(value, shift):
    shift %= LANES
    return pltpu.roll(value, shift, 1) if shift else value


def depth_kernel(flags, x_ref, t1, t2, t3, from_lo, from_hi, t1_out, t2_out, t3_out, lo_out, hi_out):
    lane = lanes()
    low = jnp.where(flags[4] > 0, from_lo[...].astype(F32), 0.0)
    high = jnp.where(flags[5] > 0, from_hi[...].astype(F32), 0.0)

    def joined(own, mask_lo, shift_lo, mask_hi, shift_hi):
        value = own.astype(F32)
        value = jnp.where(mask_lo, rolled(low, shift_lo), value)
        return jnp.where(mask_hi, rolled(high, shift_hi), value)

    extra = []
    for x in range(2):
        for y in range(2):
            tile = 2 * x + y
            value = joined(
                t2[x, y], lane < 2, 32 - 2 * tile, (lane >= 34) & (lane < 36), 34 - 96 - 2 * tile
            )
            t2_out[x, y] = value.astype(BF16)
            extra.append(rolled(value, 72))
    value = joined(t3[...], lane < 2, 24, (lane >= 18) & (lane < 20), 18 - 104)
    t3_out[...] = value.astype(BF16)
    extra.append(rolled(value, 72))
    free = (lane >= 72) & (lane < 108)
    mask_lo = (lane >= 124) | (lane < 2)
    mask_hi = (lane >= 66) & (lane < 72)
    for x in range(4):
        for y in range(4):
            tile = 4 * x + y
            value = joined(t1[x, y], mask_lo, 124 - 6 * tile, mask_hi, 66 - 6 * tile)
            t1_out[x, y] = value.astype(BF16)
            k = tile % 8
            if k < 5:
                value = jnp.where(free, extra[k], value)
            (lo_out if x < 2 else hi_out)[8 + k] = value.astype(BF16)
    lo_out[0:8] = x_ref[0]
    hi_out[0:8] = x_ref[7]


def kept(flag, value):
    return jnp.where(flag > 0, value, jnp.zeros_like(value))


def width_kernel(flags, x_ref, t1, t2, t3, xr_lo, xr_hi, xr_lo2, xr_hi2, lo_out, hi_out, two_out):
    has_lo, has_hi, has_lo2, has_hi2 = flags[0], flags[1], flags[6], flags[7]
    lane = lanes()
    free = (lane >= 72) & (lane < 124)
    row = [
        rolled(kept(has_lo2, xr_lo2[...]).astype(F32), 0),
        rolled(kept(has_lo, xr_lo[12]).astype(F32), -72),
        t3[...].astype(F32),
        rolled(kept(has_hi, xr_hi[12]).astype(F32), -72),
        rolled(kept(has_hi2, xr_hi2[...]).astype(F32), 0),
    ]
    two = row[0]
    for i in range(1, 5):
        two = jnp.where(lane < 20 * i, two, rolled(row[i], 20 * i))
    two_out[...] = two.astype(BF16)
    coarse = [rolled(two, 72), rolled(two, 72 - 40), rolled(two, 72 - 80)]

    for out, fine_y, half_y in ((lo_out, 0, 0), (hi_out, 7, 2)):
        out[0] = kept(has_lo, xr_lo[fine_y])
        out[9] = kept(has_hi, xr_hi[fine_y])
        for x in range(8):
            out[1 + x] = x_ref[x, fine_y]
        for i in range(8):
            for k in range(2):
                y = half_y + k
                if i < 2:
                    value = kept(has_lo, xr_lo[8 + 4 * i + y])
                elif i < 6:
                    value = t1[i - 2, y]
                else:
                    value = kept(has_hi, xr_hi[8 + 4 * (i - 6) + y])
                if i < 2:
                    extra = kept(has_lo, xr_lo[8 + 2 * i + k]).astype(F32)
                elif i < 4:
                    extra = rolled(t2[i - 2, k].astype(F32), 72)
                elif i < 6:
                    extra = kept(has_hi, xr_hi[8 + 2 * (i - 4) + k]).astype(F32)
                else:
                    spot = 2 * (i - 6) + k
                    extra = coarse[spot] if spot < 3 else None
                if extra is not None:
                    value = jnp.where(free, extra, value.astype(F32)).astype(BF16)
                out[10 + 2 * i + k] = value


def taps(ref, x, ys):
    return jnp.concatenate(
        [
            jnp.concatenate([ref[x + d, y : y + 3].reshape(288, LANES) for y in ys], axis=1)
            for d in range(3)
        ],
        axis=0,
    )


def weighted(weight, value):
    return lax.dot_general(weight, value, (((0,), (0,)), ((), ())), preferred_element_type=F32)


def spread(ref, i, j, value, base=0, lo=None, hi=None):
    lane = lanes()
    wide = value.astype(F32)
    before, after = rolled(wide, base + 1), rolled(wide, base - 1)
    if lo is not None:
        before = jnp.where(lane == 0, lo, before)
        after = jnp.where(lane == LANES - 1, hi, after)
    ref[i, j, 0:32] = before.astype(BF16)
    ref[i, j, 32:64] = rolled(wide, base).astype(BF16) if base else value
    ref[i, j, 64:96] = after.astype(BF16)


def fine_kernel(flags, x_ref, t1, xr_lo, xr_hi, w0, mix, acc_out, e0):
    zero = jnp.zeros((96, LANES), BF16)
    for i in range(10):
        e0[i, 0] = zero
        e0[i, 9] = zero
    for k in range(8):
        s = k % 2
        column = kept(flags[0], xr_lo[8 + 4 + k // 2]).astype(F32)
        spread(e0, 0, 1 + k, kept(flags[0], xr_lo[k]), 0, rolled(column, 2 - s), rolled(column, 57 - s))
        column = kept(flags[1], xr_hi[8 + k // 2]).astype(F32)
        spread(e0, 9, 1 + k, kept(flags[1], xr_hi[k]), 0, rolled(column, 4 - s), rolled(column, 59 - s))

    def fill(c, carry):
        for part in range(2):
            for k in range(8):
                s = 2 * part + k % 2
                column = t1[c, k // 2].astype(F32)
                spread(
                    e0, 2 * c + part + 1, 1 + k, x_ref[2 * c + part, k], 0,
                    rolled(column, 4 - s), rolled(column, 59 - s),
                )
        return carry

    lax.fori_loop(0, 4, fill, 0)
    weight = jnp.concatenate([w0[...], mix[...]], axis=0)

    def fine(x, carry):
        for y in range(0, 8, 2):
            middle = jnp.concatenate([x_ref[x, y], x_ref[x, y + 1]], axis=1)
            value = weighted(weight, jnp.concatenate([taps(e0, x, [y, y + 1]), middle], axis=0))
            acc_out[x, y] = value[:, :LANES]
            acc_out[x, y + 1] = value[:, LANES:]
        return carry

    lax.fori_loop(0, 8, fine, 0)


def final_kernel(
    flags, acc, t1, t2, t3, xr_lo, xr_hi, xr_lo2, xr_hi2, yr_lo, yr_hi, yr_two,
    w0, w1, w2, w3, up, up0, out_ref, ey, edge, e1, e2, e3, v3, v2, v1, q1, rows,
):
    x_lo, x_hi, y_lo, y_hi, z_lo, z_hi, x_lo2, x_hi2, y_lo2, y_hi2 = (flags[i] for i in range(10))
    lane = lanes()

    for i in range(5):
        spread(e3, i, 0, kept(y_lo2, yr_two[...]), -20 * i)
        spread(e3, i, 1, kept(y_lo, yr_lo[22 + i // 2]), -72 - 20 * (i % 2))
        spread(e3, i, 3, kept(y_hi, yr_hi[22 + i // 2]), -72 - 20 * (i % 2))
        spread(e3, i, 4, kept(y_hi2, yr_two[...]), -20 * i)
    spread(e3, 0, 2, kept(x_lo2, xr_lo2[...]))
    spread(e3, 1, 2, kept(x_lo, xr_lo[12]), -72)
    spread(e3, 2, 2, t3[...])
    spread(e3, 3, 2, kept(x_hi, xr_hi[12]), -72)
    spread(e3, 4, 2, kept(x_hi2, xr_hi2[...]))
    for i in range(6):
        for k in range(2):
            spread(e2, i, k, kept(y_lo, yr_lo[10 + 2 * i + k]), -72)
            spread(e2, i, 4 + k, kept(y_hi, yr_hi[10 + 2 * i + k]), -72)
    for i in range(2):
        for k in range(2):
            spread(e2, i, 2 + k, kept(x_lo, xr_lo[8 + 2 * i + k]), -72)
            spread(e2, 2 + i, 2 + k, t2[i, k])
            spread(e2, 4 + i, 2 + k, kept(x_hi, xr_hi[8 + 2 * i + k]), -72)
    for i in range(8):
        for k in range(2):
            spread(e1, i, k, kept(y_lo, yr_lo[10 + 2 * i + k]))
            spread(e1, i, 6 + k, kept(y_hi, yr_hi[10 + 2 * i + k]))
    for k in range(4):
        for i in range(2):
            spread(e1, i, 2 + k, kept(x_lo, xr_lo[8 + 4 * i + k]))
            spread(e1, 6 + i, 2 + k, kept(x_hi, xr_hi[8 + 4 * i + k]))
        for i in range(4):
            spread(e1, 2 + i, 2 + k, t1[i, k])
    for i in range(10):
        sx = (i + 1) % 2
        coarse = (i + 1) // 2 + 1
        for side, ref, flag, row, s in ((0, yr_lo, y_lo, 1, 2 * sx + 1), (1, yr_hi, y_hi, 0, 2 * sx)):
            column = kept(flag, ref[10 + 2 * coarse + row]).astype(F32)
            spread(ey, side, i, kept(flag, ref[i]), 0, rolled(column, 4 - s), rolled(column, 59 - s))
    for side, dy in ((0, 0), (1, 2)):
        weight = jnp.concatenate([w0[96 * (3 * dx + dy) : 96 * (3 * dx + dy) + 96] for dx in range(3)], axis=0)
        for x in range(0, 8, 2):
            value = jnp.concatenate(
                [ey[side, x : x + 3].reshape(288, LANES), ey[side, x + 1 : x + 4].reshape(288, LANES)], axis=1
            )
            value = weighted(weight, value)
            edge[side, x] = value[:, :LANES]
            edge[side, x + 1] = value[:, LANES:]

    def along(before, centre, after):
        return [0.75 * centre + 0.25 * before, 0.75 * centre + 0.25 * after]

    def limits(count):
        inside = (lane >= 1) & (lane <= count + 2)
        inside &= (lane != 1) | (z_lo > 0)
        return inside & ((lane != count + 2) | (z_hi > 0))

    def cell_flag(position, last, lo, hi):
        return lo if position == 0 else hi if position == last else None

    def prolonged(ref, count):
        wide = dot(ref[...].reshape(count * count * 32, LANES), up[...]).reshape(count, count, 32, LANES)

        def refined(cells):
            out = []
            for k in range(2 * count - 2):
                cell = k - 1
                centre = cell // 2 + 1
                other = centre - 1 if cell % 2 == 0 else centre + 1
                out.append(0.75 * cells[centre] + 0.25 * cells[other])
            return out

        by_x = refined([wide[i] for i in range(count)])
        return [refined([row[j] for j in range(count)]) for row in by_x]

    def level(e_ref, w_ref, v_ref, size, cells, above):
        keep = limits(cells)
        for i in range(size):
            for j in range(0, size, 2):
                ys = [j, j + 1] if j + 1 < size else [j]
                value = weighted(w_ref[...], taps(e_ref, i, ys))
                for n, y in enumerate(ys):
                    part = value[:, LANES * n : LANES * (n + 1)]
                    if above is not None:
                        part = part + above[i][y]
                    good = keep
                    for flag in (cell_flag(i, size - 1, x_lo, x_hi), cell_flag(y, size - 1, y_lo, y_hi)):
                        if flag is not None:
                            good = good & (flag > 0)
                    v_ref[i, y] = jnp.where(good, part, 0.0).astype(BF16)

    level(e3, w3, v3, 3, 16, None)
    level(e2, w2, v2, 4, 32, prolonged(v3, 3))
    level(e1, w1, v1, 6, 64, prolonged(v2, 4))
    for i in range(6):
        q1[i] = dot(v1[i].reshape(6 * 32, LANES), up0[...]).reshape(6, 32, LANES)

    def fine(c, carry):
        for part in range(2):
            x = 2 * c + part
            row = 0.75 * q1[c + 1] + 0.25 * q1[c + 2 * part]
            for y in range(0, 8, 2):
                centre = y // 2 + 1
                for n, extra in enumerate(along(row[centre - 1], row[centre], row[centre + 1])):
                    total = acc[x, y + n] + extra
                    if y + n == 0:
                        total = total + edge[0, x]
                    if y + n == 7:
                        total = total + edge[1, x]
                    rows[pl.ds(x * 8 + y + n, 32, stride=64), :] = jax.nn.gelu(total, approximate=True)
        return carry

    lax.fori_loop(0, 4, fine, 0)
    out_ref[...] = rows[...].reshape(32, 8, 8, LANES).astype(BF16)


def turned(value, axis, step):
    count = lax.axis_size(axis)
    return lax.ppermute(value, axis, [(i, (i + step) % count) for i in range(count)])


def on_device(field, mixing, kernel_fine, kernel_half, kernel_quarter, kernel_eighth):
    gx, gy, gz = (lax.axis_index(a) for a in ("gx", "gy", "gz"))
    nx, ny, nz = (lax.axis_size(a) for a in ("gx", "gy", "gz"))
    slot = lax.iota(jnp.int32, 16)
    place = jnp.where((slot < 2) | (slot == 6) | (slot == 7), gx, jnp.where((slot == 4) | (slot == 5), gz, gy))
    first = np.array([1, 0, 1, 0, 1, 0, 2, 0, 2, 0] + [0] * 6, np.int32)
    last = np.array([nx, nx - 1, ny, ny - 1, nz, nz - 1, nx, nx - 2, ny, ny - 2] + [99] * 6, np.int32)
    flags = ((place >= first) & (place < last)).astype(jnp.int32)
    table, up, up0 = (jnp.asarray(m) for m in tables())
    tile = (32, LANES)

    x_own, t1, t2, t3, msg = call(
        restrict_kernel,
        [(8, 8) + tile, (4, 4) + tile, (2, 2) + tile, tile, (2,) + tile],
        [field, table],
        [
            pltpu.VMEM((32, 8, 8, LANES), BF16),
            pltpu.VMEM((512, 640), BF16),
            pltpu.VMEM((2048, LANES), F32),
            pltpu.SemaphoreType.DMA((2,)),
        ],
        0,
        pltpu.HBM,
    )
    from_hi = turned(msg[0], "gz", -1)
    from_lo = turned(msg[1], "gz", 1)
    t1, t2, t3, x_msg_lo, x_msg_hi = call(
        depth_kernel,
        [(4, 4) + tile, (2, 2) + tile, tile, (16,) + tile, (16,) + tile],
        [flags, x_own, t1, t2, t3, from_lo, from_hi],
    )
    xr_hi = turned(x_msg_lo, "gx", -1)
    xr_lo = turned(x_msg_hi, "gx", 1)
    xr_hi2 = turned(t3, "gx", -2)
    xr_lo2 = turned(t3, "gx", 2)
    y_msg_lo, y_msg_hi, two = call(
        width_kernel,
        [(26,) + tile, (26,) + tile, tile],
        [flags, x_own, t1, t2, t3, xr_lo, xr_hi, xr_lo2, xr_hi2],
    )
    yr_hi = turned(y_msg_lo, "gy", -1)
    yr_lo = turned(y_msg_hi, "gy", 1)
    assert ny == 4
    yr_two = turned(two, "gy", 2)
    flat = [k.reshape(864, 32) for k in (kernel_fine, kernel_half, kernel_quarter, kernel_eighth)]
    (acc,) = call(
        fine_kernel,
        [(8, 8) + tile],
        [flags, x_own, t1, xr_lo, xr_hi, flat[0], mixing.T],
        [pltpu.VMEM((10, 10, 96, LANES), BF16)],
        kind=F32,
        flops=1 << 30,
    )
    (out,) = call(
        final_kernel,
        [(32, 8, 8, LANES)],
        [flags, acc, t1, t2, t3, xr_lo, xr_hi, xr_lo2, xr_hi2, yr_lo, yr_hi, yr_two,
         *flat, up, up0],
        [
            pltpu.VMEM((2, 10, 96, LANES), BF16),
            pltpu.VMEM((2, 8) + tile, F32),
            pltpu.VMEM((8, 8, 96, LANES), BF16),
            pltpu.VMEM((6, 6, 96, LANES), BF16),
            pltpu.VMEM((5, 5, 96, LANES), BF16),
            pltpu.VMEM((3, 3) + tile, BF16),
            pltpu.VMEM((4, 4) + tile, BF16),
            pltpu.VMEM((6, 6) + tile, BF16),
            pltpu.VMEM((6, 6) + tile, F32),
            pltpu.VMEM((2048, LANES), F32),
        ],
    )
    return out


def solution(mesh):
    placed = (P(None, "gx", "gy", "gz"), P(), P(), P(), P(), P())
    return jax.shard_map(
        on_device, mesh=mesh, in_specs=placed, out_specs=P(None, "gx", "gy", "gz"), check_vma=False
    )
```

time: 47.3 us -> 39.9 us (0.84)
  the two profiles are of different devices: /device:TPU:8 before, /device:TPU:64 now
where the time goes in v2:
time: 39.9 us; the launch traced here: 39.8 us
  starting transfers between devices  16.1 us (40%)
  Pallas kernels  14.2 us (36%)
  waiting for transfers between devices  6.47 us (16%)
  local copies, waits for them, and re-layouts  2.92 us (7%)
    ppermute x9, starting transfers between devices, turned(): lax.ppermute(value, axis, [(i, (i + step) % count) for i in range(count)])  16.1 us
    pallas_call x5, Pallas kernels, call(): pl.pallas_call(kernel, out_shape=[jax.ShapeDtypeStruct(shape, kind) for s...  14.2 us
    ppermute x9, waiting for transfers between devices, turned(): lax.ppermute(value, axis, [(i, (i + step) % count) for i in range(count)])  6.47 us
    unnamed x23, local copies, waits for them, and re-layouts  2.92 us
  transfers between devices with their start and end apart: 9, of which 3 were waited for; matrix products, arithmetic and copies ran while one was open for 0% of the time, Pallas kernels for 13%

profile of v2, /device:TPU:64, one launch (start us, length us, event | category | flops | bytes accessed | tf_op | source)
XLA Modules:
  0.0 39.8 jit_solution(17486717439883920172)
XLA Ops:
  0.0 1.1 %copy-done = bf16[512,640]{1,0:T(8,128)(2,1)S(1)} copy-done((bf16[512,640]{1,0:T(8,128)(2,1)S(1)}, bf16[512,640]{1,0:T(8,128)(2,1)}, u32[]{:S(2)}) %copy-start) | copy-done | bytes 655384
  1.1 1.0 %copy-done.1 = bf16[32,8,8,128]{3,2,1,0:T(8,128)(2,1)S(1)} copy-done((bf16[32,8,8,128]{3,2,1,0:T(8,128)(2,1)S(1)}, bf16[32,8,8,128]{3,2,1,0:T(8,128)(2,1)}, u32[]{:S(2)}) %copy-start.1) | copy-done | bytes 524312
  2.1 1.5 %shard_map.109 = (bf16[8,8,32,128]{3,2,1,0:T(8,128)(2,1)S(1)}, bf16[4,4,32,128]{3,2,1,0:T(8,128)(2,1)S(1)}, bf16[2,2,32,128]{3,2,1,0:T(8,128)(2,1)S(1)}, bf16[32...) custom-call(bf16[32,8,8,128]{3,2,1,0:T(8,128)(2,1)S(1)} %copy-done.1, bf16[512,640]{1,0:T(8,128)(2,1)S(1)} %copy-done), custom_call_target="tpu_custom_call" | custom-call | flops 1048576 | bytes 1048576 | tf_op jit(solution)/shard_map/pallas_call | solution.py:64
  3.6 0.0 collective-permute-start
  3.7 2.9 %collective-permute-start.1 = (bf16[32,128]{1,0:T(8,128)(2,1)S(1)}, bf16[32,128]{1,0:T(8,128)(2,1)S(1)}, u32[]{:S(2)}, u32[]{:S(2)}) collective-permute-start(bf16[32,128]{1,0:T(8,128)(2,1)S(1)} %get-tuple-element.31), channel_id=1, source_target_pairs={{0,7},{1,0},{2,1},{3,2},{4,3},{5,4},{6,5},{7,6},{8,15},{9,8},{10,9... | collective-permute-start | bytes 24584 | tf_op jit(solution)/shard_map/ppermute | solution.py:387
  6.6 0.7 %copy-done.9 = s32[16]{0:T(128)S(1)} copy-done((s32[16]{0:T(128)S(1)}, s32[16]{0:T(128)}, u32[]{:S(2)}) %copy-start.9) | copy-done | bytes 88
  7.3 0.0 copy-done.10
  7.3 0.7 %collective-permute-done.from_lo = bf16[32,128]{1,0:T(8,128)(2,1)S(1)} collective-permute-done((bf16[32,128]{1,0:T(8,128)(2,1)S(1)}, bf16[32,128]{1,0:T(8,128)(2,1)S(1)}, u32[]{:S(2)}, u32[]{:S(2)}) %collective-permute-start) | collective-permute-done | bytes 8224 | tf_op jit(solution)/shard_map/ppermute | solution.py:387
  7.9 0.0 collective-permute-done.1.from_hi
  8.0 0.7 %shard_map.110 = (bf16[4,4,32,128]{3,2,1,0:T(8,128)(2,1)S(1)}, bf16[2,2,32,128]{3,2,1,0:T(8,128)(2,1)S(1)}, bf16[32,128]{1,0:T(8,128)(2,1)S(1)}, bf16[16,32,128]...) custom-call(s32[16]{0:T(128)S(1)} %and_convert_fusion.flags, bf16[8,8,32,128]{3,2,1,0:T(8,128)(2,1)S(1)} %get-tuple-element.18.x_ref, ...), custom_call_target="tpu_custom_call" | custom-call | flops 1048576 | bytes 1048576 | tf_op jit(solution)/shard_map/pallas_call | solution.py:64
  8.7 2.0 %collective-permute-start.2 = (bf16[16,32,128]{2,1,0:T(8,128)(2,1)S(1)}, bf16[16,32,128]{2,1,0:T(8,128)(2,1)S(1)}, u32[]{:S(2)}, u32[]{:S(2)}) collective-permute-start(bf16[16,32,128]{2,1,0:T(8,128)(2,1)S(1)} %get-tuple-element.24), channel_id=1, source_target_pairs={{0,32},{32,64},{64,96},{96,128},{128,160},{160,192},{192,224},{224... | collective-permute-start | bytes 393224 | tf_op jit(solution)/shard_map/ppermute | solution.py:387
  10.7 0.1 collective-permute-start.3
  10.8 5.7 %collective-permute-start.4 = (bf16[32,128]{1,0:T(8,128)(2,1)S(1)}, bf16[32,128]{1,0:T(8,128)(2,1)S(1)}, u32[]{:S(2)}, u32[]{:S(2)}) collective-permute-start(bf16[32,128]{1,0:T(8,128)(2,1)S(1)} %get-tuple-element.27.t3), channel_id=1, source_target_pairs={{0,64},{32,96},{64,128},{96,160},{128,192},{160,224},{192,0},{224,... | collective-permute-start | bytes 24584 | tf_op jit(solution)/shard_map/ppermute | solution.py:387
  16.5 0.0 collective-permute-start.5
  16.5 1.4 %collective-permute-done.4.xr_lo2 = bf16[32,128]{1,0:T(8,128)(2,1)S(1)} collective-permute-done((bf16[32,128]{1,0:T(8,128)(2,1)S(1)}, bf16[32,128]{1,0:T(8,128)(2,1)S(1)}, u32[]{:S(2)}, u32[]{:S(2)}) %collective-permute-start.4) | collective-permute-done | bytes 8224 | tf_op jit(solution)/shard_map/ppermute | solution.py:387
  17.9 4.4 %collective-permute-done.5.xr_hi2 = bf16[32,128]{1,0:T(8,128)(2,1)S(1)} collective-permute-done((bf16[32,128]{1,0:T(8,128)(2,1)S(1)}, bf16[32,128]{1,0:T(8,128)(2,1)S(1)}, u32[]{:S(2)}, u32[]{:S(2)}) %collective-permute-start.5) | collective-permute-done | bytes 8224 | tf_op jit(solution)/shard_map/ppermute | solution.py:387
  22.3 0.0 collective-permute-done.2.xr_lo
  22.3 0.0 collective-permute-done.3.xr_hi
  22.3 0.0 copy-start.2
  22.3 0.8 %shard_map.112 = (bf16[26,32,128]{2,1,0:T(8,128)(2,1)S(1)}, bf16[26,32,128]{2,1,0:T(8,128)(2,1)S(1)}, bf16[32,128]{1,0:T(8,128)(2,1)S(1)}) custom-call(s32[16]{0:T(128)S(1)} %and_convert_fusion.flags, bf16[8,8,32,128]{3,2,1,0:T(8,128)(2,1)S(1)} %get-tuple-element.18.x_ref, bf16[4,4,32,128]{3,2,1,0:T(8,128)(2,1)S(1)} %get-tuple-element.23.t1, ...), custom_call_target="tpu_custom_call" | custom-call | flops 1048576 | bytes 1048576 | tf_op jit(solution)/shard_map/pallas_call | solution.py:64
  23.1 1.7 %collective-permute-start.6 = (bf16[26,32,128]{2,1,0:T(8,128)(2,1)S(1)}, bf16[26,32,128]{2,1,0:T(8,128)(2,1)S(1)}, u32[]{:S(2)}, u32[]{:S(2)}) collective-permute-start(bf16[26,32,128]{2,1,0:T(8,128)(2,1)S(1)} %get-tuple-element.28), channel_id=1, source_target_pairs={{0,8},{8,16},{16,24},{24,0},{1,9},{9,17},{17,25},{25,1},{2,10},{10... | collective-permute-start | bytes 638984 | tf_op jit(solution)/shard_map/ppermute | solution.py:387
  24.7 1.7 %collective-permute-start.7 = (bf16[26,32,128]{2,1,0:T(8,128)(2,1)S(1)}, bf16[26,32,128]{2,1,0:T(8,128)(2,1)S(1)}, u32[]{:S(2)}, u32[]{:S(2)}) collective-permute-start(bf16[26,32,128]{2,1,0:T(8,128)(2,1)S(1)} %get-tuple-element.29), channel_id=1, source_target_pairs={{0,24},{8,0},{16,8},{24,16},{1,25},{9,1},{17,9},{25,17},{2,26},{10... | collective-permute-start | bytes 638984 | tf_op jit(solution)/shard_map/ppermute | solution.py:387
  26.4 0.0 copy-done.8
  26.4 0.1 copy.12
  26.5 2.0 %collective-permute-start.8 = (bf16[32,128]{1,0:T(8,128)(2,1)S(1)}, bf16[32,128]{1,0:T(8,128)(2,1)S(1)}, u32[]{:S(2)}, u32[]{:S(2)}) collective-permute-start(bf16[32,128]{1,0:T(8,128)(2,1)S(1)} %get-tuple-element.30), channel_id=1, source_target_pairs={{0,16},{8,24},{16,0},{24,8},{1,17},{9,25},{17,1},{25,9},{2,18},{10... | collective-permute-start | bytes 24584 | tf_op jit(solution)/shard_map/ppermute | solution.py:387
  28.5 0.0 copy-start.6
  28.5 0.0 copy-start.7
  28.5 5.2 %shard_map.111.acc = f32[8,8,32,128]{3,2,1,0:T(8,128)S(1)} custom-call(s32[16]{0:T(128)S(1)} %and_convert_fusion.flags, bf16[8,8,32,128]{3,2,1,0:T(8,128)(2,1)S(1)} %get-tuple-element.18.x_ref, bf16[4,4,32,128]{3,2,1,0:T(8,128)(2,1)S(1)} %get-tuple-element.23.t1, bf16[16,32,128]{2,1,0:T(8,128)(2,1)S(1)} %collective-permute-done.2.xr_lo, ...), custom_call_target="tpu_custom_call" | custom-call | flops 1073741824 | bytes 1048576 | tf_op jit(solution)/shard_map/pallas_call | solution.py:64
  33.7 0.0 collective-permute-done.8.yr_two
  33.8 0.0 collective-permute-done.6.yr_lo
  33.8 0.0 collective-permute-done.7.yr_hi
  33.8 5.9 %shard_map.113 = bf16[32,8,8,128]{3,2,1,0:T(8,128)(2,1)} custom-call(s32[16]{0:T(128)S(1)} %and_convert_fusion.flags, f32[8,8,32,128]{3,2,1,0:T(8,128)S(1)} %shard_map.111.acc, bf16[4,4,32,128]{3,2,1,0:T(8,128)(2,1)S(1)} %get-tuple-element.23.t1, bf16[2,2,32,128]{3,2,1,0:T(8,128)(2,1)S(1)} %get-tuple-element.26.t2, ...), custom_call_target="tpu_custom_call" | custom-call | flops 1048576 | bytes 1048576 | tf_op jit(solution)/shard_map/pallas_call | solution.py:64
  (16 shorter events, 0.0 us)
Async XLA Ops:
  0.0 1.1 %copy-start = (bf16[512,640]{1,0:T(8,128)(2,1)S(1)}, bf16[512,640]{1,0:T(8,128)(2,1)}, u32[]{:S(2)}) copy-start(bf16[512,640]{1,0:T(8,128)(2,1)} %constant.34.clone.table_hbm) | copy-start | bytes 1966084
  1.1 1.0 %copy-start.1 = (bf16[32,8,8,128]{3,2,1,0:T(8,128)(2,1)S(1)}, bf16[32,8,8,128]{3,2,1,0:T(8,128)(2,1)}, u32[]{:S(2)}) copy-start(bf16[32,8,8,128]{3,2,1,0:T(8,128)(2,1)} %field_hbm.1) | copy-start | bytes 1572868
  3.6 4.3 %collective-permute-start = (bf16[32,128]{1,0:T(8,128)(2,1)S(1)}, bf16[32,128]{1,0:T(8,128)(2,1)S(1)}, u32[]{:S(2)}, u32[]{:S(2)}) collective-permute-start(bf16[32,128]{1,0:T(8,128)(2,1)S(1)} %get-tuple-element.32), channel_id=1, source_target_pairs={{0,1},{1,2},{2,3},{3,4},{4,5},{5,6},{6,7},{7,0},{8,9},{9,10},{10,1... | collective-permute-start | bytes 24584 | tf_op jit(solution)/shard_map/ppermute | solution.py:387
  3.7 4.3 %collective-permute-start.1 = (bf16[32,128]{1,0:T(8,128)(2,1)S(1)}, bf16[32,128]{1,0:T(8,128)(2,1)S(1)}, u32[]{:S(2)}, u32[]{:S(2)}) collective-permute-start(bf16[32,128]{1,0:T(8,128)(2,1)S(1)} %get-tuple-element.31), channel_id=1, source_target_pairs={{0,7},{1,0},{2,1},{3,2},{4,3},{5,4},{6,5},{7,6},{8,15},{9,8},{10,9... | collective-permute-start | bytes 24584 | tf_op jit(solution)/shard_map/ppermute | solution.py:387
  6.6 0.7 %copy-start.9 = (s32[16]{0:T(128)S(1)}, s32[16]{0:T(128)}, u32[]{:S(2)}) copy-start(s32[16]{0:T(128)} %constant.33.clone) | copy-start | bytes 196
  6.6 0.7 %copy-start.10 = (s32[16]{0:T(128)S(1)}, s32[16]{0:T(128)}, u32[]{:S(2)}) copy-start(s32[16]{0:T(128)} %constant.32.clone) | copy-start | bytes 196
  8.7 13.6 %collective-permute-start.2 = (bf16[16,32,128]{2,1,0:T(8,128)(2,1)S(1)}, bf16[16,32,128]{2,1,0:T(8,128)(2,1)S(1)}, u32[]{:S(2)}, u32[]{:S(2)}) collective-permute-start(bf16[16,32,128]{2,1,0:T(8,128)(2,1)S(1)} %get-tuple-element.24), channel_id=1, source_target_pairs={{0,32},{32,64},{64,96},{96,128},{128,160},{160,192},{192,224},{224... | collective-permute-start | bytes 393224 | tf_op jit(solution)/shard_map/ppermute | solution.py:387
  10.7 11.6 %collective-permute-start.3 = (bf16[16,32,128]{2,1,0:T(8,128)(2,1)S(1)}, bf16[16,32,128]{2,1,0:T(8,128)(2,1)S(1)}, u32[]{:S(2)}, u32[]{:S(2)}) collective-permute-start(bf16[16,32,128]{2,1,0:T(8,128)(2,1)S(1)} %get-tuple-element.25), channel_id=1, source_target_pairs={{0,224},{32,0},{64,32},{96,64},{128,96},{160,128},{192,160},{224,1... | collective-permute-start | bytes 393224 | tf_op jit(solution)/shard_map/ppermute | solution.py:387
  10.8 7.1 %collective-permute-start.4 = (bf16[32,128]{1,0:T(8,128)(2,1)S(1)}, bf16[32,128]{1,0:T(8,128)(2,1)S(1)}, u32[]{:S(2)}, u32[]{:S(2)}) collective-permute-start(bf16[32,128]{1,0:T(8,128)(2,1)S(1)} %get-tuple-element.27.t3), channel_id=1, source_target_pairs={{0,64},{32,96},{64,128},{96,160},{128,192},{160,224},{192,0},{224,... | collective-permute-start | bytes 24584 | tf_op jit(solution)/shard_map/ppermute | solution.py:387
  16.5 5.8 %collective-permute-start.5 = (bf16[32,128]{1,0:T(8,128)(2,1)S(1)}, bf16[32,128]{1,0:T(8,128)(2,1)S(1)}, u32[]{:S(2)}, u32[]{:S(2)}) collective-permute-start(bf16[32,128]{1,0:T(8,128)(2,1)S(1)} %get-tuple-element.27.t3), channel_id=1, source_target_pairs={{0,192},{32,224},{64,0},{96,32},{128,64},{160,96},{192,128},{224,1... | collective-permute-start | bytes 24584 | tf_op jit(solution)/shard_map/ppermute | solution.py:387
  22.3 4.1 %copy-start.8 = (bf16[32,32]{1,0:T(8,128)(2,1)S(1)}, bf16[32,32]{1,0:T(8,128)(2,1)}, u32[]{:S(2)}) copy-start(bf16[32,32]{1,0:T(8,128)(2,1)} %param.12) | copy-start | bytes 6148
  22.3 6.2 %copy-start.2 = (bf16[3,3,3,32,32]{4,3,2,1,0:T(8,128)(2,1)S(1)}, bf16[3,3,3,32,32]{4,3,2,1,0:T(8,128)(2,1)}, u32[]{:S(2)}) copy-start(bf16[3,3,3,32,32]{4,3,2,1,0:T(8,128)(2,1)} %param.13) | copy-start | bytes 165892
  23.1 10.7 %collective-permute-start.6 = (bf16[26,32,128]{2,1,0:T(8,128)(2,1)S(1)}, bf16[26,32,128]{2,1,0:T(8,128)(2,1)S(1)}, u32[]{:S(2)}, u32[]{:S(2)}) collective-permute-start(bf16[26,32,128]{2,1,0:T(8,128)(2,1)S(1)} %get-tuple-element.28), channel_id=1, source_target_pairs={{0,8},{8,16},{16,24},{24,0},{1,9},{9,17},{17,25},{25,1},{2,10},{10... | collective-permute-start | bytes 638984 | tf_op jit(solution)/shard_map/ppermute | solution.py:387
  24.7 9.0 %collective-permute-start.7 = (bf16[26,32,128]{2,1,0:T(8,128)(2,1)S(1)}, bf16[26,32,128]{2,1,0:T(8,128)(2,1)S(1)}, u32[]{:S(2)}, u32[]{:S(2)}) collective-permute-start(bf16[26,32,128]{2,1,0:T(8,128)(2,1)S(1)} %get-tuple-element.29), channel_id=1, source_target_pairs={{0,24},{8,0},{16,8},{24,16},{1,25},{9,1},{17,9},{25,17},{2,26},{10... | collective-permute-start | bytes 638984 | tf_op jit(solution)/shard_map/ppermute | solution.py:387
  26.5 7.3 %collective-permute-start.8 = (bf16[32,128]{1,0:T(8,128)(2,1)S(1)}, bf16[32,128]{1,0:T(8,128)(2,1)S(1)}, u32[]{:S(2)}, u32[]{:S(2)}) collective-permute-start(bf16[32,128]{1,0:T(8,128)(2,1)S(1)} %get-tuple-element.30), channel_id=1, source_target_pairs={{0,16},{8,24},{16,0},{24,8},{1,17},{9,25},{17,1},{25,9},{2,18},{10... | collective-permute-start | bytes 24584 | tf_op jit(solution)/shard_map/ppermute | solution.py:387
  28.5 5.3 %copy-start.3 = (bf16[3,3,3,32,32]{4,3,2,1,0:T(8,128)(2,1)S(1)}, bf16[3,3,3,32,32]{4,3,2,1,0:T(8,128)(2,1)}, u32[]{:S(2)}) copy-start(bf16[3,3,3,32,32]{4,3,2,1,0:T(8,128)(2,1)} %param.14) | copy-start | bytes 165892
  28.5 5.3 %copy-start.4 = (bf16[3,3,3,32,32]{4,3,2,1,0:T(8,128)(2,1)S(1)}, bf16[3,3,3,32,32]{4,3,2,1,0:T(8,128)(2,1)}, u32[]{:S(2)}) copy-start(bf16[3,3,3,32,32]{4,3,2,1,0:T(8,128)(2,1)} %param.15) | copy-start | bytes 165892
  28.5 5.3 %copy-start.5 = (bf16[3,3,3,32,32]{4,3,2,1,0:T(8,128)(2,1)S(1)}, bf16[3,3,3,32,32]{4,3,2,1,0:T(8,128)(2,1)}, u32[]{:S(2)}) copy-start(bf16[3,3,3,32,32]{4,3,2,1,0:T(8,128)(2,1)} %param.16) | copy-start | bytes 165892
  28.5 5.3 %copy-start.6 = (bf16[128,128]{1,0:T(8,128)(2,1)S(1)}, bf16[128,128]{1,0:T(8,128)(2,1)}, u32[]{:S(2)}) copy-start(bf16[128,128]{1,0:T(8,128)(2,1)} %constant.35.clone.up) | copy-start | bytes 98308
  28.5 5.3 %copy-start.7 = (bf16[128,128]{1,0:T(8,128)(2,1)S(1)}, bf16[128,128]{1,0:T(8,128)(2,1)}, u32[]{:S(2)}) copy-start(bf16[128,128]{1,0:T(8,128)(2,1)} %constant.36.clone.up0) | copy-start | bytes 98308

commit v3 on v2

--- a/solution.py
+++ b/solution.py
@@ -12,34 +12,6 @@
 
 
 def tables():
-    r1 = np.zeros((512, 128), np.float32)
-    r2 = np.zeros((512, 128), np.float32)
-    r3 = np.zeros((512, 384), np.float32)
-    for s in range(4):
-        base = s * 128
-        for z in range(128):
-            r1[base + z, 2 + z // 2] = 0.125
-        r1[base, 72 + s] = 1.0
-        r1[base + 127, 76 + s] = 1.0
-        for z in range(64):
-            r2[base + 2 + z, 2 + z // 2] = 0.125
-        for k, lane in enumerate((2, 3, 72, 73, 74, 75)):
-            r2[base + lane, 40 + 6 * s + k] = 1.0
-        for k, lane in enumerate((76, 77, 78, 79, 64, 65)):
-            r2[base + lane, 64 + 6 * s + k] = 1.0
-        for z in range(32):
-            r3[base + 2 + z, 2 + z // 2] = 0.125
-        for sub in range(4):
-            tile = (2 * (s // 2) + sub // 2) * 4 + 2 * (s % 2) + sub % 2
-            for k in range(6):
-                r3[base + 40 + 6 * sub + k, 128 + 6 * tile + k] = 1.0
-                r3[base + 64 + 6 * sub + k, 256 + 6 * tile + k] = 1.0
-        for k in range(2):
-            r3[base + 2 + k, 128 + 96 + 2 * s + k] = 1.0
-            r3[base + 32 + k, 256 + 96 + 2 * s + k] = 1.0
-            for half in range(2):
-                r3[base + 2 + 2 * k + half, 128 + 104 + k] = 0.125
-                r3[base + 30 + 2 * k + half, 256 + 104 + k] = 0.125
     up = np.zeros((128, 128), np.float32)
     up0 = np.zeros((128, 128), np.float32)
     for out in range(128):
@@ -51,16 +23,58 @@
         centre = out // 2 + 2
         up0[centre, out] += 0.75
         up0[centre + step, out] += 0.25
-    return tuple(m.astype(BF16) for m in (np.concatenate([r1, r2, r3], axis=1), up, up0))
+    return tuple(m.astype(BF16) for m in (up, up0))
+
+
+def restrictions(table):
+    row = lax.broadcasted_iota(jnp.int32, (512, LANES), 0)
+    lane = lax.broadcasted_iota(jnp.int32, (1, LANES), 1)
+    spot = row & 127
+    base = row - spot
+    eighth = jnp.float32(0.125)
+
+    def put(k, *terms):
+        value = jnp.zeros((512, LANES), F32)
+        for mask, amount in terms:
+            value = jnp.where(mask, amount, value)
+        table[:, LANES * k : LANES * (k + 1)] = value.astype(BF16)
+
+    def at(target, valid):
+        return row == jnp.where(valid, target, -1)
+
+    put(
+        0,
+        ((spot >> 1) + 2 == lane, eighth),
+        (at((lane - 72) * 128, (lane >= 72) & (lane < 76)), 1.0),
+        (at((lane - 76) * 128 + 127, (lane >= 76) & (lane < 80)), 1.0),
+    )
+    halves = ((spot - 2) >> 1) + 2 == lane
+    sub = ((lane - 40) * 43) >> 8
+    k = lane - 40 - 6 * sub
+    low = at(sub * 128 + jnp.where(k < 2, 2 + k, 70 + k), (lane >= 40) & (lane < 64))
+    sub = ((lane - 64) * 43) >> 8
+    k = lane - 64 - 6 * sub
+    high = at(sub * 128 + jnp.where(k < 4, 76 + k, 60 + k), (lane >= 64) & (lane < 88))
+    put(1, (halves & (spot < 66) & (spot >= 2), eighth), (low, 1.0), (high, 1.0))
+    put(2, (halves & (spot < 34) & (spot >= 2), eighth))
+    tile = (lane * 43) >> 8
+    k = lane - 6 * tile
+    quad = (tile >> 3) * 2 + ((tile & 3) >> 1)
+    sub = ((tile >> 2) & 1) * 2 + (tile & 1)
+    last = (lane - 104) * 2
+    for n, start, own, own3 in ((3, 40, 2, 2), (4, 64, 32, 30)):
+        target = jnp.where(lane < 96, quad * 128 + start + 6 * sub + k, ((lane - 96) >> 1) * 128 + own + (lane & 1))
+        tail = ((spot - own3) & ~1) == jnp.where((lane >= 104) & (lane < 106), last, -1000)
+        put(n, (at(target, lane < 104), 1.0), (tail, eighth))
 
 
 def dot(a, b):
     return jnp.dot(a, b, preferred_element_type=F32)
 
 
-def call(kernel, outs, args, scratch=(), scalars=1, space=pltpu.VMEM, kind=BF16, flops=1 << 20):
+def call(kernel, outs, args, scratch=(), scalars=1, kind=BF16, flops=1 << 20):
     specs = [pl.BlockSpec(memory_space=pltpu.SMEM)] * scalars
-    specs += [pl.BlockSpec(memory_space=space)] * (len(args) - scalars)
+    specs += [pl.BlockSpec(memory_space=pltpu.VMEM)] * (len(args) - scalars)
     return pl.pallas_call(
         kernel,
         out_shape=[jax.ShapeDtypeStruct(shape, kind) for shape in outs],
@@ -73,19 +87,11 @@
     )(*args)
 
 
-def restrict_kernel(field_hbm, table_hbm, x_out, t1_out, t2_out, t3_out, msg_out, field, table, rows, sems):
-    copies = [
-        pltpu.make_async_copy(field_hbm, field, sems.at[0]),
-        pltpu.make_async_copy(table_hbm, table, sems.at[1]),
-    ]
-    for copy in copies:
-        copy.start()
-    copies[0].wait()
+def restrict_kernel(field, table, x_out, t1_out, t2_out, t3_out, msg_out, rows):
     rows[...] = field[...].astype(F32).reshape(2048, LANES)
     for x in range(8):
         for y in range(8):
             x_out[x, y] = rows[pl.ds(x * 8 + y, 32, stride=64), :].astype(BF16)
-    copies[1].wait()
 
     def four(ref, x, y):
         return jnp.concatenate(
@@ -392,24 +398,20 @@
     nx, ny, nz = (lax.axis_size(a) for a in ("gx", "gy", "gz"))
     slot = lax.iota(jnp.int32, 16)
     place = jnp.where((slot < 2) | (slot == 6) | (slot == 7), gx, jnp.where((slot == 4) | (slot == 5), gz, gy))
-    first = np.array([1, 0, 1, 0, 1, 0, 2, 0, 2, 0] + [0] * 6, np.int32)
-    last = np.array([nx, nx - 1, ny, ny - 1, nz, nz - 1, nx, nx - 2, ny, ny - 2] + [99] * 6, np.int32)
-    flags = ((place >= first) & (place < last)).astype(jnp.int32)
-    table, up, up0 = (jnp.asarray(m) for m in tables())
+    side = slot & 1
+    width = jnp.where(slot < 6, 1, 2)
+    count = jnp.where((slot < 2) | (slot == 6) | (slot == 7), nx, jnp.where((slot == 4) | (slot == 5), nz, ny))
+    flags = jnp.where(side == 0, place >= width, place < count - width).astype(jnp.int32)
+    up, up0 = (jnp.asarray(m) for m in tables())
     tile = (32, LANES)
 
+    (table,) = call(restrictions, [(512, 640)], [], scalars=0, flops=1 << 26)
     x_own, t1, t2, t3, msg = call(
         restrict_kernel,
         [(8, 8) + tile, (4, 4) + tile, (2, 2) + tile, tile, (2,) + tile],
         [field, table],
-        [
-            pltpu.VMEM((32, 8, 8, LANES), BF16),
-            pltpu.VMEM((512, 640), BF16),
-            pltpu.VMEM((2048, LANES), F32),
-            pltpu.SemaphoreType.DMA((2,)),
-        ],
+        [pltpu.VMEM((2048, LANES), F32)],
         0,
-        pltpu.HBM,
     )
     from_hi = turned(msg[0], "gz", -1)
     from_lo = turned(msg[1], "gz", 1)

time: 39.9 us -> 38.5 us (0.965)
  local copies, waits for them, and re-layouts: 2.92 us -> 0.82 us
  waiting for transfers between devices: 6.47 us -> 7.14 us
    unnamed x23 -> x17, local copies, waits for them, and re-layouts: 2.92 us -> 0.81 us
    ppermute x9, waiting for transfers between devices: 6.47 us -> 7.14 us  [turned(): lax.ppermute(value, axis, [(i, (i + step) % count) for i in range(count)])]
    pallas_call x5 -> x6, Pallas kernels: 14.2 us -> 14.3 us  [call(): pl.pallas_call(kernel, out_shape=[jax.ShapeDtypeStruct(shape, kind) for s...]
  transfers between devices with their start and end apart: 9 -> 9, of which waited for: 3 -> 3; matrix products, arithmetic and copies ran while one was open for 0% -> 0% of each run, Pallas kernels for 13% -> 14%
where the time goes in v3:
time: 38.5 us; the launch traced here: 38.4 us
  starting transfers between devices  16.1 us (42%)
  Pallas kernels  14.3 us (37%)
  waiting for transfers between devices  7.14 us (19%)
  local copies, waits for them, and re-layouts  0.82 us (2%)
    ppermute x9, starting transfers between devices, turned(): lax.ppermute(value, axis, [(i, (i + step) % count) for i in range(count)])  16.1 us
    pallas_call x6, Pallas kernels, call(): pl.pallas_call(kernel, out_shape=[jax.ShapeDtypeStruct(shape, kind) for s...  14.3 us
    ppermute x9, waiting for transfers between devices, turned(): lax.ppermute(value, axis, [(i, (i + step) % count) for i in range(count)])  7.14 us
    unnamed x17, local copies, waits for them, and re-layouts  0.81 us
  transfers between devices with their start and end apart: 9, of which 3 were waited for; matrix products, arithmetic and copies ran while one was open for 0% of the time, Pallas kernels for 14%

profile of v3, /device:TPU:64, one launch (start us, length us, event | category | flops | bytes accessed | tf_op | source)
XLA Modules:
  0.0 38.4 jit_solution(4113559962547293942)
XLA Ops:
  0.0 0.3 shard_map.82.table
  0.3 0.7 %copy-done = bf16[32,8,8,128]{3,2,1,0:T(8,128)(2,1)S(1)} copy-done((bf16[32,8,8,128]{3,2,1,0:T(8,128)(2,1)S(1)}, bf16[32,8,8,128]{3,2,1,0:T(8,128)(2,1)}, u32[]{:S(2)}) %copy-start) | copy-done | bytes 524312
  1.0 1.2 %shard_map.83 = (bf16[8,8,32,128]{3,2,1,0:T(8,128)(2,1)S(1)}, bf16[4,4,32,128]{3,2,1,0:T(8,128)(2,1)S(1)}, bf16[2,2,32,128]{3,2,1,0:T(8,128)(2,1)S(1)}, bf16[32,...) custom-call(bf16[32,8,8,128]{3,2,1,0:T(8,128)(2,1)S(1)} %copy-done, bf16[512,640]{1,0:T(8,128)(2,1)S(1)} %shard_map.82.table), custom_call_target="tpu_custom_call" | custom-call | flops 1048576 | bytes 1048576 | tf_op jit(solution)/shard_map/pallas_call | solution.py:78
  2.3 0.0 collective-permute-start
  2.3 2.9 %collective-permute-start.1 = (bf16[32,128]{1,0:T(8,128)(2,1)S(1)}, bf16[32,128]{1,0:T(8,128)(2,1)S(1)}, u32[]{:S(2)}, u32[]{:S(2)}) collective-permute-start(bf16[32,128]{1,0:T(8,128)(2,1)S(1)} %get-tuple-element.31), channel_id=1, source_target_pairs={{0,7},{1,0},{2,1},{3,2},{4,3},{5,4},{6,5},{7,6},{8,15},{9,8},{10,9... | collective-permute-start | bytes 24584 | tf_op jit(solution)/shard_map/ppermute | solution.py:393
  5.3 1.3 %collective-permute-done.from_lo = bf16[32,128]{1,0:T(8,128)(2,1)S(1)} collective-permute-done((bf16[32,128]{1,0:T(8,128)(2,1)S(1)}, bf16[32,128]{1,0:T(8,128)(2,1)S(1)}, u32[]{:S(2)}, u32[]{:S(2)}) %collective-permute-start) | collective-permute-done | bytes 8224 | tf_op jit(solution)/shard_map/ppermute | solution.py:393
  6.6 0.0 collective-permute-done.1.from_hi
  6.6 0.7 %shard_map.84 = (bf16[4,4,32,128]{3,2,1,0:T(8,128)(2,1)S(1)}, bf16[2,2,32,128]{3,2,1,0:T(8,128)(2,1)S(1)}, bf16[32,128]{1,0:T(8,128)(2,1)S(1)}, bf16[16,32,128]{2,1,0:T(8,128)(2,1)S(1)}, bf16[16,32,128]{2,1,0:T(8,128)(2,1)S(1)}) custom-call(s32[16]{0:T(128)S(1)} %select_convert_fusion.flags, bf16[8,8,32,128]{3,2,1,0:T(8,128)(2,1)S(1)} %get-tuple-element.18.x_ref, ...), custom_call_target="tpu_custom_call" | custom-call | flops 1048576 | bytes 1048576 | tf_op jit(solution)/shard_map/pallas_call | solution.py:78
  7.4 2.0 %collective-permute-start.2 = (bf16[16,32,128]{2,1,0:T(8,128)(2,1)S(1)}, bf16[16,32,128]{2,1,0:T(8,128)(2,1)S(1)}, u32[]{:S(2)}, u32[]{:S(2)}) collective-permute-start(bf16[16,32,128]{2,1,0:T(8,128)(2,1)S(1)} %get-tuple-element.24), channel_id=1, source_target_pairs={{0,32},{32,64},{64,96},{96,128},{128,160},{160,192},{192,224},{224... | collective-permute-start | bytes 393224 | tf_op jit(solution)/shard_map/ppermute | solution.py:393
  9.3 0.1 collective-permute-start.3
  9.5 5.7 %collective-permute-start.4 = (bf16[32,128]{1,0:T(8,128)(2,1)S(1)}, bf16[32,128]{1,0:T(8,128)(2,1)S(1)}, u32[]{:S(2)}, u32[]{:S(2)}) collective-permute-start(bf16[32,128]{1,0:T(8,128)(2,1)S(1)} %get-tuple-element.27.t3), channel_id=1, source_target_pairs={{0,64},{32,96},{64,128},{96,160},{128,192},{160,224},{192,0},{224,... | collective-permute-start | bytes 24584 | tf_op jit(solution)/shard_map/ppermute | solution.py:393
  15.1 0.0 collective-permute-start.5
  15.2 1.4 %collective-permute-done.4.xr_lo2 = bf16[32,128]{1,0:T(8,128)(2,1)S(1)} collective-permute-done((bf16[32,128]{1,0:T(8,128)(2,1)S(1)}, bf16[32,128]{1,0:T(8,128)(2,1)S(1)}, u32[]{:S(2)}, u32[]{:S(2)}) %collective-permute-start.4) | collective-permute-done | bytes 8224 | tf_op jit(solution)/shard_map/ppermute | solution.py:393
  16.5 4.4 %collective-permute-done.5.xr_hi2 = bf16[32,128]{1,0:T(8,128)(2,1)S(1)} collective-permute-done((bf16[32,128]{1,0:T(8,128)(2,1)S(1)}, bf16[32,128]{1,0:T(8,128)(2,1)S(1)}, u32[]{:S(2)}, u32[]{:S(2)}) %collective-permute-start.5) | collective-permute-done | bytes 8224 | tf_op jit(solution)/shard_map/ppermute | solution.py:393
  20.9 0.0 collective-permute-done.2.xr_lo
  20.9 0.0 collective-permute-done.3.xr_hi
  20.9 0.0 copy-start.1
  20.9 0.8 %shard_map.86 = (bf16[26,32,128]{2,1,0:T(8,128)(2,1)S(1)}, bf16[26,32,128]{2,1,0:T(8,128)(2,1)S(1)}, bf16[32,128]{1,0:T(8,128)(2,1)S(1)}) custom-call(s32[16]{0:T(128)S(1)} %select_convert_fusion.flags, bf16[8,8,32,128]{3,2,1,0:T(8,128)(2,1)S(1)} %get-tuple-element.18.x_ref, bf16[4,4,32,128]{3,2,1,0:T(8,128)(2,1)S(1)} %get-tuple-element.23.t1, ...), custom_call_target="tpu_custom_call" | custom-call | flops 1048576 | bytes 1048576 | tf_op jit(solution)/shard_map/pallas_call | solution.py:78
  21.7 1.7 %collective-permute-start.6 = (bf16[26,32,128]{2,1,0:T(8,128)(2,1)S(1)}, bf16[26,32,128]{2,1,0:T(8,128)(2,1)S(1)}, u32[]{:S(2)}, u32[]{:S(2)}) collective-permute-start(bf16[26,32,128]{2,1,0:T(8,128)(2,1)S(1)} %get-tuple-element.28), channel_id=1, source_target_pairs={{0,8},{8,16},{16,24},{24,0},{1,9},{9,17},{17,25},{25,1},{2,10},{10... | collective-permute-start | bytes 638984 | tf_op jit(solution)/shard_map/ppermute | solution.py:393
  23.4 1.7 %collective-permute-start.7 = (bf16[26,32,128]{2,1,0:T(8,128)(2,1)S(1)}, bf16[26,32,128]{2,1,0:T(8,128)(2,1)S(1)}, u32[]{:S(2)}, u32[]{:S(2)}) collective-permute-start(bf16[26,32,128]{2,1,0:T(8,128)(2,1)S(1)} %get-tuple-element.29), channel_id=1, source_target_pairs={{0,24},{8,0},{16,8},{24,16},{1,25},{9,1},{17,9},{25,17},{2,26},{10... | collective-permute-start | bytes 638984 | tf_op jit(solution)/shard_map/ppermute | solution.py:393
  25.1 0.0 copy-done.7
  25.1 0.1 copy.9
  25.1 2.0 %collective-permute-start.8 = (bf16[32,128]{1,0:T(8,128)(2,1)S(1)}, bf16[32,128]{1,0:T(8,128)(2,1)S(1)}, u32[]{:S(2)}, u32[]{:S(2)}) collective-permute-start(bf16[32,128]{1,0:T(8,128)(2,1)S(1)} %get-tuple-element.30), channel_id=1, source_target_pairs={{0,16},{8,24},{16,0},{24,8},{1,17},{9,25},{17,1},{25,9},{2,18},{10... | collective-permute-start | bytes 24584 | tf_op jit(solution)/shard_map/ppermute | solution.py:393
  27.1 0.0 copy-done.1
  27.2 0.0 copy-start.5
  27.2 0.0 copy-start.6
  27.2 5.2 %shard_map.85.acc = f32[8,8,32,128]{3,2,1,0:T(8,128)S(1)} custom-call(s32[16]{0:T(128)S(1)} %select_convert_fusion.flags, bf16[8,8,32,128]{3,2,1,0:T(8,128)(2,1)S(1)} %get-tuple-element.18.x_ref, bf16[4,4,32,128]{3,2,1,0:T(8,128)(2,1)S(1)} %get-tuple-element.23.t1, bf16[16,32,128]{2,1,0:T(8,128)(2,1)S(1)} %collective-permute-done.2.xr_lo, ...), custom_call_target="tpu_custom_call" | custom-call | flops 1073741824 | bytes 1048576 | tf_op jit(solution)/shard_map/pallas_call | solution.py:78
  32.4 0.0 collective-permute-done.8.yr_two
  32.4 0.0 collective-permute-done.6.yr_lo
  32.4 0.0 collective-permute-done.7.yr_hi
  32.4 0.0 copy-done.2
  32.5 5.9 %shard_map.87 = bf16[32,8,8,128]{3,2,1,0:T(8,128)(2,1)} custom-call(s32[16]{0:T(128)S(1)} %select_convert_fusion.flags, f32[8,8,32,128]{3,2,1,0:T(8,128)S(1)} %shard_map.85.acc, bf16[4,4,32,128]{3,2,1,0:T(8,128)(2,1)S(1)} %get-tuple-element.23.t1, bf16[2,2,32,128]{3,2,1,0:T(8,128)(2,1)S(1)} %get-tuple-element.26.t2, ...), custom_call_target="tpu_custom_call" | custom-call | flops 1048576 | bytes 1048576 | tf_op jit(solution)/shard_map/pallas_call | solution.py:78
  (11 shorter events, 0.0 us)
Async XLA Ops:
  0.0 1.0 %copy-start = (bf16[32,8,8,128]{3,2,1,0:T(8,128)(2,1)S(1)}, bf16[32,8,8,128]{3,2,1,0:T(8,128)(2,1)}, u32[]{:S(2)}) copy-start(bf16[32,8,8,128]{3,2,1,0:T(8,128)(2,1)} %field.1) | copy-start | bytes 1572868
  2.3 4.3 %collective-permute-start = (bf16[32,128]{1,0:T(8,128)(2,1)S(1)}, bf16[32,128]{1,0:T(8,128)(2,1)S(1)}, u32[]{:S(2)}, u32[]{:S(2)}) collective-permute-start(bf16[32,128]{1,0:T(8,128)(2,1)S(1)} %get-tuple-element.32), channel_id=1, source_target_pairs={{0,1},{1,2},{2,3},{3,4},{4,5},{5,6},{6,7},{7,0},{8,9},{9,10},{10,1... | collective-permute-start | bytes 24584 | tf_op jit(solution)/shard_map/ppermute | solution.py:393
  2.3 4.3 %collective-permute-start.1 = (bf16[32,128]{1,0:T(8,128)(2,1)S(1)}, bf16[32,128]{1,0:T(8,128)(2,1)S(1)}, u32[]{:S(2)}, u32[]{:S(2)}) collective-permute-start(bf16[32,128]{1,0:T(8,128)(2,1)S(1)} %get-tuple-element.31), channel_id=1, source_target_pairs={{0,7},{1,0},{2,1},{3,2},{4,3},{5,4},{6,5},{7,6},{8,15},{9,8},{10,9... | collective-permute-start | bytes 24584 | tf_op jit(solution)/shard_map/ppermute | solution.py:393
  7.4 13.6 %collective-permute-start.2 = (bf16[16,32,128]{2,1,0:T(8,128)(2,1)S(1)}, bf16[16,32,128]{2,1,0:T(8,128)(2,1)S(1)}, u32[]{:S(2)}, u32[]{:S(2)}) collective-permute-start(bf16[16,32,128]{2,1,0:T(8,128)(2,1)S(1)} %get-tuple-element.24), channel_id=1, source_target_pairs={{0,32},{32,64},{64,96},{96,128},{128,160},{160,192},{192,224},{224... | collective-permute-start | bytes 393224 | tf_op jit(solution)/shard_map/ppermute | solution.py:393
  9.3 11.6 %collective-permute-start.3 = (bf16[16,32,128]{2,1,0:T(8,128)(2,1)S(1)}, bf16[16,32,128]{2,1,0:T(8,128)(2,1)S(1)}, u32[]{:S(2)}, u32[]{:S(2)}) collective-permute-start(bf16[16,32,128]{2,1,0:T(8,128)(2,1)S(1)} %get-tuple-element.25), channel_id=1, source_target_pairs={{0,224},{32,0},{64,32},{96,64},{128,96},{160,128},{192,160},{224,1... | collective-permute-start | bytes 393224 | tf_op jit(solution)/shard_map/ppermute | solution.py:393
  9.5 7.1 %collective-permute-start.4 = (bf16[32,128]{1,0:T(8,128)(2,1)S(1)}, bf16[32,128]{1,0:T(8,128)(2,1)S(1)}, u32[]{:S(2)}, u32[]{:S(2)}) collective-permute-start(bf16[32,128]{1,0:T(8,128)(2,1)S(1)} %get-tuple-element.27.t3), channel_id=1, source_target_pairs={{0,64},{32,96},{64,128},{96,160},{128,192},{160,224},{192,0},{224,... | collective-permute-start | bytes 24584 | tf_op jit(solution)/shard_map/ppermute | solution.py:393
  15.1 5.8 %collective-permute-start.5 = (bf16[32,128]{1,0:T(8,128)(2,1)S(1)}, bf16[32,128]{1,0:T(8,128)(2,1)S(1)}, u32[]{:S(2)}, u32[]{:S(2)}) collective-permute-start(bf16[32,128]{1,0:T(8,128)(2,1)S(1)} %get-tuple-element.27.t3), channel_id=1, source_target_pairs={{0,192},{32,224},{64,0},{96,32},{128,64},{160,96},{192,128},{224,1... | collective-permute-start | bytes 24584 | tf_op jit(solution)/shard_map/ppermute | solution.py:393
  20.9 4.1 %copy-start.7 = (bf16[32,32]{1,0:T(8,128)(2,1)S(1)}, bf16[32,32]{1,0:T(8,128)(2,1)}, u32[]{:S(2)}) copy-start(bf16[32,32]{1,0:T(8,128)(2,1)} %param.9) | copy-start | bytes 6148
  20.9 6.2 %copy-start.1 = (bf16[3,3,3,32,32]{4,3,2,1,0:T(8,128)(2,1)S(1)}, bf16[3,3,3,32,32]{4,3,2,1,0:T(8,128)(2,1)}, u32[]{:S(2)}) copy-start(bf16[3,3,3,32,32]{4,3,2,1,0:T(8,128)(2,1)} %param.10) | copy-start | bytes 165892
  21.7 10.7 %collective-permute-start.6 = (bf16[26,32,128]{2,1,0:T(8,128)(2,1)S(1)}, bf16[26,32,128]{2,1,0:T(8,128)(2,1)S(1)}, u32[]{:S(2)}, u32[]{:S(2)}) collective-permute-start(bf16[26,32,128]{2,1,0:T(8,128)(2,1)S(1)} %get-tuple-element.28), channel_id=1, source_target_pairs={{0,8},{8,16},{16,24},{24,0},{1,9},{9,17},{17,25},{25,1},{2,10},{10... | collective-permute-start | bytes 638984 | tf_op jit(solution)/shard_map/ppermute | solution.py:393
  23.4 9.0 %collective-permute-start.7 = (bf16[26,32,128]{2,1,0:T(8,128)(2,1)S(1)}, bf16[26,32,128]{2,1,0:T(8,128)(2,1)S(1)}, u32[]{:S(2)}, u32[]{:S(2)}) collective-permute-start(bf16[26,32,128]{2,1,0:T(8,128)(2,1)S(1)} %get-tuple-element.29), channel_id=1, source_target_pairs={{0,24},{8,0},{16,8},{24,16},{1,25},{9,1},{17,9},{25,17},{2,26},{10... | collective-permute-start | bytes 638984 | tf_op jit(solution)/shard_map/ppermute | solution.py:393
  25.1 7.3 %collective-permute-start.8 = (bf16[32,128]{1,0:T(8,128)(2,1)S(1)}, bf16[32,128]{1,0:T(8,128)(2,1)S(1)}, u32[]{:S(2)}, u32[]{:S(2)}) collective-permute-start(bf16[32,128]{1,0:T(8,128)(2,1)S(1)} %get-tuple-element.30), channel_id=1, source_target_pairs={{0,16},{8,24},{16,0},{24,8},{1,17},{9,25},{17,1},{25,9},{2,18},{10... | collective-permute-start | bytes 24584 | tf_op jit(solution)/shard_map/ppermute | solution.py:393
  27.1 5.3 %copy-start.2 = (bf16[3,3,3,32,32]{4,3,2,1,0:T(8,128)(2,1)S(1)}, bf16[3,3,3,32,32]{4,3,2,1,0:T(8,128)(2,1)}, u32[]{:S(2)}) copy-start(bf16[3,3,3,32,32]{4,3,2,1,0:T(8,128)(2,1)} %param.11) | copy-start | bytes 165892
  27.1 5.3 %copy-start.3 = (bf16[3,3,3,32,32]{4,3,2,1,0:T(8,128)(2,1)S(1)}, bf16[3,3,3,32,32]{4,3,2,1,0:T(8,128)(2,1)}, u32[]{:S(2)}) copy-start(bf16[3,3,3,32,32]{4,3,2,1,0:T(8,128)(2,1)} %param.12) | copy-start | bytes 165892
  27.1 5.3 %copy-start.4 = (bf16[3,3,3,32,32]{4,3,2,1,0:T(8,128)(2,1)S(1)}, bf16[3,3,3,32,32]{4,3,2,1,0:T(8,128)(2,1)}, u32[]{:S(2)}) copy-start(bf16[3,3,3,32,32]{4,3,2,1,0:T(8,128)(2,1)} %param.13) | copy-start | bytes 165892
  27.2 5.3 %copy-start.5 = (bf16[128,128]{1,0:T(8,128)(2,1)S(1)}, bf16[128,128]{1,0:T(8,128)(2,1)}, u32[]{:S(2)}) copy-start(bf16[128,128]{1,0:T(8,128)(2,1)} %constant.35.clone.up) | copy-start | bytes 98308
  27.2 5.3 %copy-start.6 = (bf16[128,128]{1,0:T(8,128)(2,1)S(1)}, bf16[128,128]{1,0:T(8,128)(2,1)}, u32[]{:S(2)}) copy-start(bf16[128,128]{1,0:T(8,128)(2,1)} %constant.36.clone.up0) | copy-start | bytes 98308

commit v4 on v3

--- a/solution.py
+++ b/solution.py
@@ -6,9 +6,11 @@
 from jax.experimental.pallas import tpu as pltpu
 from jax.sharding import PartitionSpec as P
 
+
 INTERPRET = False
 F32, BF16 = jnp.float32, jnp.bfloat16
 LANES = 128
+GROUP = 4
 
 
 def tables():
@@ -30,7 +32,6 @@
     row = lax.broadcasted_iota(jnp.int32, (512, LANES), 0)
     lane = lax.broadcasted_iota(jnp.int32, (1, LANES), 1)
     spot = row & 127
-    base = row - spot
     eighth = jnp.float32(0.125)
 
     def put(k, *terms):
@@ -206,16 +207,6 @@
                 out[10 + 2 * i + k] = value
 
 
-def taps(ref, x, ys):
-    return jnp.concatenate(
-        [
-            jnp.concatenate([ref[x + d, y : y + 3].reshape(288, LANES) for y in ys], axis=1)
-            for d in range(3)
-        ],
-        axis=0,
-    )
-
-
 def weighted(weight, value):
     return lax.dot_general(weight, value, (((0,), (0,)), ((), ())), preferred_element_type=F32)
 
@@ -232,48 +223,139 @@
     ref[i, j, 64:96] = after.astype(BF16)
 
 
-def fine_kernel(flags, x_ref, t1, xr_lo, xr_hi, w0, mix, acc_out, e0):
-    zero = jnp.zeros((96, LANES), BF16)
+def block(w, dz):
+    return jnp.concatenate([w[96 * k + 32 * dz : 96 * k + 32 * dz + 32] for k in range(9)], axis=0)
+
+
+def weights_kernel(w0, w1, w2, w3, mix, f_out, a1_out, a2_out, a3_out):
+    row = lax.broadcasted_iota(jnp.int32, (32, 96), 0)
+    column = lax.broadcasted_iota(jnp.int32, (32, 96), 1)
+    spots = [jnp.where(column == row + 32 * dz, 1.0, 0.0).astype(BF16) for dz in range(3)]
+
+    def placed(dz, value):
+        return lax.dot_general(spots[dz], value, (((0,), (1,)), ((), ())), preferred_element_type=F32)
+
+    for w, out in ((w0, f_out), (w1, a1_out), (w2, a2_out), (w3, a3_out)):
+        total = placed(0, block(w, 0)) + placed(1, block(w, 1)) + placed(2, block(w, 2))
+        out[:, 0:288] = total.astype(BF16)
+    mixed = lax.dot_general(spots[1], mix[...], (((0,), (0,)), ((), ())), preferred_element_type=F32)
+    f_out[:, 288:320] = mixed.astype(BF16)
+
+
+def around(ref, x, ys):
+    return jnp.concatenate(
+        [jnp.concatenate([ref[x + d, y : y + 3].reshape(96, LANES) for y in ys], axis=1) for d in range(3)],
+        axis=0,
+    )
+
+
+def shifted(value, n, lo=None, hi=None):
+    part = value[:, LANES * n : LANES * (n + 1)]
+    before, after = rolled(part[0:32], 1), rolled(part[64:96], -1)
+    if lo is not None:
+        lane = lanes()
+        before = jnp.where(lane == 0, lo, before)
+        after = jnp.where(lane == LANES - 1, hi, after)
+    return part[32:64] + before + after
+
+
+def fine_kernel(x_ref, t1, w0, wf, acc_out, f0):
+    lane = lanes()
+    zero = jnp.zeros((32, LANES), BF16)
     for i in range(10):
-        e0[i, 0] = zero
-        e0[i, 9] = zero
+        f0[i, 0] = zero
+        f0[i, 9] = zero
+        f0[0, i] = zero
+        f0[9, i] = zero
+    f0[1:9, 1:9] = x_ref[...]
+    low = jnp.zeros((32, LANES), F32)
+    high = jnp.zeros((32, LANES), F32)
+    for i in range(4):
+        for j in range(4):
+            value = t1[i, j].astype(F32)
+            for sx in range(2):
+                spot = 12 * (2 * i + sx + 1) + 2 * j + 1
+                here = (lane >= spot) & (lane < spot + 2)
+                low = jnp.where(here, rolled(value, spot - 124 - 2 * sx), low)
+                high = jnp.where(here, rolled(value, spot - 68 - 2 * sx), high)
+
+    def columns(value, dz):
+        near = [rolled(value, -12 * dx - dy).astype(BF16) for dx in (-1, 0, 1) for dy in (-1, 0, 1)]
+        return weighted(block(w0, dz), jnp.concatenate(near, axis=0))
+
+    low, high = columns(low, 0), columns(high, 2)
+    for x in range(8):
+        for y in range(0, 8, GROUP):
+            ys = range(y, y + GROUP)
+            middle = jnp.concatenate([x_ref[x, k] for k in ys], axis=1)
+            value = dot(wf[...], jnp.concatenate([around(f0, x, ys), middle], axis=0))
+            for n, k in enumerate(ys):
+                spot = 12 * (x + 1) + k + 1
+                acc_out[x, k] = shifted(value, n, rolled(low, -spot), rolled(high, 127 - spot))
+
+
+def own_rows_kernel(
+    flags, t1, t2, t3, xr_lo, xr_hi, xr_lo2, xr_hi2, w0, wf1, wf2, wf3,
+    edge_out, a1_out, a2_out, a3_out, ex, f1, f2, f3,
+):
+    x_lo, x_hi, x_lo2, x_hi2 = flags[0], flags[1], flags[6], flags[7]
+    zero = jnp.zeros((32, LANES), BF16)
+    for ref, size in ((f1, 6), (f2, 4), (f3, 3)):
+        for i in range(size + 2):
+            for j in (0, 1, size, size + 1):
+                ref[i, j] = zero
+    for side in range(2):
+        for j in (0, 9):
+            ex[side, j] = jnp.zeros((96, LANES), BF16)
     for k in range(8):
         s = k % 2
-        column = kept(flags[0], xr_lo[8 + 4 + k // 2]).astype(F32)
-        spread(e0, 0, 1 + k, kept(flags[0], xr_lo[k]), 0, rolled(column, 2 - s), rolled(column, 57 - s))
-        column = kept(flags[1], xr_hi[8 + k // 2]).astype(F32)
-        spread(e0, 9, 1 + k, kept(flags[1], xr_hi[k]), 0, rolled(column, 4 - s), rolled(column, 59 - s))
-
-    def fill(c, carry):
-        for part in range(2):
-            for k in range(8):
-                s = 2 * part + k % 2
-                column = t1[c, k // 2].astype(F32)
-                spread(
-                    e0, 2 * c + part + 1, 1 + k, x_ref[2 * c + part, k], 0,
-                    rolled(column, 4 - s), rolled(column, 59 - s),
-                )
-        return carry
-
-    lax.fori_loop(0, 4, fill, 0)
-    weight = jnp.concatenate([w0[...], mix[...]], axis=0)
-
-    def fine(x, carry):
+        column = kept(x_lo, xr_lo[8 + 4 + k // 2]).astype(F32)
+        spread(ex, 0, 1 + k, kept(x_lo, xr_lo[k]), 0, rolled(column, 2 - s), rolled(column, 57 - s))
+        column = kept(x_hi, xr_hi[8 + k // 2]).astype(F32)
+        spread(ex, 1, 1 + k, kept(x_hi, xr_hi[k]), 0, rolled(column, 4 - s), rolled(column, 59 - s))
+
+    def back(value):
+        return rolled(value.astype(F32), -72).astype(BF16)
+
+    for k in range(4):
+        for i in range(2):
+            f1[i, 2 + k] = kept(x_lo, xr_lo[8 + 4 * i + k])
+            f1[6 + i, 2 + k] = kept(x_hi, xr_hi[8 + 4 * i + k])
+        for i in range(4):
+            f1[2 + i, 2 + k] = t1[i, k]
+    for i in range(2):
+        for k in range(2):
+            f2[i, 2 + k] = back(kept(x_lo, xr_lo[8 + 2 * i + k]))
+            f2[2 + i, 2 + k] = t2[i, k]
+            f2[4 + i, 2 + k] = back(kept(x_hi, xr_hi[8 + 2 * i + k]))
+    f3[0, 2] = kept(x_lo2, xr_lo2[...])
+    f3[1, 2] = back(kept(x_lo, xr_lo[12]))
+    f3[2, 2] = t3[...]
+    f3[3, 2] = back(kept(x_hi, xr_hi[12]))
+    f3[4, 2] = kept(x_hi2, xr_hi2[...])
+
+    for side, dx in ((0, 0), (1, 2)):
+        weight = w0[288 * dx : 288 * dx + 288]
         for y in range(0, 8, 2):
-            middle = jnp.concatenate([x_ref[x, y], x_ref[x, y + 1]], axis=1)
-            value = weighted(weight, jnp.concatenate([taps(e0, x, [y, y + 1]), middle], axis=0))
-            acc_out[x, y] = value[:, :LANES]
-            acc_out[x, y + 1] = value[:, LANES:]
-        return carry
-
-    lax.fori_loop(0, 8, fine, 0)
+            value = jnp.concatenate(
+                [ex[side, y : y + 3].reshape(288, LANES), ex[side, y + 1 : y + 4].reshape(288, LANES)], axis=1
+            )
+            value = weighted(weight, value)
+            edge_out[side, y] = value[:, :LANES]
+            edge_out[side, y + 1] = value[:, LANES:]
+    for ref, w, out, size in ((f3, wf3, a3_out, 3), (f2, wf2, a2_out, 4), (f1, wf1, a1_out, 6)):
+        for i in range(size):
+            value = dot(w[...], around(ref, i, range(size)))
+            for j in range(size):
+                out[i, j] = shifted(value, j)
 
 
 def final_kernel(
-    flags, acc, t1, t2, t3, xr_lo, xr_hi, xr_lo2, xr_hi2, yr_lo, yr_hi, yr_two,
+    flags, acc, edge_x, a1, a2, a3, yr_lo, yr_hi, yr_two,
     w0, w1, w2, w3, up, up0, out_ref, ey, edge, e1, e2, e3, v3, v2, v1, q1, rows,
 ):
-    x_lo, x_hi, y_lo, y_hi, z_lo, z_hi, x_lo2, x_hi2, y_lo2, y_hi2 = (flags[i] for i in range(10))
+    x_lo, x_hi, y_lo, y_hi, z_lo, z_hi = (flags[i] for i in range(6))
+    y_lo2, y_hi2 = flags[8], flags[9]
     lane = lanes()
 
     for i in range(5):
@@ -281,30 +363,14 @@
         spread(e3, i, 1, kept(y_lo, yr_lo[22 + i // 2]), -72 - 20 * (i % 2))
         spread(e3, i, 3, kept(y_hi, yr_hi[22 + i // 2]), -72 - 20 * (i % 2))
         spread(e3, i, 4, kept(y_hi2, yr_two[...]), -20 * i)
-    spread(e3, 0, 2, kept(x_lo2, xr_lo2[...]))
-    spread(e3, 1, 2, kept(x_lo, xr_lo[12]), -72)
-    spread(e3, 2, 2, t3[...])
-    spread(e3, 3, 2, kept(x_hi, xr_hi[12]), -72)
-    spread(e3, 4, 2, kept(x_hi2, xr_hi2[...]))
     for i in range(6):
         for k in range(2):
             spread(e2, i, k, kept(y_lo, yr_lo[10 + 2 * i + k]), -72)
             spread(e2, i, 4 + k, kept(y_hi, yr_hi[10 + 2 * i + k]), -72)
-    for i in range(2):
-        for k in range(2):
-            spread(e2, i, 2 + k, kept(x_lo, xr_lo[8 + 2 * i + k]), -72)
-            spread(e2, 2 + i, 2 + k, t2[i, k])
-            spread(e2, 4 + i, 2 + k, kept(x_hi, xr_hi[8 + 2 * i + k]), -72)
     for i in range(8):
         for k in range(2):
             spread(e1, i, k, kept(y_lo, yr_lo[10 + 2 * i + k]))
             spread(e1, i, 6 + k, kept(y_hi, yr_hi[10 + 2 * i + k]))
-    for k in range(4):
-        for i in range(2):
-            spread(e1, i, 2 + k, kept(x_lo, xr_lo[8 + 4 * i + k]))
-            spread(e1, 6 + i, 2 + k, kept(x_hi, xr_hi[8 + 4 * i + k]))
-        for i in range(4):
-            spread(e1, 2 + i, 2 + k, t1[i, k])
     for i in range(10):
         sx = (i + 1) % 2
         coarse = (i + 1) // 2 + 1
@@ -347,29 +413,44 @@
         by_x = refined([wide[i] for i in range(count)])
         return [refined([row[j] for j in range(count)]) for row in by_x]
 
-    def level(e_ref, w_ref, v_ref, size, cells, above):
+    def level(e_ref, w_ref, own, v_ref, size, cells, above):
         keep = limits(cells)
-        for i in range(size):
-            for j in range(0, size, 2):
-                ys = [j, j + 1] if j + 1 < size else [j]
-                value = weighted(w_ref[...], taps(e_ref, i, ys))
-                for n, y in enumerate(ys):
-                    part = value[:, LANES * n : LANES * (n + 1)]
+        for j in range(size):
+            dys = [dy for dy in range(3) if not 2 <= j + dy < size]
+            weight = jnp.concatenate(
+                [w_ref[96 * (3 * dx + dy) : 96 * (3 * dx + dy) + 96] for dx in range(3) for dy in dys], axis=0
+            ) if dys else None
+            for i in range(0, size, 2):
+                xs = [i, i + 1] if i + 1 < size else [i]
+                if dys:
+                    value = jnp.concatenate(
+                        [
+                            jnp.concatenate([e_ref[x + dx, j + dy] for x in xs], axis=1)
+                            for dx in range(3)
+                            for dy in dys
+                        ],
+                        axis=0,
+                    )
+                    value = weighted(weight, value)
+                for n, x in enumerate(xs):
+                    part = own[x, j]
+                    if dys:
+                        part = part + value[:, LANES * n : LANES * (n + 1)]
                     if above is not None:
-                        part = part + above[i][y]
+                        part = part + above[x][j]
                     good = keep
-                    for flag in (cell_flag(i, size - 1, x_lo, x_hi), cell_flag(y, size - 1, y_lo, y_hi)):
+                    for flag in (cell_flag(x, size - 1, x_lo, x_hi), cell_flag(j, size - 1, y_lo, y_hi)):
                         if flag is not None:
                             good = good & (flag > 0)
-                    v_ref[i, y] = jnp.where(good, part, 0.0).astype(BF16)
-
-    level(e3, w3, v3, 3, 16, None)
-    level(e2, w2, v2, 4, 32, prolonged(v3, 3))
-    level(e1, w1, v1, 6, 64, prolonged(v2, 4))
+                    v_ref[x, j] = jnp.where(good, part, 0.0).astype(BF16)
+
+    level(e3, w3, a3, v3, 3, 16, None)
+    level(e2, w2, a2, v2, 4, 32, prolonged(v3, 3))
+    level(e1, w1, a1, v1, 6, 64, prolonged(v2, 4))
     for i in range(6):
         q1[i] = dot(v1[i].reshape(6 * 32, LANES), up0[...]).reshape(6, 32, LANES)
 
-    def fine(c, carry):
+    def fine(c, side):
         for part in range(2):
             x = 2 * c + part
             row = 0.75 * q1[c + 1] + 0.25 * q1[c + 2 * part]
@@ -381,10 +462,13 @@
                         total = total + edge[0, x]
                     if y + n == 7:
                         total = total + edge[1, x]
+                    if side == part:
+                        total = total + edge_x[side, y + n]
                     rows[pl.ds(x * 8 + y + n, 32, stride=64), :] = jax.nn.gelu(total, approximate=True)
-        return carry
-
-    lax.fori_loop(0, 4, fine, 0)
+
+    fine(0, 0)
+    lax.fori_loop(1, 3, lambda c, carry: (fine(c, -1), carry)[1], 0)
+    fine(3, 1)
     out_ref[...] = rows[...].reshape(32, 8, 8, LANES).astype(BF16)
 
 
@@ -413,8 +497,12 @@
         [pltpu.VMEM((2048, LANES), F32)],
         0,
     )
+    flat = [k.reshape(864, 32) for k in (kernel_fine, kernel_half, kernel_quarter, kernel_eighth)]
+    mixing, *flat, t3 = lax.optimization_barrier((mixing, *flat, t3))
+    wf = call(weights_kernel, [(96, 320)] + [(96, 288)] * 3, [*flat, mixing], scalars=0, flops=1 << 28)
     from_hi = turned(msg[0], "gz", -1)
     from_lo = turned(msg[1], "gz", 1)
+    from_lo, *wf = lax.optimization_barrier((from_lo, *wf))
     t1, t2, t3, x_msg_lo, x_msg_hi = call(
         depth_kernel,
         [(4, 4) + tile, (2, 2) + tile, tile, (16,) + tile, (16,) + tile],
@@ -424,6 +512,16 @@
     xr_lo = turned(x_msg_hi, "gx", 1)
     xr_hi2 = turned(t3, "gx", -2)
     xr_lo2 = turned(t3, "gx", 2)
+    (acc,) = call(
+        fine_kernel,
+        [(8, 8) + tile],
+        [x_own, t1, flat[0], wf[0]],
+        [pltpu.VMEM((10, 10) + tile, BF16)],
+        0,
+        kind=F32,
+        flops=1 << 30,
+    )
+    xr_lo, acc = lax.optimization_barrier((xr_lo, acc))
     y_msg_lo, y_msg_hi, two = call(
         width_kernel,
         [(26,) + tile, (26,) + tile, tile],
@@ -433,20 +531,23 @@
     yr_lo = turned(y_msg_hi, "gy", 1)
     assert ny == 4
     yr_two = turned(two, "gy", 2)
-    flat = [k.reshape(864, 32) for k in (kernel_fine, kernel_half, kernel_quarter, kernel_eighth)]
-    (acc,) = call(
-        fine_kernel,
-        [(8, 8) + tile],
-        [flags, x_own, t1, xr_lo, xr_hi, flat[0], mixing.T],
-        [pltpu.VMEM((10, 10, 96, LANES), BF16)],
+    edge_x, a1, a2, a3 = call(
+        own_rows_kernel,
+        [(2, 8) + tile, (6, 6) + tile, (4, 4) + tile, (3, 3) + tile],
+        [flags, t1, t2, t3, xr_lo, xr_hi, xr_lo2, xr_hi2, flat[0], *wf[1:]],
+        [
+            pltpu.VMEM((2, 10, 96, LANES), BF16),
+            pltpu.VMEM((8, 8) + tile, BF16),
+            pltpu.VMEM((6, 6) + tile, BF16),
+            pltpu.VMEM((5, 5) + tile, BF16),
+        ],
         kind=F32,
         flops=1 << 30,
     )
     (out,) = call(
         final_kernel,
         [(32, 8, 8, LANES)],
-        [flags, acc, t1, t2, t3, xr_lo, xr_hi, xr_lo2, xr_hi2, yr_lo, yr_hi, yr_two,
-         *flat, up, up0],
+        [flags, acc, edge_x, a1, a2, a3, yr_lo, yr_hi, yr_two, *flat, up, up0],
         [
             pltpu.VMEM((2, 10, 96, LANES), BF16),
             pltpu.VMEM((2, 8) + tile, F32),
@@ -465,6 +566,5 @@
 
 def solution(mesh):
     placed = (P(None, "gx", "gy", "gz"), P(), P(), P(), P(), P())
-    return jax.shard_map(
-        on_device, mesh=mesh, in_specs=placed, out_specs=P(None, "gx", "gy", "gz"), check_vma=False
-    )
+
+    return jax.shard_map(on_device, mesh=mesh, in_specs=placed, out_specs=P(None, "gx", "gy", "gz"), check_vma=False)

time: 38.5 us -> 37.5 us (0.974)
  the two profiles are of different devices: /device:TPU:64 before, /device:TPU:8 now
where the time goes in v4:
time: 37.5 us; the launch traced here: 37.3 us
  starting transfers between devices  15.6 us (42%)
  Pallas kernels  12.2 us (33%)
  waiting for transfers between devices  8.11 us (22%)
  local copies, waits for them, and re-layouts  1.37 us (4%)
    ppermute x9, starting transfers between devices, turned(): lax.ppermute(value, axis, [(i, (i + step) % count) for i in range(count)])  15.6 us
    pallas_call x8, Pallas kernels, call(): pl.pallas_call(kernel, out_shape=[jax.ShapeDtypeStruct(shape, kind) for s...  12.2 us
    ppermute x9, waiting for transfers between devices, turned(): lax.ppermute(value, axis, [(i, (i + step) % count) for i in range(count)])  8.11 us
    unnamed x16, local copies, waits for them, and re-layouts  1.36 us
  transfers between devices with their start and end apart: 9, of which 3 were waited for; matrix products, arithmetic and copies ran while one was open for 0% of the time, Pallas kernels for 12%

profile of v4, /device:TPU:8, one launch (start us, length us, event | category | flops | bytes accessed | tf_op | source)
XLA Modules:
  0.0 37.3 jit_solution(2890922188699211642)
XLA Ops:
  0.0 0.3 shard_map.82.table
  0.3 0.7 %copy-done = bf16[32,8,8,128]{3,2,1,0:T(8,128)(2,1)S(1)} copy-done((bf16[32,8,8,128]{3,2,1,0:T(8,128)(2,1)S(1)}, bf16[32,8,8,128]{3,2,1,0:T(8,128)(2,1)}, u32[]{:S(2)}) %copy-start) | copy-done | bytes 524312
  1.1 1.2 %shard_map.83 = (bf16[8,8,32,128]{3,2,1,0:T(8,128)(2,1)S(1)}, bf16[4,4,32,128]{3,2,1,0:T(8,128)(2,1)S(1)}, bf16[2,2,32,128]{3,2,1,0:T(8,128)(2,1)S(1)}, bf16[32,...) custom-call(bf16[32,8,8,128]{3,2,1,0:T(8,128)(2,1)S(1)} %copy-done, bf16[512,640]{1,0:T(8,128)(2,1)S(1)} %shard_map.82.table), custom_call_target="tpu_custom_call" | custom-call | flops 1048576 | bytes 1048576 | tf_op jit(solution)/shard_map/pallas_call | solution.py:79
  2.3 2.2 %collective-permute-start.1 = (bf16[32,128]{1,0:T(8,128)(2,1)S(1)}, bf16[32,128]{1,0:T(8,128)(2,1)S(1)}, u32[]{:S(2)}, u32[]{:S(2)}) collective-permute-start(bf16[32,128]{1,0:T(8,128)(2,1)S(1)} %get-tuple-element.73), channel_id=1, source_target_pairs={{0,7},{1,0},{2,1},{3,2},{4,3},{5,4},{6,5},{7,6},{8,15},{9,8},{10,9... | collective-permute-start | bytes 24584 | tf_op jit(solution)/shard_map/ppermute | solution.py:477
  4.5 0.0 collective-permute-start
  4.5 0.0 copy-done.1
  4.5 0.0 copy-done.2
  4.5 0.0 copy-done.3
  4.6 0.0 copy-done.4
  4.6 0.6 %copy-done.7 = bf16[32,32]{1,0:T(8,128)(2,1)S(1)} copy-done((bf16[32,32]{1,0:T(8,128)(2,1)S(1)}, bf16[32,32]{1,0:T(8,128)(2,1)}, u32[]{:S(2)}) %copy-start.7) | copy-done | bytes 2072
  5.2 0.6 %shard_map.84 = (bf16[96,320]{1,0:T(8,128)(2,1)S(1)}, bf16[96,288]{1,0:T(8,128)(2,1)S(1)}, bf16[96,288]{1,0:T(8,128)(2,1)S(1)}, bf16[96,288]{1,0:T(8,128)(2,1)S(1)}) custom-call(bf16[864,32]{1,0:T(8,128)(2,1)S(1)} %bitcast.8, bf16[864,32]{1,0:T(8,128)(2,1)S(1)} %bitcast.12, bf16[864,32]{1,0:T(8,128)(2,1)S(1)} %bitcast.14, bf16[864,32]{1,0:T(8,128)(2,1)S(1)} %bitcast.16, ...), custom_call_target="tpu_custom_call" | custom-call | flops 268435456 | bytes 1048576 | tf_op jit(solution)/shard_map/pallas_call | solution.py:79
  5.8 3.0 %collective-permute-done.from_lo = bf16[32,128]{1,0:T(8,128)(2,1)S(1)} collective-permute-done((bf16[32,128]{1,0:T(8,128)(2,1)S(1)}, bf16[32,128]{1,0:T(8,128)(2,1)S(1)}, u32[]{:S(2)}, u32[]{:S(2)}) %collective-permute-start) | collective-permute-done | bytes 8224 | tf_op jit(solution)/shard_map/ppermute | solution.py:477
  8.8 0.0 collective-permute-done.1.from_hi
  8.8 0.7 %shard_map.85 = (bf16[4,4,32,128]{3,2,1,0:T(8,128)(2,1)S(1)}, bf16[2,2,32,128]{3,2,1,0:T(8,128)(2,1)S(1)}, bf16[32,128]{1,0:T(8,128)(2,1)S(1)}, bf16[16,32,128]{2,1,0:T(8,128)(2,1)S(1)}, bf16[16,32,128]{2,1,0:T(8,128)(2,1)S(1)}) custom-call(s32[16]{0:T(128)S(1)} %select_convert_fusion.flags, bf16[8,8,32,128]{3,2,1,0:T(8,128)(2,1)S(1)} %get-tuple-element.39.x_ref, ...), custom_call_target="tpu_custom_call" | custom-call | flops 1048576 | bytes 1048576 | tf_op jit(solution)/shard_map/pallas_call | solution.py:79
  9.5 2.0 %collective-permute-start.2 = (bf16[16,32,128]{2,1,0:T(8,128)(2,1)S(1)}, bf16[16,32,128]{2,1,0:T(8,128)(2,1)S(1)}, u32[]{:S(2)}, u32[]{:S(2)}) collective-permute-start(bf16[16,32,128]{2,1,0:T(8,128)(2,1)S(1)} %get-tuple-element.55), channel_id=1, source_target_pairs={{0,32},{32,64},{64,96},{96,128},{128,160},{160,192},{192,224},{224... | collective-permute-start | bytes 393224 | tf_op jit(solution)/shard_map/ppermute | solution.py:477
  11.5 4.0 %collective-permute-start.3 = (bf16[16,32,128]{2,1,0:T(8,128)(2,1)S(1)}, bf16[16,32,128]{2,1,0:T(8,128)(2,1)S(1)}, u32[]{:S(2)}, u32[]{:S(2)}) collective-permute-start(bf16[16,32,128]{2,1,0:T(8,128)(2,1)S(1)} %get-tuple-element.62), channel_id=1, source_target_pairs={{0,224},{32,0},{64,32},{96,64},{128,96},{160,128},{192,160},{224,1... | collective-permute-start | bytes 393224 | tf_op jit(solution)/shard_map/ppermute | solution.py:477
  15.6 2.4 %collective-permute-start.5 = (bf16[32,128]{1,0:T(8,128)(2,1)S(1)}, bf16[32,128]{1,0:T(8,128)(2,1)S(1)}, u32[]{:S(2)}, u32[]{:S(2)}) collective-permute-start(bf16[32,128]{1,0:T(8,128)(2,1)S(1)} %get-tuple-element.60.t3), channel_id=1, source_target_pairs={{0,192},{32,224},{64,0},{96,32},{128,64},{160,96},{192,128},{224,1... | collective-permute-start | bytes 24584 | tf_op jit(solution)/shard_map/ppermute | solution.py:477
  17.9 0.5 %collective-permute-start.4 = (bf16[32,128]{1,0:T(8,128)(2,1)S(1)}, bf16[32,128]{1,0:T(8,128)(2,1)S(1)}, u32[]{:S(2)}, u32[]{:S(2)}) collective-permute-start(bf16[32,128]{1,0:T(8,128)(2,1)S(1)} %get-tuple-element.60.t3), channel_id=1, source_target_pairs={{0,64},{32,96},{64,128},{96,160},{128,192},{160,224},{192,0},{224,... | collective-permute-start | bytes 24584 | tf_op jit(solution)/shard_map/ppermute | solution.py:477
  18.5 1.7 %shard_map.86.acc = f32[8,8,32,128]{3,2,1,0:T(8,128)S(1)} custom-call(bf16[8,8,32,128]{3,2,1,0:T(8,128)(2,1)S(1)} %get-tuple-element.39.x_ref, bf16[4,4,32,128]{3,2,1,0:T(8,128)(2,1)S(1)} %get-tuple-element.56.t1, bf16[864,32]{1,0:T(8,128)(2,1)S(1)} %bitcast.9, bf16[96,320]{1,0:T(8,128)(2,1)S(1)} %get-tuple-element.57.wf), custom_call_target="tpu_custom_call" | custom-call | flops 1073741824 | bytes 1048576 | tf_op jit(solution)/shard_map/pallas_call | solution.py:79
  20.2 0.0 collective-permute-done.2.xr_lo
  20.2 0.0 collective-permute-done.5.xr_hi2
  20.2 3.5 %collective-permute-done.4.xr_lo2 = bf16[32,128]{1,0:T(8,128)(2,1)S(1)} collective-permute-done((bf16[32,128]{1,0:T(8,128)(2,1)S(1)}, bf16[32,128]{1,0:T(8,128)(2,1)S(1)}, u32[]{:S(2)}, u32[]{:S(2)}) %collective-permute-start.4) | collective-permute-done | bytes 8224 | tf_op jit(solution)/shard_map/ppermute | solution.py:477
  23.7 0.0 collective-permute-done.3.xr_hi
  23.7 0.8 %shard_map.88 = (bf16[26,32,128]{2,1,0:T(8,128)(2,1)S(1)}, bf16[26,32,128]{2,1,0:T(8,128)(2,1)S(1)}, bf16[32,128]{1,0:T(8,128)(2,1)S(1)}) custom-call(s32[16]{0:T(128)S(1)} %select_convert_fusion.flags, bf16[8,8,32,128]{3,2,1,0:T(8,128)(2,1)S(1)} %get-tuple-element.39.x_ref, bf16[4,4,32,128]{3,2,1,0:T(8,128)(2,1)S(1)} %get-tuple-element.56.t1, ...), custom_call_target="tpu_custom_call" | custom-call | flops 1048576 | bytes 1048576 | tf_op jit(solution)/shard_map/pallas_call | solution.py:79
  24.5 1.7 %collective-permute-start.6 = (bf16[26,32,128]{2,1,0:T(8,128)(2,1)S(1)}, bf16[26,32,128]{2,1,0:T(8,128)(2,1)S(1)}, u32[]{:S(2)}, u32[]{:S(2)}) collective-permute-start(bf16[26,32,128]{2,1,0:T(8,128)(2,1)S(1)} %get-tuple-element.70), channel_id=1, source_target_pairs={{0,8},{8,16},{16,24},{24,0},{1,9},{9,17},{17,25},{25,1},{2,10},{10... | collective-permute-start | bytes 638984 | tf_op jit(solution)/shard_map/ppermute | solution.py:477
  26.2 0.5 %collective-permute-start.7 = (bf16[26,32,128]{2,1,0:T(8,128)(2,1)S(1)}, bf16[26,32,128]{2,1,0:T(8,128)(2,1)S(1)}, u32[]{:S(2)}, u32[]{:S(2)}) collective-permute-start(bf16[26,32,128]{2,1,0:T(8,128)(2,1)S(1)} %get-tuple-element.71), channel_id=1, source_target_pairs={{0,24},{8,0},{16,8},{24,16},{1,25},{9,1},{17,9},{25,17},{2,26},{10... | collective-permute-start | bytes 638984 | tf_op jit(solution)/shard_map/ppermute | solution.py:477
  26.6 2.3 %collective-permute-start.8 = (bf16[32,128]{1,0:T(8,128)(2,1)S(1)}, bf16[32,128]{1,0:T(8,128)(2,1)S(1)}, u32[]{:S(2)}, u32[]{:S(2)}) collective-permute-start(bf16[32,128]{1,0:T(8,128)(2,1)S(1)} %get-tuple-element.72), channel_id=1, source_target_pairs={{0,16},{8,24},{16,0},{24,8},{1,17},{9,25},{17,1},{25,9},{2,18},{10... | collective-permute-start | bytes 24584 | tf_op jit(solution)/shard_map/ppermute | solution.py:477
  28.9 2.3 %shard_map.87 = (f32[2,8,32,128]{3,2,1,0:T(8,128)S(1)}, f32[6,6,32,128]{3,2,1,0:T(8,128)S(1)}, f32[4,4,32,128]{3,2,1,0:T(8,128)S(1)}, f32[3,3,32,128]{3,2,1,0:T(8,128)S(1)}) custom-call(s32[16]{0:T(128)S(1)} %select_convert_fusion.flags, bf16[4,4,32,128]{3,2,1,0:T(8,128)(2,1)S(1)} %get-tuple-element.56.t1, bf16[2,2,32,128]{3,2,1,0:T(8,128)(2,1)S(1)} %get-tuple-element.59.t2, ...), custom_call_target="tpu_custom_call" | custom-call | flops 1073741824 | bytes 1048576 | tf_op jit(solution)/shard_map/pallas_call | solution.py:79
  31.2 1.6 %collective-permute-done.8.yr_two = bf16[32,128]{1,0:T(8,128)(2,1)S(1)} collective-permute-done((bf16[32,128]{1,0:T(8,128)(2,1)S(1)}, bf16[32,128]{1,0:T(8,128)(2,1)S(1)}, u32[]{:S(2)}, u32[]{:S(2)}) %collective-permute-start.8) | collective-permute-done | bytes 8224 | tf_op jit(solution)/shard_map/ppermute | solution.py:477
  32.8 0.0 collective-permute-done.6.yr_lo
  32.8 0.0 collective-permute-done.7.yr_hi
  32.8 4.5 %shard_map.89 = bf16[32,8,8,128]{3,2,1,0:T(8,128)(2,1)} custom-call(s32[16]{0:T(128)S(1)} %select_convert_fusion.flags, f32[8,8,32,128]{3,2,1,0:T(8,128)S(1)} %shard_map.86.acc, f32[2,8,32,128]{3,2,1,0:T(8,128)S(1)} %get-tuple-element.66.edge_x, f32[6,6,32,128]{3,2,1,0:T(8,128)S(1)} %get-tuple-element.67.a1, f32[4,4,32,128]{3,2,1,0:T(8,128)S(1)} %get-tuple-element.68.a2, ...), custom_call_target="tpu_custom_call" | custom-call | flops 1048576 | bytes 1048576 | tf_op jit(solution)/shard_map/pallas_call | solution.py:79
  (12 shorter events, 0.0 us)
Async XLA Ops:
  0.0 1.0 %copy-start = (bf16[32,8,8,128]{3,2,1,0:T(8,128)(2,1)S(1)}, bf16[32,8,8,128]{3,2,1,0:T(8,128)(2,1)}, u32[]{:S(2)}) copy-start(bf16[32,8,8,128]{3,2,1,0:T(8,128)(2,1)} %field.1) | copy-start | bytes 1572868
  1.0 3.5 %copy-start.1 = (bf16[3,3,3,32,32]{4,3,2,1,0:T(8,128)(2,1)S(1)}, bf16[3,3,3,32,32]{4,3,2,1,0:T(8,128)(2,1)}, u32[]{:S(2)}) copy-start(bf16[3,3,3,32,32]{4,3,2,1,0:T(8,128)(2,1)} %param.10) | copy-start | bytes 165892
  1.0 3.5 %copy-start.2 = (bf16[3,3,3,32,32]{4,3,2,1,0:T(8,128)(2,1)S(1)}, bf16[3,3,3,32,32]{4,3,2,1,0:T(8,128)(2,1)}, u32[]{:S(2)}) copy-start(bf16[3,3,3,32,32]{4,3,2,1,0:T(8,128)(2,1)} %param.11) | copy-start | bytes 165892
  1.0 3.5 %copy-start.3 = (bf16[3,3,3,32,32]{4,3,2,1,0:T(8,128)(2,1)S(1)}, bf16[3,3,3,32,32]{4,3,2,1,0:T(8,128)(2,1)}, u32[]{:S(2)}) copy-start(bf16[3,3,3,32,32]{4,3,2,1,0:T(8,128)(2,1)} %param.12) | copy-start | bytes 165892
  1.0 3.5 %copy-start.4 = (bf16[3,3,3,32,32]{4,3,2,1,0:T(8,128)(2,1)S(1)}, bf16[3,3,3,32,32]{4,3,2,1,0:T(8,128)(2,1)}, u32[]{:S(2)}) copy-start(bf16[3,3,3,32,32]{4,3,2,1,0:T(8,128)(2,1)} %param.13) | copy-start | bytes 165892
  2.3 6.5 %collective-permute-start.1 = (bf16[32,128]{1,0:T(8,128)(2,1)S(1)}, bf16[32,128]{1,0:T(8,128)(2,1)S(1)}, u32[]{:S(2)}, u32[]{:S(2)}) collective-permute-start(bf16[32,128]{1,0:T(8,128)(2,1)S(1)} %get-tuple-element.73), channel_id=1, source_target_pairs={{0,7},{1,0},{2,1},{3,2},{4,3},{5,4},{6,5},{7,6},{8,15},{9,8},{10,9... | collective-permute-start | bytes 24584 | tf_op jit(solution)/shard_map/ppermute | solution.py:477
  4.5 4.3 %collective-permute-start = (bf16[32,128]{1,0:T(8,128)(2,1)S(1)}, bf16[32,128]{1,0:T(8,128)(2,1)S(1)}, u32[]{:S(2)}, u32[]{:S(2)}) collective-permute-start(bf16[32,128]{1,0:T(8,128)(2,1)S(1)} %get-tuple-element.74), channel_id=1, source_target_pairs={{0,1},{1,2},{2,3},{3,4},{4,5},{5,6},{6,7},{7,0},{8,9},{9,10},{10,1... | collective-permute-start | bytes 24584 | tf_op jit(solution)/shard_map/ppermute | solution.py:477
  4.5 0.7 %copy-start.7 = (bf16[32,32]{1,0:T(8,128)(2,1)S(1)}, bf16[32,32]{1,0:T(8,128)(2,1)}, u32[]{:S(2)}) copy-start(bf16[32,32]{1,0:T(8,128)(2,1)} %mix) | copy-start | bytes 6148
  9.5 10.6 %collective-permute-start.2 = (bf16[16,32,128]{2,1,0:T(8,128)(2,1)S(1)}, bf16[16,32,128]{2,1,0:T(8,128)(2,1)S(1)}, u32[]{:S(2)}, u32[]{:S(2)}) collective-permute-start(bf16[16,32,128]{2,1,0:T(8,128)(2,1)S(1)} %get-tuple-element.55), channel_id=1, source_target_pairs={{0,32},{32,64},{64,96},{96,128},{128,160},{160,192},{192,224},{224... | collective-permute-start | bytes 393224 | tf_op jit(solution)/shard_map/ppermute | solution.py:477
  11.5 12.2 %collective-permute-start.3 = (bf16[16,32,128]{2,1,0:T(8,128)(2,1)S(1)}, bf16[16,32,128]{2,1,0:T(8,128)(2,1)S(1)}, u32[]{:S(2)}, u32[]{:S(2)}) collective-permute-start(bf16[16,32,128]{2,1,0:T(8,128)(2,1)S(1)} %get-tuple-element.62), channel_id=1, source_target_pairs={{0,224},{32,0},{64,32},{96,64},{128,96},{160,128},{192,160},{224,1... | collective-permute-start | bytes 393224 | tf_op jit(solution)/shard_map/ppermute | solution.py:477
  15.6 4.6 %collective-permute-start.5 = (bf16[32,128]{1,0:T(8,128)(2,1)S(1)}, bf16[32,128]{1,0:T(8,128)(2,1)S(1)}, u32[]{:S(2)}, u32[]{:S(2)}) collective-permute-start(bf16[32,128]{1,0:T(8,128)(2,1)S(1)} %get-tuple-element.60.t3), channel_id=1, source_target_pairs={{0,192},{32,224},{64,0},{96,32},{128,64},{160,96},{192,128},{224,1... | collective-permute-start | bytes 24584 | tf_op jit(solution)/shard_map/ppermute | solution.py:477
  17.9 5.8 %collective-permute-start.4 = (bf16[32,128]{1,0:T(8,128)(2,1)S(1)}, bf16[32,128]{1,0:T(8,128)(2,1)S(1)}, u32[]{:S(2)}, u32[]{:S(2)}) collective-permute-start(bf16[32,128]{1,0:T(8,128)(2,1)S(1)} %get-tuple-element.60.t3), channel_id=1, source_target_pairs={{0,64},{32,96},{64,128},{96,160},{128,192},{160,224},{192,0},{224,... | collective-permute-start | bytes 24584 | tf_op jit(solution)/shard_map/ppermute | solution.py:477
  24.5 8.3 %collective-permute-start.6 = (bf16[26,32,128]{2,1,0:T(8,128)(2,1)S(1)}, bf16[26,32,128]{2,1,0:T(8,128)(2,1)S(1)}, u32[]{:S(2)}, u32[]{:S(2)}) collective-permute-start(bf16[26,32,128]{2,1,0:T(8,128)(2,1)S(1)} %get-tuple-element.70), channel_id=1, source_target_pairs={{0,8},{8,16},{16,24},{24,0},{1,9},{9,17},{17,25},{25,1},{2,10},{10... | collective-permute-start | bytes 638984 | tf_op jit(solution)/shard_map/ppermute | solution.py:477
  26.2 6.7 %collective-permute-start.7 = (bf16[26,32,128]{2,1,0:T(8,128)(2,1)S(1)}, bf16[26,32,128]{2,1,0:T(8,128)(2,1)S(1)}, u32[]{:S(2)}, u32[]{:S(2)}) collective-permute-start(bf16[26,32,128]{2,1,0:T(8,128)(2,1)S(1)} %get-tuple-element.71), channel_id=1, source_target_pairs={{0,24},{8,0},{16,8},{24,16},{1,25},{9,1},{17,9},{25,17},{2,26},{10... | collective-permute-start | bytes 638984 | tf_op jit(solution)/shard_map/ppermute | solution.py:477
  26.6 6.2 %copy-start.5 = (bf16[128,128]{1,0:T(8,128)(2,1)S(1)}, bf16[128,128]{1,0:T(8,128)(2,1)}, u32[]{:S(2)}) copy-start(bf16[128,128]{1,0:T(8,128)(2,1)} %constant.36.clone.up0) | copy-start | bytes 98308
  26.6 6.2 %copy-start.6 = (bf16[128,128]{1,0:T(8,128)(2,1)S(1)}, bf16[128,128]{1,0:T(8,128)(2,1)}, u32[]{:S(2)}) copy-start(bf16[128,128]{1,0:T(8,128)(2,1)} %constant.35.clone.up) | copy-start | bytes 98308
  26.6 6.2 %collective-permute-start.8 = (bf16[32,128]{1,0:T(8,128)(2,1)S(1)}, bf16[32,128]{1,0:T(8,128)(2,1)S(1)}, u32[]{:S(2)}, u32[]{:S(2)}) collective-permute-start(bf16[32,128]{1,0:T(8,128)(2,1)S(1)} %get-tuple-element.72), channel_id=1, source_target_pairs={{0,16},{8,24},{16,0},{24,8},{1,17},{9,25},{17,1},{25,9},{2,18},{10... | collective-permute-start | bytes 24584 | tf_op jit(solution)/shard_map/ppermute | solution.py:477

commit v5 on v4

--- a/solution.py
+++ b/solution.py
@@ -73,14 +73,14 @@
     return jnp.dot(a, b, preferred_element_type=F32)
 
 
-def call(kernel, outs, args, scratch=(), scalars=1, kind=BF16, flops=1 << 20):
+def call(kernel, outs, args, scratch=(), scalars=1, kind=BF16, flops=1 << 20, out_space=pltpu.VMEM):
     specs = [pl.BlockSpec(memory_space=pltpu.SMEM)] * scalars
     specs += [pl.BlockSpec(memory_space=pltpu.VMEM)] * (len(args) - scalars)
     return pl.pallas_call(
         kernel,
         out_shape=[jax.ShapeDtypeStruct(shape, kind) for shape in outs],
         in_specs=specs,
-        out_specs=[pl.BlockSpec(memory_space=pltpu.VMEM)] * len(outs),
+        out_specs=[pl.BlockSpec(memory_space=out_space)] * len(outs),
         scratch_shapes=list(scratch),
         compiler_params=pltpu.CompilerParams(vmem_limit_bytes=48 * 1024 * 1024),
         cost_estimate=pl.CostEstimate(flops=flops, transcendentals=0, bytes_accessed=1 << 20),
@@ -352,25 +352,34 @@
 
 def final_kernel(
     flags, acc, edge_x, a1, a2, a3, yr_lo, yr_hi, yr_two,
-    w0, w1, w2, w3, up, up0, out_ref, ey, edge, e1, e2, e3, v3, v2, v1, q1, rows,
+    w0, wf1, wf2, wf3, up, up0, out_hbm, ey, edge, f1, f2, f3, v3, v2, v1, q1, rows, out, sems,
 ):
     x_lo, x_hi, y_lo, y_hi, z_lo, z_hi = (flags[i] for i in range(6))
     y_lo2, y_hi2 = flags[8], flags[9]
     lane = lanes()
 
+    zero = jnp.zeros((32, LANES), BF16)
+    for ref, size in ((f1, 6), (f2, 4), (f3, 3)):
+        for i in range(size + 2):
+            for j in range(2, size):
+                ref[i, j] = zero
+
+    def back(flag, value, shift):
+        return rolled(kept(flag, value).astype(F32), -shift).astype(BF16)
+
     for i in range(5):
-        spread(e3, i, 0, kept(y_lo2, yr_two[...]), -20 * i)
-        spread(e3, i, 1, kept(y_lo, yr_lo[22 + i // 2]), -72 - 20 * (i % 2))
-        spread(e3, i, 3, kept(y_hi, yr_hi[22 + i // 2]), -72 - 20 * (i % 2))
-        spread(e3, i, 4, kept(y_hi2, yr_two[...]), -20 * i)
+        f3[i, 0] = back(y_lo2, yr_two[...], 20 * i)
+        f3[i, 1] = back(y_lo, yr_lo[22 + i // 2], 72 + 20 * (i % 2))
+        f3[i, 3] = back(y_hi, yr_hi[22 + i // 2], 72 + 20 * (i % 2))
+        f3[i, 4] = back(y_hi2, yr_two[...], 20 * i)
     for i in range(6):
         for k in range(2):
-            spread(e2, i, k, kept(y_lo, yr_lo[10 + 2 * i + k]), -72)
-            spread(e2, i, 4 + k, kept(y_hi, yr_hi[10 + 2 * i + k]), -72)
+            f2[i, k] = back(y_lo, yr_lo[10 + 2 * i + k], 72)
+            f2[i, 4 + k] = back(y_hi, yr_hi[10 + 2 * i + k], 72)
     for i in range(8):
         for k in range(2):
-            spread(e1, i, k, kept(y_lo, yr_lo[10 + 2 * i + k]))
-            spread(e1, i, 6 + k, kept(y_hi, yr_hi[10 + 2 * i + k]))
+            f1[i, k] = kept(y_lo, yr_lo[10 + 2 * i + k])
+            f1[i, 6 + k] = kept(y_hi, yr_hi[10 + 2 * i + k])
     for i in range(10):
         sx = (i + 1) % 2
         coarse = (i + 1) // 2 + 1
@@ -413,63 +422,51 @@
         by_x = refined([wide[i] for i in range(count)])
         return [refined([row[j] for j in range(count)]) for row in by_x]
 
-    def level(e_ref, w_ref, own, v_ref, size, cells, above):
+    def level(ref, w_ref, own, v_ref, size, cells, above):
         keep = limits(cells)
-        for j in range(size):
-            dys = [dy for dy in range(3) if not 2 <= j + dy < size]
-            weight = jnp.concatenate(
-                [w_ref[96 * (3 * dx + dy) : 96 * (3 * dx + dy) + 96] for dx in range(3) for dy in dys], axis=0
-            ) if dys else None
-            for i in range(0, size, 2):
-                xs = [i, i + 1] if i + 1 < size else [i]
-                if dys:
-                    value = jnp.concatenate(
-                        [
-                            jnp.concatenate([e_ref[x + dx, j + dy] for x in xs], axis=1)
-                            for dx in range(3)
-                            for dy in dys
-                        ],
-                        axis=0,
-                    )
-                    value = weighted(weight, value)
-                for n, x in enumerate(xs):
-                    part = own[x, j]
-                    if dys:
-                        part = part + value[:, LANES * n : LANES * (n + 1)]
-                    if above is not None:
-                        part = part + above[x][j]
-                    good = keep
-                    for flag in (cell_flag(x, size - 1, x_lo, x_hi), cell_flag(j, size - 1, y_lo, y_hi)):
-                        if flag is not None:
-                            good = good & (flag > 0)
-                    v_ref[x, j] = jnp.where(good, part, 0.0).astype(BF16)
-
-    level(e3, w3, a3, v3, 3, 16, None)
-    level(e2, w2, a2, v2, 4, 32, prolonged(v3, 3))
-    level(e1, w1, a1, v1, 6, 64, prolonged(v2, 4))
+        touched = [j for j in range(size) if j < 2 or j >= size - 2]
+        for x in range(size):
+            value = dot(w_ref[...], around(ref, x, touched))
+            for j in range(size):
+                part = own[x, j]
+                if j in touched:
+                    part = part + shifted(value, touched.index(j))
+                if above is not None:
+                    part = part + above[x][j]
+                good = keep
+                for flag in (cell_flag(x, size - 1, x_lo, x_hi), cell_flag(j, size - 1, y_lo, y_hi)):
+                    if flag is not None:
+                        good = good & (flag > 0)
+                v_ref[x, j] = jnp.where(good, part, 0.0).astype(BF16)
+
+    level(f3, wf3, a3, v3, 3, 16, None)
+    level(f2, wf2, a2, v2, 4, 32, prolonged(v3, 3))
+    level(f1, wf1, a1, v1, 6, 64, prolonged(v2, 4))
     for i in range(6):
         q1[i] = dot(v1[i].reshape(6 * 32, LANES), up0[...]).reshape(6, 32, LANES)
 
-    def fine(c, side):
-        for part in range(2):
-            x = 2 * c + part
-            row = 0.75 * q1[c + 1] + 0.25 * q1[c + 2 * part]
-            for y in range(0, 8, 2):
-                centre = y // 2 + 1
-                for n, extra in enumerate(along(row[centre - 1], row[centre], row[centre + 1])):
-                    total = acc[x, y + n] + extra
-                    if y + n == 0:
-                        total = total + edge[0, x]
-                    if y + n == 7:
-                        total = total + edge[1, x]
-                    if side == part:
-                        total = total + edge_x[side, y + n]
-                    rows[pl.ds(x * 8 + y + n, 32, stride=64), :] = jax.nn.gelu(total, approximate=True)
-
-    fine(0, 0)
-    lax.fori_loop(1, 3, lambda c, carry: (fine(c, -1), carry)[1], 0)
-    fine(3, 1)
-    out_ref[...] = rows[...].reshape(32, 8, 8, LANES).astype(BF16)
+    copies = []
+    for x in range(8):
+        c, part = x // 2, x % 2
+        row = 0.75 * q1[c + 1] + 0.25 * q1[c + 2 * part]
+        for y in range(0, 8, 2):
+            centre = y // 2 + 1
+            for n, extra in enumerate(along(row[centre - 1], row[centre], row[centre + 1])):
+                total = acc[x, y + n] + extra
+                if y + n == 0:
+                    total = total + edge[0, x]
+                if y + n == 7:
+                    total = total + edge[1, x]
+                if x == 0:
+                    total = total + edge_x[0, y + n]
+                if x == 7:
+                    total = total + edge_x[1, y + n]
+                rows[x, pl.ds(y + n, 32, stride=8), :] = jax.nn.gelu(total, approximate=True)
+        out[x] = rows[x].reshape(32, 8, LANES).astype(BF16)
+        copies.append(pltpu.make_async_copy(out.at[x], out_hbm.at[:, x], sems.at[x]))
+        copies[-1].start()
+    for copy in copies:
+        copy.wait()
 
 
 def turned(value, axis, step):
@@ -547,19 +544,22 @@
     (out,) = call(
         final_kernel,
         [(32, 8, 8, LANES)],
-        [flags, acc, edge_x, a1, a2, a3, yr_lo, yr_hi, yr_two, *flat, up, up0],
+        [flags, acc, edge_x, a1, a2, a3, yr_lo, yr_hi, yr_two, flat[0], *wf[1:], up, up0],
         [
             pltpu.VMEM((2, 10, 96, LANES), BF16),
             pltpu.VMEM((2, 8) + tile, F32),
-            pltpu.VMEM((8, 8, 96, LANES), BF16),
-            pltpu.VMEM((6, 6, 96, LANES), BF16),
-            pltpu.VMEM((5, 5, 96, LANES), BF16),
+            pltpu.VMEM((8, 8) + tile, BF16),
+            pltpu.VMEM((6, 6) + tile, BF16),
+            pltpu.VMEM((5, 5) + tile, BF16),
             pltpu.VMEM((3, 3) + tile, BF16),
             pltpu.VMEM((4, 4) + tile, BF16),
             pltpu.VMEM((6, 6) + tile, BF16),
             pltpu.VMEM((6, 6) + tile, F32),
-            pltpu.VMEM((2048, LANES), F32),
+            pltpu.VMEM((8, 256, LANES), F32),
+            pltpu.VMEM((8, 32, 8, LANES), BF16),
+            pltpu.SemaphoreType.DMA((8,)),
         ],
+        out_space=pl.ANY,
     )
     return out
 

time: 37.5 us -> 36.9 us (0.984)
  Pallas kernels: 12.2 us -> 11.4 us
    pallas_call x8, Pallas kernels: 12.2 us -> 11.4 us  [call(): pl.pallas_call(kernel, out_shape=[jax.ShapeDtypeStruct(shape, kind) for s...]
where the time goes in v5:
time: 36.9 us; the launch traced here: 36.7 us
  starting transfers between devices  15.6 us (42%)
  Pallas kernels  11.4 us (31%)
  waiting for transfers between devices  8.11 us (22%)
  local copies, waits for them, and re-layouts  1.37 us (4%)
    ppermute x9, starting transfers between devices, turned(): lax.ppermute(value, axis, [(i, (i + step) % count) for i in range(count)])  15.6 us
    pallas_call x8, Pallas kernels, call(): pl.pallas_call(kernel, out_shape=[jax.ShapeDtypeStruct(shape, kind) for s...  11.4 us
    ppermute x9, waiting for transfers between devices, turned(): lax.ppermute(value, axis, [(i, (i + step) % count) for i in range(count)])  8.11 us
    unnamed x16, local copies, waits for them, and re-layouts  1.36 us
  transfers between devices with their start and end apart: 9, of which 3 were waited for; matrix products, arithmetic and copies ran while one was open for 0% of the time, Pallas kernels for 12%

profile of v5, /device:TPU:8, one launch (start us, length us, event | category | flops | bytes accessed | tf_op | source)
XLA Modules:
  0.0 36.7 jit_solution(5008322615595568804)
XLA Ops:
  0.0 0.3 shard_map.82.table
  0.3 0.7 %copy-done = bf16[32,8,8,128]{3,2,1,0:T(8,128)(2,1)S(1)} copy-done((bf16[32,8,8,128]{3,2,1,0:T(8,128)(2,1)S(1)}, bf16[32,8,8,128]{3,2,1,0:T(8,128)(2,1)}, u32[]{:S(2)}) %copy-start) | copy-done | bytes 524312
  1.1 1.2 %shard_map.83 = (bf16[8,8,32,128]{3,2,1,0:T(8,128)(2,1)S(1)}, bf16[4,4,32,128]{3,2,1,0:T(8,128)(2,1)S(1)}, bf16[2,2,32,128]{3,2,1,0:T(8,128)(2,1)S(1)}, bf16[32,...) custom-call(bf16[32,8,8,128]{3,2,1,0:T(8,128)(2,1)S(1)} %copy-done, bf16[512,640]{1,0:T(8,128)(2,1)S(1)} %shard_map.82.table), custom_call_target="tpu_custom_call" | custom-call | flops 1048576 | bytes 1048576 | tf_op jit(solution)/shard_map/pallas_call | solution.py:79
  2.3 2.2 %collective-permute-start.1 = (bf16[32,128]{1,0:T(8,128)(2,1)S(1)}, bf16[32,128]{1,0:T(8,128)(2,1)S(1)}, u32[]{:S(2)}, u32[]{:S(2)}) collective-permute-start(bf16[32,128]{1,0:T(8,128)(2,1)S(1)} %get-tuple-element.73), channel_id=1, source_target_pairs={{0,7},{1,0},{2,1},{3,2},{4,3},{5,4},{6,5},{7,6},{8,15},{9,8},{10,9... | collective-permute-start | bytes 24584 | tf_op jit(solution)/shard_map/ppermute | solution.py:474
  4.5 0.0 collective-permute-start
  4.5 0.0 copy-done.1
  4.5 0.0 copy-done.4
  4.6 0.0 copy-done.5
  4.6 0.0 copy-done.6
  4.6 0.6 %copy-done.7 = bf16[32,32]{1,0:T(8,128)(2,1)S(1)} copy-done((bf16[32,32]{1,0:T(8,128)(2,1)S(1)}, bf16[32,32]{1,0:T(8,128)(2,1)}, u32[]{:S(2)}) %copy-start.7) | copy-done | bytes 2072
  5.2 0.6 %shard_map.84 = (bf16[96,320]{1,0:T(8,128)(2,1)S(1)}, bf16[96,288]{1,0:T(8,128)(2,1)S(1)}, bf16[96,288]{1,0:T(8,128)(2,1)S(1)}, bf16[96,288]{1,0:T(8,128)(2,1)S(1)}) custom-call(bf16[864,32]{1,0:T(8,128)(2,1)S(1)} %bitcast.8, bf16[864,32]{1,0:T(8,128)(2,1)S(1)} %bitcast.12, bf16[864,32]{1,0:T(8,128)(2,1)S(1)} %bitcast.13, bf16[864,32]{1,0:T(8,128)(2,1)S(1)} %bitcast.14, ...), custom_call_target="tpu_custom_call" | custom-call | flops 268435456 | bytes 1048576 | tf_op jit(solution)/shard_map/pallas_call | solution.py:79
  5.8 3.0 %collective-permute-done.from_lo = bf16[32,128]{1,0:T(8,128)(2,1)S(1)} collective-permute-done((bf16[32,128]{1,0:T(8,128)(2,1)S(1)}, bf16[32,128]{1,0:T(8,128)(2,1)S(1)}, u32[]{:S(2)}, u32[]{:S(2)}) %collective-permute-start) | collective-permute-done | bytes 8224 | tf_op jit(solution)/shard_map/ppermute | solution.py:474
  8.8 0.0 collective-permute-done.1.from_hi
  8.8 0.7 %shard_map.85 = (bf16[4,4,32,128]{3,2,1,0:T(8,128)(2,1)S(1)}, bf16[2,2,32,128]{3,2,1,0:T(8,128)(2,1)S(1)}, bf16[32,128]{1,0:T(8,128)(2,1)S(1)}, bf16[16,32,128]{2,1,0:T(8,128)(2,1)S(1)}, bf16[16,32,128]{2,1,0:T(8,128)(2,1)S(1)}) custom-call(s32[16]{0:T(128)S(1)} %select_convert_fusion.flags, bf16[8,8,32,128]{3,2,1,0:T(8,128)(2,1)S(1)} %get-tuple-element.39.x_ref, ...), custom_call_target="tpu_custom_call" | custom-call | flops 1048576 | bytes 1048576 | tf_op jit(solution)/shard_map/pallas_call | solution.py:79
  9.5 2.0 %collective-permute-start.2 = (bf16[16,32,128]{2,1,0:T(8,128)(2,1)S(1)}, bf16[16,32,128]{2,1,0:T(8,128)(2,1)S(1)}, u32[]{:S(2)}, u32[]{:S(2)}) collective-permute-start(bf16[16,32,128]{2,1,0:T(8,128)(2,1)S(1)} %get-tuple-element.55), channel_id=1, source_target_pairs={{0,32},{32,64},{64,96},{96,128},{128,160},{160,192},{192,224},{224... | collective-permute-start | bytes 393224 | tf_op jit(solution)/shard_map/ppermute | solution.py:474
  11.5 4.0 %collective-permute-start.3 = (bf16[16,32,128]{2,1,0:T(8,128)(2,1)S(1)}, bf16[16,32,128]{2,1,0:T(8,128)(2,1)S(1)}, u32[]{:S(2)}, u32[]{:S(2)}) collective-permute-start(bf16[16,32,128]{2,1,0:T(8,128)(2,1)S(1)} %get-tuple-element.62), channel_id=1, source_target_pairs={{0,224},{32,0},{64,32},{96,64},{128,96},{160,128},{192,160},{224,1... | collective-permute-start | bytes 393224 | tf_op jit(solution)/shard_map/ppermute | solution.py:474
  15.6 2.4 %collective-permute-start.5 = (bf16[32,128]{1,0:T(8,128)(2,1)S(1)}, bf16[32,128]{1,0:T(8,128)(2,1)S(1)}, u32[]{:S(2)}, u32[]{:S(2)}) collective-permute-start(bf16[32,128]{1,0:T(8,128)(2,1)S(1)} %get-tuple-element.60.t3), channel_id=1, source_target_pairs={{0,192},{32,224},{64,0},{96,32},{128,64},{160,96},{192,128},{224,1... | collective-permute-start | bytes 24584 | tf_op jit(solution)/shard_map/ppermute | solution.py:474
  17.9 0.5 %collective-permute-start.4 = (bf16[32,128]{1,0:T(8,128)(2,1)S(1)}, bf16[32,128]{1,0:T(8,128)(2,1)S(1)}, u32[]{:S(2)}, u32[]{:S(2)}) collective-permute-start(bf16[32,128]{1,0:T(8,128)(2,1)S(1)} %get-tuple-element.60.t3), channel_id=1, source_target_pairs={{0,64},{32,96},{64,128},{96,160},{128,192},{160,224},{192,0},{224,... | collective-permute-start | bytes 24584 | tf_op jit(solution)/shard_map/ppermute | solution.py:474
  18.5 1.7 %shard_map.86.acc = f32[8,8,32,128]{3,2,1,0:T(8,128)S(1)} custom-call(bf16[8,8,32,128]{3,2,1,0:T(8,128)(2,1)S(1)} %get-tuple-element.39.x_ref, bf16[4,4,32,128]{3,2,1,0:T(8,128)(2,1)S(1)} %get-tuple-element.56.t1, bf16[864,32]{1,0:T(8,128)(2,1)S(1)} %bitcast.9, bf16[96,320]{1,0:T(8,128)(2,1)S(1)} %get-tuple-element.57.wf), custom_call_target="tpu_custom_call" | custom-call | flops 1073741824 | bytes 1048576 | tf_op jit(solution)/shard_map/pallas_call | solution.py:79
  20.2 0.0 collective-permute-done.2.xr_lo
  20.2 0.0 collective-permute-done.5.xr_hi2
  20.2 3.5 %collective-permute-done.4.xr_lo2 = bf16[32,128]{1,0:T(8,128)(2,1)S(1)} collective-permute-done((bf16[32,128]{1,0:T(8,128)(2,1)S(1)}, bf16[32,128]{1,0:T(8,128)(2,1)S(1)}, u32[]{:S(2)}, u32[]{:S(2)}) %collective-permute-start.4) | collective-permute-done | bytes 8224 | tf_op jit(solution)/shard_map/ppermute | solution.py:474
  23.7 0.0 collective-permute-done.3.xr_hi
  23.7 0.8 %shard_map.88 = (bf16[26,32,128]{2,1,0:T(8,128)(2,1)S(1)}, bf16[26,32,128]{2,1,0:T(8,128)(2,1)S(1)}, bf16[32,128]{1,0:T(8,128)(2,1)S(1)}) custom-call(s32[16]{0:T(128)S(1)} %select_convert_fusion.flags, bf16[8,8,32,128]{3,2,1,0:T(8,128)(2,1)S(1)} %get-tuple-element.39.x_ref, bf16[4,4,32,128]{3,2,1,0:T(8,128)(2,1)S(1)} %get-tuple-element.56.t1, ...), custom_call_target="tpu_custom_call" | custom-call | flops 1048576 | bytes 1048576 | tf_op jit(solution)/shard_map/pallas_call | solution.py:79
  24.5 1.7 %collective-permute-start.6 = (bf16[26,32,128]{2,1,0:T(8,128)(2,1)S(1)}, bf16[26,32,128]{2,1,0:T(8,128)(2,1)S(1)}, u32[]{:S(2)}, u32[]{:S(2)}) collective-permute-start(bf16[26,32,128]{2,1,0:T(8,128)(2,1)S(1)} %get-tuple-element.70), channel_id=1, source_target_pairs={{0,8},{8,16},{16,24},{24,0},{1,9},{9,17},{17,25},{25,1},{2,10},{10... | collective-permute-start | bytes 638984 | tf_op jit(solution)/shard_map/ppermute | solution.py:474
  26.2 0.5 %collective-permute-start.7 = (bf16[26,32,128]{2,1,0:T(8,128)(2,1)S(1)}, bf16[26,32,128]{2,1,0:T(8,128)(2,1)S(1)}, u32[]{:S(2)}, u32[]{:S(2)}) collective-permute-start(bf16[26,32,128]{2,1,0:T(8,128)(2,1)S(1)} %get-tuple-element.71), channel_id=1, source_target_pairs={{0,24},{8,0},{16,8},{24,16},{1,25},{9,1},{17,9},{25,17},{2,26},{10... | collective-permute-start | bytes 638984 | tf_op jit(solution)/shard_map/ppermute | solution.py:474
  26.6 2.3 %collective-permute-start.8 = (bf16[32,128]{1,0:T(8,128)(2,1)S(1)}, bf16[32,128]{1,0:T(8,128)(2,1)S(1)}, u32[]{:S(2)}, u32[]{:S(2)}) collective-permute-start(bf16[32,128]{1,0:T(8,128)(2,1)S(1)} %get-tuple-element.72), channel_id=1, source_target_pairs={{0,16},{8,24},{16,0},{24,8},{1,17},{9,25},{17,1},{25,9},{2,18},{10... | collective-permute-start | bytes 24584 | tf_op jit(solution)/shard_map/ppermute | solution.py:474
  28.9 2.3 %shard_map.87 = (f32[2,8,32,128]{3,2,1,0:T(8,128)S(1)}, f32[6,6,32,128]{3,2,1,0:T(8,128)S(1)}, f32[4,4,32,128]{3,2,1,0:T(8,128)S(1)}, f32[3,3,32,128]{3,2,1,0:T(8,128)S(1)}) custom-call(s32[16]{0:T(128)S(1)} %select_convert_fusion.flags, bf16[4,4,32,128]{3,2,1,0:T(8,128)(2,1)S(1)} %get-tuple-element.56.t1, bf16[2,2,32,128]{3,2,1,0:T(8,128)(2,1)S(1)} %get-tuple-element.59.t2, ...), custom_call_target="tpu_custom_call" | custom-call | flops 1073741824 | bytes 1048576 | tf_op jit(solution)/shard_map/pallas_call | solution.py:79
  31.2 1.6 %collective-permute-done.8.yr_two = bf16[32,128]{1,0:T(8,128)(2,1)S(1)} collective-permute-done((bf16[32,128]{1,0:T(8,128)(2,1)S(1)}, bf16[32,128]{1,0:T(8,128)(2,1)S(1)}, u32[]{:S(2)}, u32[]{:S(2)}) %collective-permute-start.8) | collective-permute-done | bytes 8224 | tf_op jit(solution)/shard_map/ppermute | solution.py:474
  32.8 0.0 collective-permute-done.6.yr_lo
  32.8 0.0 collective-permute-done.7.yr_hi
  32.8 3.7 %shard_map.89 = bf16[32,8,8,128]{3,2,1,0:T(8,128)(2,1)} custom-call(s32[16]{0:T(128)S(1)} %select_convert_fusion.flags, f32[8,8,32,128]{3,2,1,0:T(8,128)S(1)} %shard_map.86.acc, f32[2,8,32,128]{3,2,1,0:T(8,128)S(1)} %get-tuple-element.66.edge_x, f32[6,6,32,128]{3,2,1,0:T(8,128)S(1)} %get-tuple-element.67.a1, f32[4,4,32,128]{3,2,1,0:T(8,128)S(1)} %get-tuple-element.68.a2, ...), custom_call_target="tpu_custom_call" | custom-call | flops 1048576 | bytes 1048576 | tf_op jit(solution)/shard_map/pallas_call | solution.py:79
  (12 shorter events, 0.0 us)
Async XLA Ops:
  0.0 1.0 %copy-start = (bf16[32,8,8,128]{3,2,1,0:T(8,128)(2,1)S(1)}, bf16[32,8,8,128]{3,2,1,0:T(8,128)(2,1)}, u32[]{:S(2)}) copy-start(bf16[32,8,8,128]{3,2,1,0:T(8,128)(2,1)} %field.1) | copy-start | bytes 1572868
  1.0 3.5 %copy-start.1 = (bf16[3,3,3,32,32]{4,3,2,1,0:T(8,128)(2,1)S(1)}, bf16[3,3,3,32,32]{4,3,2,1,0:T(8,128)(2,1)}, u32[]{:S(2)}) copy-start(bf16[3,3,3,32,32]{4,3,2,1,0:T(8,128)(2,1)} %param.10) | copy-start | bytes 165892
  1.0 3.5 %copy-start.4 = (bf16[3,3,3,32,32]{4,3,2,1,0:T(8,128)(2,1)S(1)}, bf16[3,3,3,32,32]{4,3,2,1,0:T(8,128)(2,1)}, u32[]{:S(2)}) copy-start(bf16[3,3,3,32,32]{4,3,2,1,0:T(8,128)(2,1)} %param.11) | copy-start | bytes 165892
  1.0 3.5 %copy-start.5 = (bf16[3,3,3,32,32]{4,3,2,1,0:T(8,128)(2,1)S(1)}, bf16[3,3,3,32,32]{4,3,2,1,0:T(8,128)(2,1)}, u32[]{:S(2)}) copy-start(bf16[3,3,3,32,32]{4,3,2,1,0:T(8,128)(2,1)} %param.12) | copy-start | bytes 165892
  1.0 3.5 %copy-start.6 = (bf16[3,3,3,32,32]{4,3,2,1,0:T(8,128)(2,1)S(1)}, bf16[3,3,3,32,32]{4,3,2,1,0:T(8,128)(2,1)}, u32[]{:S(2)}) copy-start(bf16[3,3,3,32,32]{4,3,2,1,0:T(8,128)(2,1)} %param.13) | copy-start | bytes 165892
  2.3 6.5 %collective-permute-start.1 = (bf16[32,128]{1,0:T(8,128)(2,1)S(1)}, bf16[32,128]{1,0:T(8,128)(2,1)S(1)}, u32[]{:S(2)}, u32[]{:S(2)}) collective-permute-start(bf16[32,128]{1,0:T(8,128)(2,1)S(1)} %get-tuple-element.73), channel_id=1, source_target_pairs={{0,7},{1,0},{2,1},{3,2},{4,3},{5,4},{6,5},{7,6},{8,15},{9,8},{10,9... | collective-permute-start | bytes 24584 | tf_op jit(solution)/shard_map/ppermute | solution.py:474
  4.5 4.3 %collective-permute-start = (bf16[32,128]{1,0:T(8,128)(2,1)S(1)}, bf16[32,128]{1,0:T(8,128)(2,1)S(1)}, u32[]{:S(2)}, u32[]{:S(2)}) collective-permute-start(bf16[32,128]{1,0:T(8,128)(2,1)S(1)} %get-tuple-element.74), channel_id=1, source_target_pairs={{0,1},{1,2},{2,3},{3,4},{4,5},{5,6},{6,7},{7,0},{8,9},{9,10},{10,1... | collective-permute-start | bytes 24584 | tf_op jit(solution)/shard_map/ppermute | solution.py:474
  4.5 0.7 %copy-start.7 = (bf16[32,32]{1,0:T(8,128)(2,1)S(1)}, bf16[32,32]{1,0:T(8,128)(2,1)}, u32[]{:S(2)}) copy-start(bf16[32,32]{1,0:T(8,128)(2,1)} %mix) | copy-start | bytes 6148
  9.5 10.6 %collective-permute-start.2 = (bf16[16,32,128]{2,1,0:T(8,128)(2,1)S(1)}, bf16[16,32,128]{2,1,0:T(8,128)(2,1)S(1)}, u32[]{:S(2)}, u32[]{:S(2)}) collective-permute-start(bf16[16,32,128]{2,1,0:T(8,128)(2,1)S(1)} %get-tuple-element.55), channel_id=1, source_target_pairs={{0,32},{32,64},{64,96},{96,128},{128,160},{160,192},{192,224},{224... | collective-permute-start | bytes 393224 | tf_op jit(solution)/shard_map/ppermute | solution.py:474
  11.5 12.2 %collective-permute-start.3 = (bf16[16,32,128]{2,1,0:T(8,128)(2,1)S(1)}, bf16[16,32,128]{2,1,0:T(8,128)(2,1)S(1)}, u32[]{:S(2)}, u32[]{:S(2)}) collective-permute-start(bf16[16,32,128]{2,1,0:T(8,128)(2,1)S(1)} %get-tuple-element.62), channel_id=1, source_target_pairs={{0,224},{32,0},{64,32},{96,64},{128,96},{160,128},{192,160},{224,1... | collective-permute-start | bytes 393224 | tf_op jit(solution)/shard_map/ppermute | solution.py:474
  15.6 4.6 %collective-permute-start.5 = (bf16[32,128]{1,0:T(8,128)(2,1)S(1)}, bf16[32,128]{1,0:T(8,128)(2,1)S(1)}, u32[]{:S(2)}, u32[]{:S(2)}) collective-permute-start(bf16[32,128]{1,0:T(8,128)(2,1)S(1)} %get-tuple-element.60.t3), channel_id=1, source_target_pairs={{0,192},{32,224},{64,0},{96,32},{128,64},{160,96},{192,128},{224,1... | collective-permute-start | bytes 24584 | tf_op jit(solution)/shard_map/ppermute | solution.py:474
  17.9 5.8 %collective-permute-start.4 = (bf16[32,128]{1,0:T(8,128)(2,1)S(1)}, bf16[32,128]{1,0:T(8,128)(2,1)S(1)}, u32[]{:S(2)}, u32[]{:S(2)}) collective-permute-start(bf16[32,128]{1,0:T(8,128)(2,1)S(1)} %get-tuple-element.60.t3), channel_id=1, source_target_pairs={{0,64},{32,96},{64,128},{96,160},{128,192},{160,224},{192,0},{224,... | collective-permute-start | bytes 24584 | tf_op jit(solution)/shard_map/ppermute | solution.py:474
  24.5 8.3 %collective-permute-start.6 = (bf16[26,32,128]{2,1,0:T(8,128)(2,1)S(1)}, bf16[26,32,128]{2,1,0:T(8,128)(2,1)S(1)}, u32[]{:S(2)}, u32[]{:S(2)}) collective-permute-start(bf16[26,32,128]{2,1,0:T(8,128)(2,1)S(1)} %get-tuple-element.70), channel_id=1, source_target_pairs={{0,8},{8,16},{16,24},{24,0},{1,9},{9,17},{17,25},{25,1},{2,10},{10... | collective-permute-start | bytes 638984 | tf_op jit(solution)/shard_map/ppermute | solution.py:474
  26.2 6.7 %collective-permute-start.7 = (bf16[26,32,128]{2,1,0:T(8,128)(2,1)S(1)}, bf16[26,32,128]{2,1,0:T(8,128)(2,1)S(1)}, u32[]{:S(2)}, u32[]{:S(2)}) collective-permute-start(bf16[26,32,128]{2,1,0:T(8,128)(2,1)S(1)} %get-tuple-element.71), channel_id=1, source_target_pairs={{0,24},{8,0},{16,8},{24,16},{1,25},{9,1},{17,9},{25,17},{2,26},{10... | collective-permute-start | bytes 638984 | tf_op jit(solution)/shard_map/ppermute | solution.py:474
  26.6 6.2 %copy-start.2 = (bf16[128,128]{1,0:T(8,128)(2,1)S(1)}, bf16[128,128]{1,0:T(8,128)(2,1)}, u32[]{:S(2)}) copy-start(bf16[128,128]{1,0:T(8,128)(2,1)} %constant.36.clone.up0) | copy-start | bytes 98308
  26.6 6.2 %copy-start.3 = (bf16[128,128]{1,0:T(8,128)(2,1)S(1)}, bf16[128,128]{1,0:T(8,128)(2,1)}, u32[]{:S(2)}) copy-start(bf16[128,128]{1,0:T(8,128)(2,1)} %constant.35.clone.up) | copy-start | bytes 98308
  26.6 6.2 %collective-permute-start.8 = (bf16[32,128]{1,0:T(8,128)(2,1)S(1)}, bf16[32,128]{1,0:T(8,128)(2,1)S(1)}, u32[]{:S(2)}, u32[]{:S(2)}) collective-permute-start(bf16[32,128]{1,0:T(8,128)(2,1)S(1)} %get-tuple-element.72), channel_id=1, source_target_pairs={{0,16},{8,24},{16,0},{24,8},{1,17},{9,25},{17,1},{25,9},{2,18},{10... | collective-permute-start | bytes 24584 | tf_op jit(solution)/shard_map/ppermute | solution.py:474

commit v6 on v5

--- a/solution.py
+++ b/solution.py
@@ -73,9 +73,8 @@
     return jnp.dot(a, b, preferred_element_type=F32)
 
 
-def call(kernel, outs, args, scratch=(), scalars=1, kind=BF16, flops=1 << 20, out_space=pltpu.VMEM):
-    specs = [pl.BlockSpec(memory_space=pltpu.SMEM)] * scalars
-    specs += [pl.BlockSpec(memory_space=pltpu.VMEM)] * (len(args) - scalars)
+def call(kernel, outs, args, scratch=(), kind=BF16, flops=1 << 20, out_space=pltpu.VMEM):
+    specs = [pl.BlockSpec(memory_space=pltpu.VMEM)] * len(args)
     return pl.pallas_call(
         kernel,
         out_shape=[jax.ShapeDtypeStruct(shape, kind) for shape in outs],
@@ -122,8 +121,8 @@
 
 def depth_kernel(flags, x_ref, t1, t2, t3, from_lo, from_hi, t1_out, t2_out, t3_out, lo_out, hi_out):
     lane = lanes()
-    low = jnp.where(flags[4] > 0, from_lo[...].astype(F32), 0.0)
-    high = jnp.where(flags[5] > 0, from_hi[...].astype(F32), 0.0)
+    low = from_lo[...].astype(F32) * flags[4:5]
+    high = from_hi[...].astype(F32) * flags[5:6]
 
     def joined(own, mask_lo, shift_lo, mask_hi, shift_hi):
         value = own.astype(F32)
@@ -159,11 +158,11 @@
 
 
 def kept(flag, value):
-    return jnp.where(flag > 0, value, jnp.zeros_like(value))
+    return value * jnp.broadcast_to(flag, value.shape).astype(BF16)
 
 
 def width_kernel(flags, x_ref, t1, t2, t3, xr_lo, xr_hi, xr_lo2, xr_hi2, lo_out, hi_out, two_out):
-    has_lo, has_hi, has_lo2, has_hi2 = flags[0], flags[1], flags[6], flags[7]
+    has_lo, has_hi, has_lo2, has_hi2 = flags[0:1], flags[1:2], flags[6:7], flags[7:8]
     lane = lanes()
     free = (lane >= 72) & (lane < 124)
     row = [
@@ -298,7 +297,7 @@
     flags, t1, t2, t3, xr_lo, xr_hi, xr_lo2, xr_hi2, w0, wf1, wf2, wf3,
     edge_out, a1_out, a2_out, a3_out, ex, f1, f2, f3,
 ):
-    x_lo, x_hi, x_lo2, x_hi2 = flags[0], flags[1], flags[6], flags[7]
+    x_lo, x_hi, x_lo2, x_hi2 = flags[0:1], flags[1:2], flags[6:7], flags[7:8]
     zero = jnp.zeros((32, LANES), BF16)
     for ref, size in ((f1, 6), (f2, 4), (f3, 3)):
         for i in range(size + 2):
@@ -354,8 +353,8 @@
     flags, acc, edge_x, a1, a2, a3, yr_lo, yr_hi, yr_two,
     w0, wf1, wf2, wf3, up, up0, out_hbm, ey, edge, f1, f2, f3, v3, v2, v1, q1, rows, out, sems,
 ):
-    x_lo, x_hi, y_lo, y_hi, z_lo, z_hi = (flags[i] for i in range(6))
-    y_lo2, y_hi2 = flags[8], flags[9]
+    x_lo, x_hi, y_lo, y_hi, z_lo, z_hi = (flags[i : i + 1] for i in range(6))
+    y_lo2, y_hi2 = flags[8:9], flags[9:10]
     lane = lanes()
 
     zero = jnp.zeros((32, LANES), BF16)
@@ -400,9 +399,9 @@
         return [0.75 * centre + 0.25 * before, 0.75 * centre + 0.25 * after]
 
     def limits(count):
-        inside = (lane >= 1) & (lane <= count + 2)
-        inside &= (lane != 1) | (z_lo > 0)
-        return inside & ((lane != count + 2) | (z_hi > 0))
+        spot = lax.broadcasted_iota(jnp.int32, (1, LANES), 1)
+        inside = jnp.where((spot >= 1) & (spot <= count + 2), 1.0, 0.0)
+        return jnp.where(spot == 1, z_lo, jnp.where(spot == count + 2, z_hi, inside))
 
     def cell_flag(position, last, lo, hi):
         return lo if position == 0 else hi if position == last else None
@@ -436,8 +435,8 @@
                 good = keep
                 for flag in (cell_flag(x, size - 1, x_lo, x_hi), cell_flag(j, size - 1, y_lo, y_hi)):
                     if flag is not None:
-                        good = good & (flag > 0)
-                v_ref[x, j] = jnp.where(good, part, 0.0).astype(BF16)
+                        good = good * flag
+                v_ref[x, j] = (part * good).astype(BF16)
 
     level(f3, wf3, a3, v3, 3, 16, None)
     level(f2, wf2, a2, v2, 4, 32, prolonged(v3, 3))
@@ -477,26 +476,25 @@
 def on_device(field, mixing, kernel_fine, kernel_half, kernel_quarter, kernel_eighth):
     gx, gy, gz = (lax.axis_index(a) for a in ("gx", "gy", "gz"))
     nx, ny, nz = (lax.axis_size(a) for a in ("gx", "gy", "gz"))
-    slot = lax.iota(jnp.int32, 16)
+    slot = lax.broadcasted_iota(jnp.int32, (16, LANES), 0)
     place = jnp.where((slot < 2) | (slot == 6) | (slot == 7), gx, jnp.where((slot == 4) | (slot == 5), gz, gy))
     side = slot & 1
     width = jnp.where(slot < 6, 1, 2)
     count = jnp.where((slot < 2) | (slot == 6) | (slot == 7), nx, jnp.where((slot == 4) | (slot == 5), nz, ny))
-    flags = jnp.where(side == 0, place >= width, place < count - width).astype(jnp.int32)
+    flags = jnp.where(side == 0, place >= width, place < count - width).astype(F32)
     up, up0 = (jnp.asarray(m) for m in tables())
     tile = (32, LANES)
 
-    (table,) = call(restrictions, [(512, 640)], [], scalars=0, flops=1 << 26)
+    (table,) = call(restrictions, [(512, 640)], [], flops=1 << 26)
     x_own, t1, t2, t3, msg = call(
         restrict_kernel,
         [(8, 8) + tile, (4, 4) + tile, (2, 2) + tile, tile, (2,) + tile],
         [field, table],
         [pltpu.VMEM((2048, LANES), F32)],
-        0,
     )
     flat = [k.reshape(864, 32) for k in (kernel_fine, kernel_half, kernel_quarter, kernel_eighth)]
     mixing, *flat, t3 = lax.optimization_barrier((mixing, *flat, t3))
-    wf = call(weights_kernel, [(96, 320)] + [(96, 288)] * 3, [*flat, mixing], scalars=0, flops=1 << 28)
+    wf = call(weights_kernel, [(96, 320)] + [(96, 288)] * 3, [*flat, mixing], flops=1 << 28)
     from_hi = turned(msg[0], "gz", -1)
     from_lo = turned(msg[1], "gz", 1)
     from_lo, *wf = lax.optimization_barrier((from_lo, *wf))
@@ -514,7 +512,6 @@
         [(8, 8) + tile],
         [x_own, t1, flat[0], wf[0]],
         [pltpu.VMEM((10, 10) + tile, BF16)],
-        0,
         kind=F32,
         flops=1 << 30,
     )

time: 36.9 us -> 35.2 us (0.954)
  Pallas kernels: 11.4 us -> 9.04 us
  waiting for transfers between devices: 8.11 us -> 8.74 us
    pallas_call x8, Pallas kernels: 11.4 us -> 9.04 us  [call(): pl.pallas_call(kernel, out_shape=[jax.ShapeDtypeStruct(shape, kind) for s...]
    ppermute x9, waiting for transfers between devices: 8.11 us -> 8.74 us  [turned(): lax.ppermute(value, axis, [(i, (i + step) % count) for i in range(count)])]
  transfers between devices with their start and end apart: 9 -> 9, of which waited for: 3 -> 3; matrix products, arithmetic and copies ran while one was open for 0% -> 0% of each run, Pallas kernels for 12% -> 11%
where the time goes in v6:
time: 35.2 us; the launch traced here: 35 us
  starting transfers between devices  15.6 us (44%)
  Pallas kernels  9.04 us (26%)
  waiting for transfers between devices  8.74 us (25%)
  local copies, waits for them, and re-layouts  1.29 us (4%)
    ppermute x9, starting transfers between devices, turned(): lax.ppermute(value, axis, [(i, (i + step) % count) for i in range(count)])  15.6 us
    pallas_call x8, Pallas kernels, call(): pl.pallas_call(kernel, out_shape=[jax.ShapeDtypeStruct(shape, kind) for s...  9.04 us
    ppermute x9, waiting for transfers between devices, turned(): lax.ppermute(value, axis, [(i, (i + step) % count) for i in range(count)])  8.74 us
    unnamed x16, local copies, waits for them, and re-layouts  1.28 us
  transfers between devices with their start and end apart: 9, of which 3 were waited for; matrix products, arithmetic and copies ran while one was open for 0% of the time, Pallas kernels for 11%

profile of v6, /device:TPU:8, one launch (start us, length us, event | category | flops | bytes accessed | tf_op | source)
XLA Modules:
  0.0 35.0 jit_solution(5301049752147922993)
XLA Ops:
  0.0 0.3 shard_map.82.table
  0.3 0.7 %copy-done = bf16[32,8,8,128]{3,2,1,0:T(8,128)(2,1)S(1)} copy-done((bf16[32,8,8,128]{3,2,1,0:T(8,128)(2,1)S(1)}, bf16[32,8,8,128]{3,2,1,0:T(8,128)(2,1)}, u32[]{:S(2)}) %copy-start) | copy-done | bytes 524312
  1.1 1.2 %shard_map.83 = (bf16[8,8,32,128]{3,2,1,0:T(8,128)(2,1)S(1)}, bf16[4,4,32,128]{3,2,1,0:T(8,128)(2,1)S(1)}, bf16[2,2,32,128]{3,2,1,0:T(8,128)(2,1)S(1)}, bf16[32,...) custom-call(bf16[32,8,8,128]{3,2,1,0:T(8,128)(2,1)S(1)} %copy-done, bf16[512,640]{1,0:T(8,128)(2,1)S(1)} %shard_map.82.table), custom_call_target="tpu_custom_call" | custom-call | flops 1048576 | bytes 1048576 | tf_op jit(solution)/shard_map/pallas_call | solution.py:78
  2.3 2.2 %collective-permute-start.1 = (bf16[32,128]{1,0:T(8,128)(2,1)S(1)}, bf16[32,128]{1,0:T(8,128)(2,1)S(1)}, u32[]{:S(2)}, u32[]{:S(2)}) collective-permute-start(bf16[32,128]{1,0:T(8,128)(2,1)S(1)} %get-tuple-element.73), channel_id=1, source_target_pairs={{0,7},{1,0},{2,1},{3,2},{4,3},{5,4},{6,5},{7,6},{8,15},{9,8},{10,9... | collective-permute-start | bytes 24584 | tf_op jit(solution)/shard_map/ppermute | solution.py:473
  4.5 0.0 collective-permute-start
  4.6 0.0 copy-start.7
  4.6 0.1 fusion.1.flags
  4.7 0.0 copy-done.1
  4.7 0.0 copy-done.4
  4.7 0.6 %copy-done.7 = bf16[32,32]{1,0:T(8,128)(2,1)S(1)} copy-done((bf16[32,32]{1,0:T(8,128)(2,1)S(1)}, bf16[32,32]{1,0:T(8,128)(2,1)}, u32[]{:S(2)}) %copy-start.7) | copy-done | bytes 2072
  5.3 0.6 %shard_map.84 = (bf16[96,320]{1,0:T(8,128)(2,1)S(1)}, bf16[96,288]{1,0:T(8,128)(2,1)S(1)}, bf16[96,288]{1,0:T(8,128)(2,1)S(1)}, bf16[96,288]{1,0:T(8,128)(2,1)S(1)}) custom-call(bf16[864,32]{1,0:T(8,128)(2,1)S(1)} %bitcast.8, bf16[864,32]{1,0:T(8,128)(2,1)S(1)} %bitcast.12, bf16[864,32]{1,0:T(8,128)(2,1)S(1)} %bitcast.13, bf16[864,32]{1,0:T(8,128)(2,1)S(1)} %bitcast.14, ...), custom_call_target="tpu_custom_call" | custom-call | flops 268435456 | bytes 1048576 | tf_op jit(solution)/shard_map/pallas_call | solution.py:78
  5.9 2.9 %collective-permute-done.from_lo = bf16[32,128]{1,0:T(8,128)(2,1)S(1)} collective-permute-done((bf16[32,128]{1,0:T(8,128)(2,1)S(1)}, bf16[32,128]{1,0:T(8,128)(2,1)S(1)}, u32[]{:S(2)}, u32[]{:S(2)}) %collective-permute-start) | collective-permute-done | bytes 8224 | tf_op jit(solution)/shard_map/ppermute | solution.py:473
  8.8 0.0 collective-permute-done.1.from_hi
  8.8 0.2 shard_map.85
  9.0 2.0 %collective-permute-start.2 = (bf16[16,32,128]{2,1,0:T(8,128)(2,1)S(1)}, bf16[16,32,128]{2,1,0:T(8,128)(2,1)S(1)}, u32[]{:S(2)}, u32[]{:S(2)}) collective-permute-start(bf16[16,32,128]{2,1,0:T(8,128)(2,1)S(1)} %get-tuple-element.55), channel_id=1, source_target_pairs={{0,32},{32,64},{64,96},{96,128},{128,160},{160,192},{192,224},{224... | collective-permute-start | bytes 393224 | tf_op jit(solution)/shard_map/ppermute | solution.py:473
  11.0 4.0 %collective-permute-start.3 = (bf16[16,32,128]{2,1,0:T(8,128)(2,1)S(1)}, bf16[16,32,128]{2,1,0:T(8,128)(2,1)S(1)}, u32[]{:S(2)}, u32[]{:S(2)}) collective-permute-start(bf16[16,32,128]{2,1,0:T(8,128)(2,1)S(1)} %get-tuple-element.62), channel_id=1, source_target_pairs={{0,224},{32,0},{64,32},{96,64},{128,96},{160,128},{192,160},{224,1... | collective-permute-start | bytes 393224 | tf_op jit(solution)/shard_map/ppermute | solution.py:473
  15.0 2.4 %collective-permute-start.5 = (bf16[32,128]{1,0:T(8,128)(2,1)S(1)}, bf16[32,128]{1,0:T(8,128)(2,1)S(1)}, u32[]{:S(2)}, u32[]{:S(2)}) collective-permute-start(bf16[32,128]{1,0:T(8,128)(2,1)S(1)} %get-tuple-element.60.t3), channel_id=1, source_target_pairs={{0,192},{32,224},{64,0},{96,32},{128,64},{160,96},{192,128},{224,1... | collective-permute-start | bytes 24584 | tf_op jit(solution)/shard_map/ppermute | solution.py:473
  17.4 0.5 %collective-permute-start.4 = (bf16[32,128]{1,0:T(8,128)(2,1)S(1)}, bf16[32,128]{1,0:T(8,128)(2,1)S(1)}, u32[]{:S(2)}, u32[]{:S(2)}) collective-permute-start(bf16[32,128]{1,0:T(8,128)(2,1)S(1)} %get-tuple-element.60.t3), channel_id=1, source_target_pairs={{0,64},{32,96},{64,128},{96,160},{128,192},{160,224},{192,0},{224,... | collective-permute-start | bytes 24584 | tf_op jit(solution)/shard_map/ppermute | solution.py:473
  17.9 1.7 %shard_map.86.acc = f32[8,8,32,128]{3,2,1,0:T(8,128)S(1)} custom-call(bf16[8,8,32,128]{3,2,1,0:T(8,128)(2,1)S(1)} %get-tuple-element.39.x_ref, bf16[4,4,32,128]{3,2,1,0:T(8,128)(2,1)S(1)} %get-tuple-element.56.t1, bf16[864,32]{1,0:T(8,128)(2,1)S(1)} %bitcast.9, bf16[96,320]{1,0:T(8,128)(2,1)S(1)} %get-tuple-element.57.wf), custom_call_target="tpu_custom_call" | custom-call | flops 1073741824 | bytes 1048576 | tf_op jit(solution)/shard_map/pallas_call | solution.py:78
  19.6 0.0 collective-permute-done.2.xr_lo
  19.6 0.0 collective-permute-done.5.xr_hi2
  19.6 3.5 %collective-permute-done.4.xr_lo2 = bf16[32,128]{1,0:T(8,128)(2,1)S(1)} collective-permute-done((bf16[32,128]{1,0:T(8,128)(2,1)S(1)}, bf16[32,128]{1,0:T(8,128)(2,1)S(1)}, u32[]{:S(2)}, u32[]{:S(2)}) %collective-permute-start.4) | collective-permute-done | bytes 8224 | tf_op jit(solution)/shard_map/ppermute | solution.py:473
  23.2 0.0 collective-permute-done.3.xr_hi
  23.2 0.2 shard_map.88
  23.4 1.7 %collective-permute-start.6 = (bf16[26,32,128]{2,1,0:T(8,128)(2,1)S(1)}, bf16[26,32,128]{2,1,0:T(8,128)(2,1)S(1)}, u32[]{:S(2)}, u32[]{:S(2)}) collective-permute-start(bf16[26,32,128]{2,1,0:T(8,128)(2,1)S(1)} %get-tuple-element.70), channel_id=1, source_target_pairs={{0,8},{8,16},{16,24},{24,0},{1,9},{9,17},{17,25},{25,1},{2,10},{10... | collective-permute-start | bytes 638984 | tf_op jit(solution)/shard_map/ppermute | solution.py:473
  25.1 0.5 %collective-permute-start.7 = (bf16[26,32,128]{2,1,0:T(8,128)(2,1)S(1)}, bf16[26,32,128]{2,1,0:T(8,128)(2,1)S(1)}, u32[]{:S(2)}, u32[]{:S(2)}) collective-permute-start(bf16[26,32,128]{2,1,0:T(8,128)(2,1)S(1)} %get-tuple-element.71), channel_id=1, source_target_pairs={{0,24},{8,0},{16,8},{24,16},{1,25},{9,1},{17,9},{25,17},{2,26},{10... | collective-permute-start | bytes 638984 | tf_op jit(solution)/shard_map/ppermute | solution.py:473
  25.5 2.3 %collective-permute-start.8 = (bf16[32,128]{1,0:T(8,128)(2,1)S(1)}, bf16[32,128]{1,0:T(8,128)(2,1)S(1)}, u32[]{:S(2)}, u32[]{:S(2)}) collective-permute-start(bf16[32,128]{1,0:T(8,128)(2,1)S(1)} %get-tuple-element.72), channel_id=1, source_target_pairs={{0,16},{8,24},{16,0},{24,8},{1,17},{9,25},{17,1},{25,9},{2,18},{10... | collective-permute-start | bytes 24584 | tf_op jit(solution)/shard_map/ppermute | solution.py:473
  27.8 1.6 %shard_map.87 = (f32[2,8,32,128]{3,2,1,0:T(8,128)S(1)}, f32[6,6,32,128]{3,2,1,0:T(8,128)S(1)}, f32[4,4,32,128]{3,2,1,0:T(8,128)S(1)}, f32[3,3,32,128]{3,2,1,0:T(8,128)S(1)}) custom-call(f32[16,128]{1,0:T(8,128)S(1)} %fusion.1.flags, bf16[4,4,32,128]{3,2,1,0:T(8,128)(2,1)S(1)} %get-tuple-element.56.t1, bf16[2,2,32,128]{3,2,1,0:T(8,128)(2,1)S(1)} %get-tuple-element.59.t2, ...), custom_call_target="tpu_custom_call" | custom-call | flops 1073741824 | bytes 1048576 | tf_op jit(solution)/shard_map/pallas_call | solution.py:78
  29.4 2.3 %collective-permute-done.8.yr_two = bf16[32,128]{1,0:T(8,128)(2,1)S(1)} collective-permute-done((bf16[32,128]{1,0:T(8,128)(2,1)S(1)}, bf16[32,128]{1,0:T(8,128)(2,1)S(1)}, u32[]{:S(2)}, u32[]{:S(2)}) %collective-permute-start.8) | collective-permute-done | bytes 8224 | tf_op jit(solution)/shard_map/ppermute | solution.py:473
  31.7 0.0 collective-permute-done.6.yr_lo
  31.7 0.0 collective-permute-done.7.yr_hi
  31.7 3.1 %shard_map.89 = bf16[32,8,8,128]{3,2,1,0:T(8,128)(2,1)} custom-call(f32[16,128]{1,0:T(8,128)S(1)} %fusion.1.flags, f32[8,8,32,128]{3,2,1,0:T(8,128)S(1)} %shard_map.86.acc, f32[2,8,32,128]{3,2,1,0:T(8,128)S(1)} %get-tuple-element.66.edge_x, f32[6,6,32,128]{3,2,1,0:T(8,128)S(1)} %get-tuple-element.67.a1, f32[4,4,32,128]{3,2,1,0:T(8,128)S(1)} %get-tuple-element.68.a2, ...), custom_call_target="tpu_custom_call" | custom-call | flops 1048576 | bytes 1048576 | tf_op jit(solution)/shard_map/pallas_call | solution.py:78
  (15 shorter events, 0.0 us)
Async XLA Ops:
  0.0 1.0 %copy-start = (bf16[32,8,8,128]{3,2,1,0:T(8,128)(2,1)S(1)}, bf16[32,8,8,128]{3,2,1,0:T(8,128)(2,1)}, u32[]{:S(2)}) copy-start(bf16[32,8,8,128]{3,2,1,0:T(8,128)(2,1)} %field.1) | copy-start | bytes 1572868
  1.0 3.6 %copy-start.1 = (bf16[3,3,3,32,32]{4,3,2,1,0:T(8,128)(2,1)S(1)}, bf16[3,3,3,32,32]{4,3,2,1,0:T(8,128)(2,1)}, u32[]{:S(2)}) copy-start(bf16[3,3,3,32,32]{4,3,2,1,0:T(8,128)(2,1)} %param.10) | copy-start | bytes 165892
  1.0 3.6 %copy-start.4 = (bf16[3,3,3,32,32]{4,3,2,1,0:T(8,128)(2,1)S(1)}, bf16[3,3,3,32,32]{4,3,2,1,0:T(8,128)(2,1)}, u32[]{:S(2)}) copy-start(bf16[3,3,3,32,32]{4,3,2,1,0:T(8,128)(2,1)} %param.11) | copy-start | bytes 165892
  1.0 3.6 %copy-start.5 = (bf16[3,3,3,32,32]{4,3,2,1,0:T(8,128)(2,1)S(1)}, bf16[3,3,3,32,32]{4,3,2,1,0:T(8,128)(2,1)}, u32[]{:S(2)}) copy-start(bf16[3,3,3,32,32]{4,3,2,1,0:T(8,128)(2,1)} %param.12) | copy-start | bytes 165892
  1.0 3.6 %copy-start.6 = (bf16[3,3,3,32,32]{4,3,2,1,0:T(8,128)(2,1)S(1)}, bf16[3,3,3,32,32]{4,3,2,1,0:T(8,128)(2,1)}, u32[]{:S(2)}) copy-start(bf16[3,3,3,32,32]{4,3,2,1,0:T(8,128)(2,1)} %param.13) | copy-start | bytes 165892
  2.3 6.5 %collective-permute-start.1 = (bf16[32,128]{1,0:T(8,128)(2,1)S(1)}, bf16[32,128]{1,0:T(8,128)(2,1)S(1)}, u32[]{:S(2)}, u32[]{:S(2)}) collective-permute-start(bf16[32,128]{1,0:T(8,128)(2,1)S(1)} %get-tuple-element.73), channel_id=1, source_target_pairs={{0,7},{1,0},{2,1},{3,2},{4,3},{5,4},{6,5},{7,6},{8,15},{9,8},{10,9... | collective-permute-start | bytes 24584 | tf_op jit(solution)/shard_map/ppermute | solution.py:473
  4.5 4.3 %collective-permute-start = (bf16[32,128]{1,0:T(8,128)(2,1)S(1)}, bf16[32,128]{1,0:T(8,128)(2,1)S(1)}, u32[]{:S(2)}, u32[]{:S(2)}) collective-permute-start(bf16[32,128]{1,0:T(8,128)(2,1)S(1)} %get-tuple-element.74), channel_id=1, source_target_pairs={{0,1},{1,2},{2,3},{3,4},{4,5},{5,6},{6,7},{7,0},{8,9},{9,10},{10,1... | collective-permute-start | bytes 24584 | tf_op jit(solution)/shard_map/ppermute | solution.py:473
  4.6 0.7 %copy-start.7 = (bf16[32,32]{1,0:T(8,128)(2,1)S(1)}, bf16[32,32]{1,0:T(8,128)(2,1)}, u32[]{:S(2)}) copy-start(bf16[32,32]{1,0:T(8,128)(2,1)} %mix) | copy-start | bytes 6148
  9.0 10.6 %collective-permute-start.2 = (bf16[16,32,128]{2,1,0:T(8,128)(2,1)S(1)}, bf16[16,32,128]{2,1,0:T(8,128)(2,1)S(1)}, u32[]{:S(2)}, u32[]{:S(2)}) collective-permute-start(bf16[16,32,128]{2,1,0:T(8,128)(2,1)S(1)} %get-tuple-element.55), channel_id=1, source_target_pairs={{0,32},{32,64},{64,96},{96,128},{128,160},{160,192},{192,224},{224... | collective-permute-start | bytes 393224 | tf_op jit(solution)/shard_map/ppermute | solution.py:473
  11.0 12.2 %collective-permute-start.3 = (bf16[16,32,128]{2,1,0:T(8,128)(2,1)S(1)}, bf16[16,32,128]{2,1,0:T(8,128)(2,1)S(1)}, u32[]{:S(2)}, u32[]{:S(2)}) collective-permute-start(bf16[16,32,128]{2,1,0:T(8,128)(2,1)S(1)} %get-tuple-element.62), channel_id=1, source_target_pairs={{0,224},{32,0},{64,32},{96,64},{128,96},{160,128},{192,160},{224,1... | collective-permute-start | bytes 393224 | tf_op jit(solution)/shard_map/ppermute | solution.py:473
  15.0 4.6 %collective-permute-start.5 = (bf16[32,128]{1,0:T(8,128)(2,1)S(1)}, bf16[32,128]{1,0:T(8,128)(2,1)S(1)}, u32[]{:S(2)}, u32[]{:S(2)}) collective-permute-start(bf16[32,128]{1,0:T(8,128)(2,1)S(1)} %get-tuple-element.60.t3), channel_id=1, source_target_pairs={{0,192},{32,224},{64,0},{96,32},{128,64},{160,96},{192,128},{224,1... | collective-permute-start | bytes 24584 | tf_op jit(solution)/shard_map/ppermute | solution.py:473
  17.4 5.8 %collective-permute-start.4 = (bf16[32,128]{1,0:T(8,128)(2,1)S(1)}, bf16[32,128]{1,0:T(8,128)(2,1)S(1)}, u32[]{:S(2)}, u32[]{:S(2)}) collective-permute-start(bf16[32,128]{1,0:T(8,128)(2,1)S(1)} %get-tuple-element.60.t3), channel_id=1, source_target_pairs={{0,64},{32,96},{64,128},{96,160},{128,192},{160,224},{192,0},{224,... | collective-permute-start | bytes 24584 | tf_op jit(solution)/shard_map/ppermute | solution.py:473
  23.4 8.3 %collective-permute-start.6 = (bf16[26,32,128]{2,1,0:T(8,128)(2,1)S(1)}, bf16[26,32,128]{2,1,0:T(8,128)(2,1)S(1)}, u32[]{:S(2)}, u32[]{:S(2)}) collective-permute-start(bf16[26,32,128]{2,1,0:T(8,128)(2,1)S(1)} %get-tuple-element.70), channel_id=1, source_target_pairs={{0,8},{8,16},{16,24},{24,0},{1,9},{9,17},{17,25},{25,1},{2,10},{10... | collective-permute-start | bytes 638984 | tf_op jit(solution)/shard_map/ppermute | solution.py:473
  25.1 6.7 %collective-permute-start.7 = (bf16[26,32,128]{2,1,0:T(8,128)(2,1)S(1)}, bf16[26,32,128]{2,1,0:T(8,128)(2,1)S(1)}, u32[]{:S(2)}, u32[]{:S(2)}) collective-permute-start(bf16[26,32,128]{2,1,0:T(8,128)(2,1)S(1)} %get-tuple-element.71), channel_id=1, source_target_pairs={{0,24},{8,0},{16,8},{24,16},{1,25},{9,1},{17,9},{25,17},{2,26},{10... | collective-permute-start | bytes 638984 | tf_op jit(solution)/shard_map/ppermute | solution.py:473
  25.5 6.2 %copy-start.2 = (bf16[128,128]{1,0:T(8,128)(2,1)S(1)}, bf16[128,128]{1,0:T(8,128)(2,1)}, u32[]{:S(2)}) copy-start(bf16[128,128]{1,0:T(8,128)(2,1)} %constant.36.clone.up0) | copy-start | bytes 98308
  25.5 6.2 %copy-start.3 = (bf16[128,128]{1,0:T(8,128)(2,1)S(1)}, bf16[128,128]{1,0:T(8,128)(2,1)}, u32[]{:S(2)}) copy-start(bf16[128,128]{1,0:T(8,128)(2,1)} %constant.35.clone.up) | copy-start | bytes 98308
  25.5 6.2 %collective-permute-start.8 = (bf16[32,128]{1,0:T(8,128)(2,1)S(1)}, bf16[32,128]{1,0:T(8,128)(2,1)S(1)}, u32[]{:S(2)}, u32[]{:S(2)}) collective-permute-start(bf16[32,128]{1,0:T(8,128)(2,1)S(1)} %get-tuple-element.72), channel_id=1, source_target_pairs={{0,16},{8,24},{16,0},{24,8},{1,17},{9,25},{17,1},{25,9},{2,18},{10... | collective-permute-start | bytes 24584 | tf_op jit(solution)/shard_map/ppermute | solution.py:473
